TPU v7x, 256 devices: a whole 4x4x8 slice. The times are simulated.
256 devices in a mesh: rows: 64 (over z, x, core), grp: 4 (over y).
Axes of the slice: x: 4, y: 4, z: 8, core: 2. Of those that a mesh axis runs over, the one named last changes fastest.
Arguments:
- user_features: bfloat16 [4, 16384, 256], P('grp', 'rows'), may hold values from -72 to 72
- w_first: bfloat16 [256, 256], replicated, may hold values from -0.375 to 0.375
- w_second: bfloat16 [256, 256], replicated, may hold values from -0.375 to 0.375
- item_embed: bfloat16 [4, 16384, 256], P('grp', 'rows'), may hold values from -27 to 27
- example_weight: float32 [4, 16384], P('grp', 'rows'), may hold values from 0.02 to 0.2
- positive: int32 [4, 16384], P('grp', 'rows'), may hold values from 0 to 16383
- item_owner: int32 [4, 16384, 1], P('grp', 'rows'), may hold values from 0 to 63; in each aligned block of 256 rows (0 to 255, 256 to 511, ..., all dimensions but the last counted through in order) at most 16 rows name the same one
- item_row: int32 [4, 16384], P('grp', 'rows'), may hold values from 0 to 4095
Outputs:
- grad_first: float32 [256, 256], replicated
- grad_second: float32 [256, 256], replicated
- grad_table: float32 [262144, 256], P('rows', 'grp')
Inputs may be any that keep to these rules, and one draw needn't show every extreme that they name: `item_owner`: within the rows of one device (aligned blocks of 256 pairs of a group) no owner is named by more than 16 pairs, a bound that some block reaches.
All inputs are finite; a program needn't handle non-finite values.
Results may differ from a plain program's by a relative error of at most 0.0023.
The roundings to bfloat16 on the way count: a program that leaves them out, or rounds other values in their place, can miss the bound.
Values may be sent and summed in bfloat16 or wider, within the bound.
No kernel may reach another device: no remote copies, remote signals or barrier semaphores. Data moves between devices by JAX's collectives and lax.ppermute only.
A program may use at most 128 MiB of HBM per device.

v0:
```python
import jax
import jax.numpy as jnp
from jax import lax
from jax.sharding import Mesh
from jax.sharding import PartitionSpec as P

ITEMS_DEV = 4096
ROWS = ("rows_0", "rows_1", "rows_2")
ROWS_GRP = ("rows_0", "rows_1", "rows_2", "grp")


def gather_turned(arrays, axis, dims):
    turned = [jnp.moveaxis(a, dim, 0) for a, dim in zip(arrays, dims)]
    widths = [t[0].size for t in turned]
    both = jnp.concatenate([t.reshape(-1, w) for t, w in zip(turned, widths)], axis=1)
    filled = lax.all_gather(both, axis, axis=0, tiled=True)
    tiles = jnp.split(filled, [sum(widths[:k]) for k in range(1, len(widths))], axis=1)
    return tuple(
        (
            jnp.moveaxis(b.reshape(-1, *t.shape[1:]), 0, dim)
            for b, t, dim in zip(tiles, turned, dims)
        )
    )


def cut_along(value, dim, count):
    before, after = (value.shape[:dim], value.shape[dim + 1 :])
    return jnp.moveaxis(value.reshape(*before, count, -1, *after), dim, 0)


def sum_at_owner(value, axis, dim):
    count = lax.axis_size(axis)
    tiles = lax.all_to_all(cut_along(value, dim, count), axis, 0, 0, tiled=True)
    return jnp.sum(tiles, axis=0)


def summed_rows(value, axes, dim):
    far, near = axes
    tiles = cut_along(value, dim, lax.axis_size(far))
    nearer = sum_at_owner(tiles, near, dim + 1)
    arrived = lax.all_to_all(nearer, far, split_axis=0, concat_axis=0, tiled=True)
    return arrived.sum(axis=0)


def padded_to(lines, count):
    spare = -lines.shape[0] % count
    if not spare:
        return lines
    return jnp.concatenate([lines, jnp.zeros((spare, *lines.shape[1:]), lines.dtype)])


def sent_to_all(value, axis):
    count = lax.axis_size(axis)
    return lax.all_to_all(
        jnp.broadcast_to(value[None], (count, *value.shape)), axis, 0, 0, tiled=True
    )


def joined_along(tiles, dim):
    shape = list(tiles.shape[1:])
    shape[dim] *= tiles.shape[0]
    return jnp.moveaxis(tiles, 0, dim).reshape(shape)


def gather_axes(value, axes, dim):
    far, near = axes
    tiles = sent_to_all(sent_to_all(value, far), near)
    return joined_along(tiles.swapaxes(0, 1).reshape(-1, *value.shape), dim)


def total_of(value, axes):
    own = summed_rows(padded_to(value, lax.axis_size(axes[0]) * lax.axis_size(axes[1])), axes, 0)
    whole = gather_axes(own, axes, 0)
    return whole[: len(value)].reshape(value.shape)


def in_one(arrays, axis):
    flat, at, done = (jnp.concatenate([a.reshape(-1) for a in arrays]), 0, [])
    total = total_of(flat, axis)
    for a in arrays:
        done.append(total[at : at + a.size].reshape(a.shape))
        at += a.size
    return tuple(done)


def one_exchange(value, axis, axes, splits, concats):
    sizes = [lax.axis_size(a) for a in axes]
    tiles = cut_along(value, splits[0], sizes[0])
    tiles = jnp.moveaxis(cut_along(tiles, splits[1] + 1, sizes[1]), 0, 1)
    inside = tiles.shape[2:]
    tiles = tiles.reshape(-1, *inside)
    tiles = lax.all_to_all(tiles, axis, split_axis=0, concat_axis=0, tiled=True)
    tiles = joined_along(tiles.reshape(*sizes, *inside), concats[0] + 1)
    return joined_along(tiles, concats[1])


def contract_first(left, right):
    return lax.dot_general(
        left, right, (((0,), (0,)), ((), ())), preferred_element_type=jnp.float32
    )


def contract_last(left, right):
    return lax.dot_general(
        left, right, (((1,), (1,)), ((), ())), preferred_element_type=jnp.float32
    )


def body(
    user_features, w_first, w_second, item_embed, example_weight, positive, item_owner, item_row
):
    features = user_features[0]
    own_items = item_embed[0]
    weights = example_weight[0]
    targets = positive[0]
    owners = item_owner[0, :, 0]
    item_rows = item_row[0]
    my_users = features.shape[0]
    feature_width = own_items.shape[1]
    peers = lax.axis_size(ROWS)
    my_index = lax.axis_index(ROWS)
    pre_act = jnp.dot(features, w_first, preferred_element_type=jnp.float32)
    hidden = jax.nn.silu(pre_act).astype(jnp.bfloat16)
    user_vecs = jnp.dot(hidden, w_second, preferred_element_type=jnp.float32).astype(jnp.bfloat16)
    gathered = lax.all_gather(own_items, ROWS, axis=0, tiled=True)
    group_users = gathered.shape[0]
    scores = contract_last(user_vecs, gathered)
    row_max = jnp.max(scores, axis=1, keepdims=True)
    log_total = row_max + jnp.log(jnp.sum(jnp.exp(scores - row_max), axis=1, keepdims=True))
    columns = lax.broadcasted_iota(jnp.int32, (1, group_users), 1)
    chosen = (columns == targets[:, None]).astype(jnp.float32)
    dscore = (weights[:, None] * (jnp.exp(scores - log_total) - chosen)).astype(jnp.bfloat16)
    grad_user = jnp.dot(dscore, gathered, preferred_element_type=jnp.float32).astype(jnp.bfloat16)
    everyone = lax.all_gather(user_vecs, ROWS, axis=0, tiled=True)
    target_all, total_all, weight_all = gather_turned(
        (targets.astype(jnp.float32), log_total[:, 0], weights), ROWS, (0, 0, 0)
    )
    back_scores = contract_last(everyone, own_items)
    own_columns = my_index * my_users + lax.broadcasted_iota(jnp.int32, (1, my_users), 1)
    hits = (own_columns == target_all.astype(jnp.int32)[:, None]).astype(jnp.float32)
    back_dscore = (weight_all[:, None] * (jnp.exp(back_scores - total_all[:, None]) - hits)).astype(
        jnp.bfloat16
    )
    grad_item = contract_first(back_dscore, everyone)
    d_second = contract_first(hidden, grad_user)
    back_grad = contract_last(grad_user, w_second)
    sigmoid_pre = jax.nn.sigmoid(pre_act)
    grad_pre = (back_grad * sigmoid_pre * (1.0 + pre_act * (1.0 - sigmoid_pre))).astype(
        jnp.bfloat16
    )
    d_first = contract_first(features, grad_pre)
    grad_first, grad_second = in_one((d_first, d_second), (("rows_0", "rows_1"), ("rows_2", "grp")))
    capacity = max(2, 4 * my_users // peers)
    member = (owners[:, None] == lax.broadcasted_iota(jnp.int32, (1, peers), 1)).astype(jnp.int32)
    before = jnp.cumsum(member, axis=0) - member
    slot_rank = jnp.sum(before * member, axis=1)
    slots = owners * capacity + slot_rank
    send_grad = jnp.zeros((peers * capacity, feature_width), jnp.float32).at[slots].set(grad_item)
    send_grad = send_grad.reshape(peers, capacity, feature_width)
    send_rows = (
        jnp.full((peers * capacity,), -1.0, jnp.float32)
        .at[slots]
        .set(item_rows.astype(jnp.float32))
    )
    groups = lax.axis_size("grp")
    rows_wide = jnp.broadcast_to(send_rows.reshape(peers, capacity, 1), (peers, capacity, groups))
    got_grad, got_rows = (
        one_exchange(send_grad, ROWS_GRP, (ROWS, "grp"), (0, 2), (0, 1)),
        one_exchange(rows_wide, ROWS_GRP, (ROWS, "grp"), (0, 2), (0, 1)),
    )
    share_width = feature_width // groups
    table_rows = got_rows.reshape(-1).astype(jnp.int32)
    table_rows = jnp.where(table_rows >= 0, table_rows, ITEMS_DEV)
    grad_table = (
        jnp.zeros((ITEMS_DEV, share_width), jnp.float32)
        .at[table_rows]
        .add(got_grad.reshape(-1, share_width), mode="drop")
    )
    return (grad_first, grad_second, grad_table)


def solution(mesh):
    torus = Mesh(
        mesh.devices.reshape(8, 4, 2, mesh.shape["grp"]), ("rows_0", "rows_1", "rows_2", "grp")
    )
    placed = (
        P("grp", ROWS, None),
        P(),
        P(),
        P("grp", ROWS, None),
        P("grp", ROWS),
        P("grp", ROWS),
        P("grp", ROWS, None),
        P("grp", ROWS),
    )
    return jax.shard_map(
        body, mesh=torus, in_specs=placed, out_specs=(P(), P(), P(ROWS, "grp")), check_vma=False
    )
```

profile of v0, /device:TPU:1, one launch (start us, length us, event | category | flops | bytes accessed | tf_op | source)
XLA Modules:
  0.0 337.8 jit_solution(12011691266853101209)
XLA Ops:
  13.0 84.9 %all-gather.6.cloned.1.call-done = bf16[1,16384,256]{2,1,0:T(8,128)(2,1)} async-done(((bf16[1,256,256]{2,1,0:T(8,128)(2,1)}), bf16[1,16384,256]{2,1,0:T(8,128)(2,1)}) %all-gather.6.cloned.1.call-update) | async-done | bytes 8388624 | tf_op jit(solution)/shard_map/all_gather | solution.py:125
  97.9 11.6 %fusion.36 = (f32[256]{0:T(256)S(1)}, f32[256,16384]{1,0:T(8,128)}) fusion(bf16[256,256]{1,0:T(8,128)(2,1)} %convolution_convert_fusion, bf16[1,16384,256]{2,1,0:T(8,128)(2,1)} %all-gather.6.cloned.1.call-done), kind=kOutput, calls=%fused_computation.61 | convolution fusion | flops 2151677696 | bytes 25297920 | tf_op jit(solution)/shard_map/dot_general | solution.py:104
  109.5 8.3 %exponential_reduce_fusion = f32[256]{0:T(256)S(1)} fusion(f32[256,16384]{1,0:T(8,128)} %get-tuple-element.21, f32[256]{0:T(256)S(1)} %get-tuple-element.20), kind=kLoop, calls=%fused_computation.10 | loop fusion | flops 8388352 | bytes 16779264 | tf_op jit(solution)/shard_map/reduce_sum | solution.py:129
  117.8 13.0 %fusion.11 = bf16[256,256]{1,0:T(8,128)(2,1)S(1)} fusion(bf16[1,16384,256]{2,1,0:T(8,128)(2,1)} %all-gather.6.cloned.1.call-done, f32[256,16384]{1,0:T(8,128)} %get-tuple-element.21, s32[256]{0:T(256)S(1)} %bitcast.120, f32[256]{0:T(256)S(1)} %log_add_fusion, f32[256]{0:T(256)S(1)} %bitcast.116), kind=kOutput, calls=%fused_computation.21 | convolution fusion | flops 2172715008 | bytes 25299968 | tf_op jit(solution)/shard_map/dot_general | solution.py:133
  133.1 4.5 %all-to-all-start = ((f32[8,32,512]{2,1,0:T(8,128)}), f32[8,32,512]{2,1,0:T(8,128)S(1)}, u32[]{:S(2)}, u32[]{:S(2)}) async-start(f32[8,32,512]{2,1,0:T(8,128)} %copy.25), calls=%async_computation | async-start | bytes 1048576 | tf_op jit(solution)/shard_map/all_to_all | solution.py:33
  137.6 1.4 scatter_custom_fusion
  139.1 7.8 %all-to-all-done = f32[8,32,512]{2,1,0:T(8,128)S(1)} async-done(((f32[8,32,512]{2,1,0:T(8,128)}), f32[8,32,512]{2,1,0:T(8,128)S(1)}, u32[]{:S(2)}, u32[]{:S(2)}) %all-to-all-start) | async-done | bytes 524320 | tf_op jit(solution)/shard_map/all_to_all | solution.py:33
  147.7 5.1 %all-to-all-start.1 = ((f32[32,1,512]{2,1,0:T(1,128)}), f32[32,1,512]{2,1,0:T(1,128)S(1)}, u32[]{:S(2)}, u32[]{:S(2)}) async-start(f32[32,1,512]{2,1,0:T(1,128)} %all_to_all.23), calls=%async_computation.1 | async-start | bytes 131072 | tf_op jit(solution)/shard_map/all_to_all | solution.py:41
  152.8 45.7 %all_gather.10 = f32[16384,3]{0,1:T(4,128)S(1)} all-gather(f32[256,3]{0,1:T(4,128)S(1)} %pad_maximum_fusion), channel_id=1, replica_groups=mesh['rows_0'=8,'rows_1'=4,'rows_2'=2,'grp'=4] {'rows_0','rows_1','rows_2'}, dimensions={0}, use_global_device_ids=true | all-gather | bytes 199680 | tf_op jit(solution)/shard_map/all_gather | solution.py:16
  199.2 6.6 %all-to-all-start.2 = ((f32[32,1,512]{2,1,0:T(1,128)}), f32[32,1,512]{2,1,0:T(1,128)S(1)}, u32[]{:S(2)}, u32[]{:S(2)}) async-start(f32[32,1,512]{2,1,0:T(1,128)} %broadcast_in_dim.17), calls=%async_computation.2 | async-start | bytes 131072 | tf_op jit(solution)/shard_map/all_to_all | solution.py:54
  206.0 8.7 %all-to-all-done.2 = f32[32,1,512]{2,1,0:T(1,128)S(1)} async-done(((f32[32,1,512]{2,1,0:T(1,128)}), f32[32,1,512]{2,1,0:T(1,128)S(1)}, u32[]{:S(2)}, u32[]{:S(2)}) %all-to-all-start.2) | async-done | bytes 65568 | tf_op jit(solution)/shard_map/all_to_all | solution.py:54
  215.4 6.6 %all-to-all-start.4 = ((f32[256,1,16,1]{2,3,1,0:T(1,128)}), f32[256,1,16,1]{2,3,1,0:T(1,128)S(1)}, u32[]{:S(2)}, u32[]{:S(2)}) async-start(f32[256,1,16,1]{2,3,1,0:T(1,128)} %bitcast.14), calls=%async_computation.4 | async-start | bytes 262144 | tf_op jit(solution)/shard_map/all_to_all | solution.py:92
  222.0 12.5 %fusion.3.clone.4 = bf16[16384,256]{1,0:T(8,128)(2,1)} fusion(bf16[16384,256]{1,0:T(8,128)(2,1)} %all-gather.4.cloned.1.call-done, s32[256]{0:T(256)S(1)} %iota_add_fusion, f32[16384]{0:T(1024)S(1)} %bitcast.109, f32[16384]{0:T(1024)S(1)} %bitcast.110, s32[16384]{0:T(1024)S(1)} %bitcast.108, bf16[1,256,256]{2,1,0:T(8,128)(2,1)S(1)} %copy-done.1), kind=kOutput, calls=%fused_computation.7.clone.clone.clone.1 | convolution fusion | flops 2172649472 | bytes 17105920 | tf_op jit(solution)/shard_map/dot_general | solution.py:104
  235.7 6.1 %all-to-all-start.3 = ((f32[8,32,512]{2,1,0:T(8,128)}), f32[8,32,512]{2,1,0:T(8,128)}, u32[]{:S(2)}, u32[]{:S(2)}) async-start(f32[8,32,512]{2,1,0:T(8,128)} %broadcast_in_dim.19), calls=%async_computation.3 | async-start | bytes 1048576 | tf_op jit(solution)/shard_map/all_to_all | solution.py:54
  241.8 8.1 %fusion.8 = f32[256,256]{1,0:T(8,128)S(1)} fusion(bf16[16384,256]{1,0:T(8,128)(2,1)} %all-gather.4.cloned.1.call-done, bf16[16384,256]{1,0:T(8,128)(2,1)} %fusion.3.clone.4), kind=kOutput, calls=%fused_computation.15 | convolution fusion | flops 2147483648 | bytes 17039360 | tf_op jit(solution)/shard_map/dot_general | solution.py:98
  249.9 1.7 scatter_custom_fusion.1
  252.5 1.5 copy.29
  254.0 3.4 %reshape.203 = f32[256,1,1024]{2,1,0:T(1,128)} reshape(f32[256,1,16,64]{3,2,1,0:T(8,128)} %bitcast.104) | data formatting | bytes 2097152
  257.5 12.3 %all-to-all-start.5 = ((f32[256,1,1024]{2,1,0:T(1,128)}), f32[256,1,1024]{2,1,0:T(1,128)S(1)}, u32[]{:S(2)}, u32[]{:S(2)}) async-start(f32[256,1,1024]{2,1,0:T(1,128)} %reshape.203), calls=%async_computation.5 | async-start | bytes 2097152 | tf_op jit(solution)/shard_map/all_to_all | solution.py:92
  273.0 27.7 %all-to-all-done.5 = f32[256,1,1024]{2,1,0:T(1,128)S(1)} async-done(((f32[256,1,1024]{2,1,0:T(1,128)}), f32[256,1,1024]{2,1,0:T(1,128)S(1)}, u32[]{:S(2)}, u32[]{:S(2)}) %all-to-all-start.5) | async-done | bytes 1048608 | tf_op jit(solution)/shard_map/all_to_all | solution.py:92
  301.2 3.1 reduce.3
  304.3 1.9 reshape.204
  306.2 23.2 %scatter_custom_fusion.2 = f32[4096,64]{1,0:T(8,128)S(1)} fusion(s32[4096]{0:T(1024)S(1)} %bitcast.111, f32[4096,64]{1,0:T(8,128)} %bitcast.105, f32[]{:T(128)} %constant.18.clone.1), kind=kCustom, calls=%fused_computation.22 | custom fusion | flops 262144 | bytes 1049088 | tf_op jit(solution)/shard_map/scatter-add | solution.py:177
  329.4 1.6 copy.31
  (60 shorter events, 16.1 us)
Async XLA Ops:
  7.2 2.0 copy-start
  7.2 90.7 %all-gather.6.cloned.1.call-start = ((), (), s32[]{:S(2)}) async-start(), calls=%async_computation.7 | async-start | bytes 8519680 | tf_op jit(solution)/shard_map/all_gather | solution.py:125
  7.9 214.1 %all-gather.4.cloned.1.call-start = ((), (), s32[]{:S(2)}) async-start(), calls=%async_computation.6 | async-start | bytes 8519680 | tf_op jit(solution)/shard_map/all_gather | solution.py:134
  109.5 8.3 %copy-start.4 = (f32[1,256]{1,0:T(1,128)S(1)}, f32[1,256]{1,0:T(1,128)}, u32[]{:S(2)}) copy-start(f32[1,256]{1,0:T(1,128)} %param.12) | copy-start | bytes 3076
  109.5 8.3 %copy-start.5 = (s32[1,256]{1,0:T(1,128)S(1)}, s32[1,256]{1,0:T(1,128)}, u32[]{:S(2)}) copy-start(s32[1,256]{1,0:T(1,128)} %param.13) | copy-start | bytes 3076
  117.8 13.4 %copy-start.2 = (bf16[1,256,256]{2,1,0:T(8,128)(2,1)S(1)}, bf16[1,256,256]{2,1,0:T(8,128)(2,1)}, u32[]{:S(2)}) copy-start(bf16[1,256,256]{2,1,0:T(8,128)(2,1)} %param.8) | copy-start | bytes 393220
  117.8 19.8 %copy-start.3 = (s32[1,256,1]{1,2,0:T(1,128)S(1)}, s32[1,256,1]{1,2,0:T(1,128)}, u32[]{:S(2)}) copy-start(s32[1,256,1]{1,2,0:T(1,128)} %param.14) | copy-start | bytes 3076
  130.9 91.1 %copy-start.1 = (bf16[1,256,256]{2,1,0:T(8,128)(2,1)S(1)}, bf16[1,256,256]{2,1,0:T(8,128)(2,1)}, u32[]{:S(2)}) copy-start(bf16[1,256,256]{2,1,0:T(8,128)(2,1)} %param.11) | copy-start | bytes 393220
  133.1 13.9 %all-to-all-start = ((f32[8,32,512]{2,1,0:T(8,128)}), f32[8,32,512]{2,1,0:T(8,128)S(1)}, u32[]{:S(2)}, u32[]{:S(2)}) async-start(f32[8,32,512]{2,1,0:T(8,128)} %copy.25), calls=%async_computation | async-start | bytes 1048576 | tf_op jit(solution)/shard_map/all_to_all | solution.py:33
  147.7 50.8 %all-to-all-start.1 = ((f32[32,1,512]{2,1,0:T(1,128)}), f32[32,1,512]{2,1,0:T(1,128)S(1)}, u32[]{:S(2)}, u32[]{:S(2)}) async-start(f32[32,1,512]{2,1,0:T(1,128)} %all_to_all.23), calls=%async_computation.1 | async-start | bytes 131072 | tf_op jit(solution)/shard_map/all_to_all | solution.py:41
  199.2 15.5 %all-to-all-start.2 = ((f32[32,1,512]{2,1,0:T(1,128)}), f32[32,1,512]{2,1,0:T(1,128)S(1)}, u32[]{:S(2)}, u32[]{:S(2)}) async-start(f32[32,1,512]{2,1,0:T(1,128)} %broadcast_in_dim.17), calls=%async_computation.2 | async-start | bytes 131072 | tf_op jit(solution)/shard_map/all_to_all | solution.py:54
  215.4 19.4 %all-to-all-start.4 = ((f32[256,1,16,1]{2,3,1,0:T(1,128)}), f32[256,1,16,1]{2,3,1,0:T(1,128)S(1)}, u32[]{:S(2)}, u32[]{:S(2)}) async-start(f32[256,1,16,1]{2,3,1,0:T(1,128)} %bitcast.14), calls=%async_computation.4 | async-start | bytes 262144 | tf_op jit(solution)/shard_map/all_to_all | solution.py:92
  235.7 21.8 %all-to-all-start.3 = ((f32[8,32,512]{2,1,0:T(8,128)}), f32[8,32,512]{2,1,0:T(8,128)}, u32[]{:S(2)}, u32[]{:S(2)}) async-start(f32[8,32,512]{2,1,0:T(8,128)} %broadcast_in_dim.19), calls=%async_computation.3 | async-start | bytes 1048576 | tf_op jit(solution)/shard_map/all_to_all | solution.py:54
  257.5 43.2 %all-to-all-start.5 = ((f32[256,1,1024]{2,1,0:T(1,128)}), f32[256,1,1024]{2,1,0:T(1,128)S(1)}, u32[]{:S(2)}, u32[]{:S(2)}) async-start(f32[256,1,1024]{2,1,0:T(1,128)} %reshape.203), calls=%async_computation.5 | async-start | bytes 2097152 | tf_op jit(solution)/shard_map/all_to_all | solution.py:92
Sparse Core Ops, SparseCore 0:
  10.8 87.1 all-gather.5
  101.3 79.9 all-gather.3
where the time goes:
time: 338 us
  waiting for transfers between devices  130 us (38%)
  matrix products  48 us (14%)
  blocking collectives  45.7 us (14%)
  starting transfers between devices  41.3 us (12%)
  other arithmetic  37.8 us (11%)
  local copies, waits for them, and re-layouts  20.6 us (6%)
  between operations  14.3 us (4%)
    all_gather x1, waiting for transfers between devices, body(): gathered = lax.all_gather(own_items, ROWS, axis=0, tiled=True)  84.9 us
    all_gather x1, blocking collectives, gather_turned(): filled = lax.all_gather(both, axis, axis=0, tiled=True)  45.7 us
    all_to_all x2, waiting for transfers between devices, one_exchange(): tiles = lax.all_to_all(tiles, axis, split_axis=0, concat_axis=0, tiled=True)  27.9 us
    dot_general x2, matrix products, contract_last(): lax.dot_general(left, right, (((1,), (1,)), ((), ())), preferred_element_...  24.1 us
    scatter-add x1, other arithmetic, body(): grad_table = jnp.zeros((ITEMS_DEV, share_width), jnp.float32).at[table_ro...  23.2 us
    all_to_all x2, starting transfers between devices, one_exchange(): tiles = lax.all_to_all(tiles, axis, split_axis=0, concat_axis=0, tiled=True)  18.9 us
    dot_general x1, matrix products, body(): jnp.dot(dscore, gathered, preferred_element_type=jnp.float32)  13 us
    all_to_all x2, starting transfers between devices, sent_to_all(): lax.all_to_all(jnp.broadcast_to(value[None], (count, *value.shape)), axis...  12.7 us
  transfers between devices with their start and end apart: 8, of which 5 were waited for; matrix products, arithmetic and copies ran while one was open for 22% of the time, Pallas kernels for 0%

commit v1 on v0

v1 whole, which is shorter than its diff:
```python
import jax
import jax.numpy as jnp
from jax import lax
from jax.experimental import pallas as pl
from jax.experimental.pallas import tpu as pltpu
from jax.sharding import Mesh
from jax.sharding import PartitionSpec as P

TABLE = 4096
CAP = 16
BLK = 256
XK = ("x", "k")
XKY = ("x", "k", "y")
ALL = ("z", "x", "k", "y")
F32 = jnp.float32
BF16 = jnp.bfloat16


def dot(left, right, dims):
    return lax.dot_general(left, right, ((dims[0:1], dims[1:2]), ((), ())), preferred_element_type=F32)


def exchange(value, axes):
    return lax.all_to_all(value, axes, 0, 0, tiled=True)


def to_all(value, axes):
    return exchange(jnp.broadcast_to(value[None], (lax.axis_size(axes), *value.shape)), axes)


def stats_kernel(items_ref, users_ref, own_ref, out_ref):
    rows = []
    sums = []
    for c in range(8):
        scores = dot(items_ref[...], users_ref[c * BLK : (c + 1) * BLK, :], (1, 1))
        top = jnp.max(scores, axis=0, keepdims=True)
        rows.append(top)
        sums.append(jnp.sum(jnp.exp(scores - top), axis=0, keepdims=True))
    chunk = jnp.concatenate(rows + sums + [own_ref[...]], axis=0)
    for p in range(8):
        out_ref[p] = chunk


def stats(items, users, own):
    return pl.pallas_call(
        stats_kernel,
        out_shape=jax.ShapeDtypeStruct((8, 24, BLK), F32),
        compiler_params=pltpu.CompilerParams(vmem_limit_bytes=56 * 2**20),
        name="stats",
    )(items, users, own)


def grads_kernel(base_ref, items_ref, turned_ref, users_ref, got_ref, gi_ref, gu_ref, acc_ref):
    shard = 8 * BLK
    place = lax.broadcasted_iota(jnp.int32, (shard, BLK), 0)
    index = (place // BLK) * shard + base_ref[0] + (place % BLK)
    for c in range(8):
        tops = got_ref[:, c, :]
        parts = got_ref[:, 8 + c, :]
        top = jnp.max(tops, axis=0, keepdims=True)
        total = top + jnp.log(jnp.sum(parts * jnp.exp(tops - top), axis=0, keepdims=True))
        weight = got_ref[c, 16:17, :]
        target = got_ref[c, 17:18, :].astype(jnp.int32)
        users = users_ref[c * BLK : (c + 1) * BLK, :]
        scores = dot(items_ref[...], users, (1, 1))
        chosen = (index == target).astype(F32)
        dscore = (weight * (jnp.exp(scores - total) - chosen)).astype(BF16)
        gu_ref[c] = dot(turned_ref[...], dscore, (1, 0))
        part = dot(dscore, users, (1, 0))
        if c == 0:
            acc_ref[...] = part
        elif c < 7:
            acc_ref[...] += part
        else:
            gi_ref[...] = (acc_ref[...] + part).astype(BF16)


def grads(base, items, turned, users, got):
    vmem = pl.BlockSpec(memory_space=pltpu.VMEM)
    return pl.pallas_call(
        grads_kernel,
        in_specs=[pl.BlockSpec(memory_space=pltpu.SMEM), vmem, vmem, vmem, vmem],
        out_shape=(
            jax.ShapeDtypeStruct((8 * BLK, 256), BF16),
            jax.ShapeDtypeStruct((8, 256, BLK), F32),
        ),
        scratch_shapes=[pltpu.VMEM((8 * BLK, 256), F32)],
        compiler_params=pltpu.CompilerParams(vmem_limit_bytes=56 * 2**20),
        name="grads",
    )(base, items, turned, users, got)


def thirds(value):
    high = value.astype(BF16)
    rest = value - high.astype(F32)
    middle = rest.astype(BF16)
    return high, middle, (rest - middle.astype(F32)).astype(BF16)


def pack_kernel(parts_ref, owner_ref, rank_ref, out_ref):
    value = jnp.sum(parts_ref[...].astype(F32), axis=0)
    pieces = thirds(value)
    lane = lax.broadcasted_iota(jnp.int32, (64 * 8, BLK), 0)
    halves = []
    for h in range(2):
        rank = rank_ref[...] - 8 * h
        slot = jnp.where((rank >= 0) & (rank < 8), owner_ref[...] * 8 + rank, -1)
        pick = (lane == slot).astype(F32).astype(BF16)
        halves.append(sum(dot(pick, piece, (1, 0)) for piece in pieces))
    for g in range(4):
        share = slice(64 * g, 64 * g + 64)
        both = jnp.concatenate([halves[0][:, share], halves[1][:, share]], axis=1)
        out_ref[:, g] = both.reshape(64, 8, 128)


def pack(parts, owner, rank):
    return pl.pallas_call(
        pack_kernel, out_shape=jax.ShapeDtypeStruct((64, 4, 8, 128), F32), name="pack"
    )(parts, owner, rank)


def table_kernel(got_ref, ids_ref, out_ref):
    both = got_ref[...].T
    value = jnp.concatenate([both[:64], both[64:]], axis=1)
    pieces = jnp.concatenate(thirds(value), axis=0)
    ids = ids_ref[...]
    upper = ids >> 8
    lower = ids & 255
    pick = (lax.broadcasted_iota(jnp.int32, (256, TABLE), 0) == lower).astype(F32).astype(BF16)
    zero = jnp.zeros((), BF16)
    for a in range(16):
        keep = jnp.broadcast_to((upper == a).astype(F32), (16, TABLE)).astype(BF16)
        kept = pieces * jnp.concatenate([keep] * 12, axis=0)
        part = dot(kept, pick, (1, 1))
        out_ref[:, a * 256 : (a + 1) * 256] = part[:64] + part[64:128] + part[128:]


def table(got, ids):
    return pl.pallas_call(
        table_kernel,
        out_shape=jax.ShapeDtypeStruct((64, TABLE), F32),
        compiler_params=pltpu.CompilerParams(vmem_limit_bytes=56 * 2**20),
        name="table",
    )(got, ids)


def tower(features, w_first, w_second):
    pre_act = jnp.dot(features, w_first, preferred_element_type=F32)
    hidden = jax.nn.silu(pre_act).astype(BF16)
    return pre_act, hidden, jnp.dot(hidden, w_second, preferred_element_type=F32).astype(BF16)


def body(user_features, w_first, w_second, item_embed, example_weight, positive, item_owner, item_row):
    features = user_features[0]
    owner = item_owner.reshape(1, BLK)
    items = to_all(item_embed[0], "z").reshape(8 * BLK, 256)
    block = to_all(features, XK).reshape(8 * BLK, 256)
    _, _, users = tower(block, w_first, w_second)

    member = (owner == lax.broadcasted_iota(jnp.int32, (64, 1), 0)).astype(F32)
    order = lax.broadcasted_iota(jnp.int32, (BLK, BLK), 0) < lax.broadcasted_iota(jnp.int32, (BLK, BLK), 1)
    before = dot(member.astype(BF16), order.astype(BF16), (1, 0))
    rank = jnp.sum(before * member, axis=0, keepdims=True).astype(jnp.int32)
    slot = owner * CAP + rank
    held = (slot == lax.broadcasted_iota(jnp.int32, (64 * CAP, 1), 0)).astype(jnp.int32)
    rows = jnp.sum(held * (item_row + 1), axis=1) - 1
    rows = jnp.broadcast_to(rows.reshape(64, 1, CAP), (64, 4, CAP)).reshape(256, CAP)
    ids = exchange(rows, ALL)
    ids = jnp.concatenate([ids[:, :8].reshape(1, -1), ids[:, 8:].reshape(1, -1)], axis=1)

    own = jnp.concatenate(
        [example_weight, positive.astype(F32), jnp.zeros((6, BLK), F32)], axis=0
    )
    got = exchange(stats(items, users, own), XK)
    base = (lax.axis_index(XK) * BLK).astype(jnp.int32).reshape(1)
    gi, gu = grads(base, items, items.T, users, got)
    gi = exchange(gi.reshape(8, BLK, 256), "z")
    gu = exchange(gu, XK)

    send = pack(gi, owner, rank).reshape(256, 8, 128)
    came = exchange(send, ALL).reshape(256 * 8, 128)
    grad_table = table(came, ids).T

    pre_act, hidden, _ = tower(features, w_first, w_second)
    grad_user = jnp.sum(gu, axis=0).T.astype(BF16)
    d_second = dot(hidden, grad_user, (0, 0))
    back_grad = dot(grad_user, w_second, (1, 1))
    gate = jax.nn.sigmoid(pre_act)
    grad_pre = (back_grad * gate * (1.0 + pre_act * (1.0 - gate))).astype(BF16)
    d_first = dot(features, grad_pre, (0, 0))
    both = jnp.concatenate([d_first, d_second], axis=0).reshape(32, 16, 256)
    both = jnp.sum(exchange(both, XKY), axis=0)
    both = jnp.sum(to_all(both, "z"), axis=0)
    both = to_all(both, XKY).reshape(512, 256)
    return both[:256], both[256:], grad_table


def solution(mesh):
    torus = Mesh(mesh.devices.reshape(8, 4, 2, mesh.shape["grp"]), ("z", "x", "k", "y"))
    rows = ("z", "x", "k")
    placed = (
        P("y", rows, None),
        P(),
        P(),
        P("y", rows, None),
        P("y", rows),
        P("y", rows),
        P("y", rows, None),
        P("y", rows),
    )
    return jax.shard_map(
        body, mesh=torus, in_specs=placed, out_specs=(P(), P(), P(rows, "y")), check_vma=False
    )
```

time: 338 us -> 272 us (0.80)
  matrix products: 48 us -> 2.89 us
  blocking collectives: 45.7 us -> 10.1 us
  other arithmetic: 37.8 us -> 3.09 us
  Pallas kernels: 0 us -> 34.1 us
  waiting for transfers between devices: 130 us -> 162 us
  between operations: 14.3 us -> 0.87 us
  local copies, waits for them, and re-layouts: 20.6 us -> 9.25 us
  starting transfers between devices: 41.3 us -> 48.3 us
    all_to_all x6 -> x9, waiting for transfers between devices: 44.5 us -> 162 us  [exchange(): return lax.all_to_all(value, axes, 0, 0, tiled=True)]
    all_gather x2 -> x0, waiting for transfers between devices: 84.9 us -> none  [the longest x1 84.9 us: body(): gathered = lax.all_gather(own_items, ROWS, axis=0, tiled=True)]
    all_gather x1 -> x0, blocking collectives: 45.7 us -> none  [gather_turned(): filled = lax.all_gather(both, axis, axis=0, tiled=True)]
    dot_general x8 -> x5, matrix products: 48 us -> 2.89 us  [the longest x1 1.84 us: tower(): jnp.dot(hidden, w_second, preferred_element_type=F32).astype(BF16)]
    pallas_call x0 -> x4, Pallas kernels: none -> 34.1 us  [the longest x1 13.2 us: table(): pl.pallas_call(table_kernel, out_shape=jax.ShapeDtypeStruct((64, TABLE),...]
    scatter-add x1 -> x0, other arithmetic: 23.2 us -> none  [body(): grad_table = jnp.zeros((ITEMS_DEV, share_width), jnp.float32).at[table_ro...]
    all_to_all x0 -> x1, blocking collectives: none -> 10.1 us  [exchange(): return lax.all_to_all(value, axes, 0, 0, tiled=True)]
    reduce_sum x4, other arithmetic: 9.15 us -> 0.4 us  [the longest x1 0.21 us: body(): rows = jnp.sum(held * (item_row + 1), axis=1) - 1]
  transfers between devices with their start and end apart: 8 -> 9, of which waited for: 5 -> 9; matrix products, arithmetic and copies ran while one was open for 22% -> 2% of each run, Pallas kernels for 0% -> 1%
where the time goes in v1:
time: 272 us; the launch traced here: 271 us
  waiting for transfers between devices  162 us (60%)
  starting transfers between devices  48.3 us (18%)
  Pallas kernels  34.1 us (13%)
  blocking collectives  10.1 us (4%)
  local copies, waits for them, and re-layouts  9.25 us (3%)
  other arithmetic  3.09 us (1%)
  matrix products  2.89 us (1%)
    all_to_all x9, waiting for transfers between devices, exchange(): return lax.all_to_all(value, axes, 0, 0, tiled=True)  162 us
    all_to_all x9, starting transfers between devices, exchange(): return lax.all_to_all(value, axes, 0, 0, tiled=True)  48.3 us
    pallas_call x1, Pallas kernels, table(): pl.pallas_call(table_kernel, out_shape=jax.ShapeDtypeStruct((64, TABLE),...  13.2 us
    pallas_call x1, Pallas kernels, grads(): pl.pallas_call(grads_kernel, in_specs=[pl.BlockSpec(memory_space=pltpu.SM...  11 us
    all_to_all x1, blocking collectives, exchange(): return lax.all_to_all(value, axes, 0, 0, tiled=True)  10.1 us
    pallas_call x1, Pallas kernels, stats(): pl.pallas_call(stats_kernel, out_shape=jax.ShapeDtypeStruct((8, 24, BLK),...  6.8 us
  transfers between devices with their start and end apart: 9, of which 9 were waited for; matrix products, arithmetic and copies ran while one was open for 2% of the time, Pallas kernels for 1%

profile of v1, /device:TPU:1, one launch (start us, length us, event | category | flops | bytes accessed | tf_op | source)
XLA Modules:
  0.0 271.0 jit_solution(6937801832565396231)
XLA Ops:
  0.7 2.0 broadcast_in_dim.38
  2.7 6.7 %all-to-all-start.1 = ((bf16[8,256,256]{2,1,0:T(8,128)(2,1)}), bf16[8,256,256]{2,1,0:T(8,128)(2,1)S(1)}, u32[]{:S(2)}, u32[]{:S(2)}) async-start(bf16[8,256,256]{2,1,0:T(8,128)(2,1)} %broadcast_in_dim.38), calls=%async_computation.1 | async-start | bytes 2097152 | tf_op jit(solution)/shard_map/all_to_all | solution.py:24
  9.4 14.9 %all-to-all-done.1 = bf16[8,256,256]{2,1,0:T(8,128)(2,1)S(1)} async-done(((bf16[8,256,256]{2,1,0:T(8,128)(2,1)}), bf16[8,256,256]{2,1,0:T(8,128)(2,1)S(1)}, u32[]{:S(2)}, u32[]{:S(2)}) %all-to-all-start.1) | async-done | bytes 1048608 | tf_op jit(solution)/shard_map/all_to_all | solution.py:24
  25.4 7.3 %all-to-all-start = ((bf16[8,256,256]{1,2,0:T(8,128)(2,1)}), bf16[8,256,256]{1,2,0:T(8,128)(2,1)S(1)}, u32[]{:S(2)}, u32[]{:S(2)}) async-start(bf16[8,256,256]{1,2,0:T(8,128)(2,1)} %broadcast_in_dim.17), calls=%async_computation | async-start | bytes 2097152 | tf_op jit(solution)/shard_map/all_to_all | solution.py:24
  35.2 26.6 %all-to-all-done = bf16[8,256,256]{1,2,0:T(8,128)(2,1)S(1)} async-done(((bf16[8,256,256]{1,2,0:T(8,128)(2,1)}), bf16[8,256,256]{1,2,0:T(8,128)(2,1)S(1)}, u32[]{:S(2)}, u32[]{:S(2)}) %all-to-all-start) | async-done | bytes 1048608 | tf_op jit(solution)/shard_map/all_to_all | solution.py:24
  63.3 6.8 %stats.1 = f32[8,24,256]{2,1,0:T(8,128)} custom-call(bf16[2048,256]{1,0:T(8,128)(2,1)} %copy.24.items_ref, bf16[2048,256]{1,0:T(8,128)(2,1)} %convolution_convert_fusion.users_ref, f32[8,256]{1,0:T(8,128)} %maximum_maximum_fusion.own_ref), custom_call_target="tpu_custom_call" | custom-call | tf_op jit(solution)/shard_map/stats/pallas_call | solution.py:45
  70.1 3.8 %all-to-all-start.2 = ((f32[8,24,256]{2,1,0:T(8,128)}), f32[8,24,256]{2,1,0:T(8,128)S(1)}, u32[]{:S(2)}, u32[]{:S(2)}) async-start(f32[8,24,256]{2,1,0:T(8,128)} %stats.1), calls=%async_computation.2 | async-start | bytes 393216 | tf_op jit(solution)/shard_map/all_to_all | solution.py:24
  73.9 5.9 %all-to-all-done.2.got_ref = f32[8,24,256]{2,1,0:T(8,128)S(1)} async-done(((f32[8,24,256]{2,1,0:T(8,128)}), f32[8,24,256]{2,1,0:T(8,128)S(1)}, u32[]{:S(2)}, u32[]{:S(2)}) %all-to-all-start.2) | async-done | bytes 196640 | tf_op jit(solution)/shard_map/all_to_all | solution.py:24
  80.5 11.0 %grads.1 = (bf16[2048,256]{1,0:T(8,128)(2,1)}, f32[8,256,256]{2,1,0:T(8,128)}) custom-call(s32[1]{0:T(128)} %bitcast.base_ref, bf16[2048,256]{1,0:T(8,128)(2,1)} %copy.24.items_ref, bf16[256,2048]{1,0:T(8,128)(2,1)} %bitcast.35, bf16[2048,256]{1,0:T(8,128)(2,1)} %convolution_convert_fusion.users_ref, f32[8,24,256]{2,1,0:T(8,128)} %copy-done.4), custom_call_target="tpu_custom_call" | custom-call | tf_op jit(solution)/shard_map/grads/pallas_call | solution.py:80
  91.5 4.6 %all-to-all-start.3 = ((f32[8,256,256]{2,1,0:T(8,128)}), f32[8,256,256]{2,1,0:T(8,128)S(1)}, u32[]{:S(2)}, u32[]{:S(2)}) async-start(f32[8,256,256]{2,1,0:T(8,128)} %get-tuple-element.5), calls=%async_computation.3 | async-start | bytes 4194304 | tf_op jit(solution)/shard_map/all_to_all | solution.py:24
  96.4 25.8 %all-to-all-done.3 = f32[8,256,256]{2,1,0:T(8,128)S(1)} async-done(((f32[8,256,256]{2,1,0:T(8,128)}), f32[8,256,256]{2,1,0:T(8,128)S(1)}, u32[]{:S(2)}, u32[]{:S(2)}) %all-to-all-start.3) | async-done | bytes 2097184 | tf_op jit(solution)/shard_map/all_to_all | solution.py:24
  124.0 6.2 %all-to-all-start.4 = ((f32[32,16,256]{2,1,0:T(8,128)}), f32[32,16,256]{2,1,0:T(8,128)S(1)}, u32[]{:S(2)}, u32[]{:S(2)}) async-start(f32[32,16,256]{2,1,0:T(8,128)} %bitcast.6), calls=%async_computation.4 | async-start | bytes 1048576 | tf_op jit(solution)/shard_map/all_to_all | solution.py:24
  130.5 10.8 %all-to-all-done.4 = f32[32,16,256]{2,1,0:T(8,128)S(1)} async-done(((f32[32,16,256]{2,1,0:T(8,128)}), f32[32,16,256]{2,1,0:T(8,128)S(1)}, u32[]{:S(2)}, u32[]{:S(2)}) %all-to-all-start.4) | async-done | bytes 524320 | tf_op jit(solution)/shard_map/all_to_all | solution.py:24
  141.9 5.9 %all-to-all-start.9 = ((s32[256,1,16]{2,1,0:T(1,128)}), s32[256,1,16]{2,1,0:T(1,128)S(1)}, u32[]{:S(2)}, u32[]{:S(2)}) async-start(s32[256,1,16]{2,1,0:T(1,128)} %bitcast.16), calls=%async_computation.9 | async-start | bytes 262144 | tf_op jit(solution)/shard_map/all_to_all | solution.py:24
  147.9 12.8 %all-to-all-done.9 = s32[256,1,16]{2,1,0:T(1,128)S(1)} async-done(((s32[256,1,16]{2,1,0:T(1,128)}), s32[256,1,16]{2,1,0:T(1,128)S(1)}, u32[]{:S(2)}, u32[]{:S(2)}) %all-to-all-start.9) | async-done | bytes 16416 | tf_op jit(solution)/shard_map/all_to_all | solution.py:24
  160.7 10.1 %all_to_all.57 = f32[8,16,256]{2,1,0:T(8,128)S(1)} all-to-all(f32[8,16,256]{2,1,0:T(8,128)S(1)} %broadcast_in_dim.40), channel_id=1, replica_groups=mesh['z'=8,'x'=4,'k'=2,'y'=4] {'z'}, dimensions={0} | all-to-all | bytes 262144 | tf_op jit(solution)/shard_map/all_to_all | solution.py:24
  170.8 3.6 %all-to-all-start.7 = ((bf16[8,256,256]{2,1,0:T(8,128)(2,1)}), bf16[8,256,256]{2,1,0:T(8,128)(2,1)S(1)}, u32[]{:S(2)}, u32[]{:S(2)}) async-start(bf16[8,256,256]{2,1,0:T(8,128)(2,1)} %bitcast.9), calls=%async_computation.7 | async-start | bytes 2097152 | tf_op jit(solution)/shard_map/all_to_all | solution.py:24
  174.4 29.0 %all-to-all-done.7.parts_ref = bf16[8,256,256]{2,1,0:T(8,128)(2,1)S(1)} async-done(((bf16[8,256,256]{2,1,0:T(8,128)(2,1)}), bf16[8,256,256]{2,1,0:T(8,128)(2,1)S(1)}, u32[]{:S(2)}, u32[]{:S(2)}) %all-to-all-start.7) | async-done | bytes 1048608 | tf_op jit(solution)/shard_map/all_to_all | solution.py:24
  204.3 4.1 %all-to-all-start.6 = ((f32[32,16,256]{2,1,0:T(8,128)}), f32[32,16,256]{2,1,0:T(8,128)S(1)}, u32[]{:S(2)}, u32[]{:S(2)}) async-start(f32[32,16,256]{2,1,0:T(8,128)} %broadcast_in_dim.41), calls=%async_computation.6 | async-start | bytes 1048576 | tf_op jit(solution)/shard_map/all_to_all | solution.py:24
  209.1 3.1 %pack.1 = f32[64,4,8,128]{3,2,1,0:T(8,128)} custom-call(bf16[8,256,256]{2,1,0:T(8,128)(2,1)} %copy-done.2, s32[1,256]{1,0:T(1,128)} %bitcast.46, s32[1,256]{1,0:T(1,128)} %bitcast.49), custom_call_target="tpu_custom_call" | custom-call | tf_op jit(solution)/shard_map/pack/pallas_call | solution.py:117
  212.2 7.5 %all-to-all-done.6 = f32[32,16,256]{2,1,0:T(8,128)S(1)} async-done(((f32[32,16,256]{2,1,0:T(8,128)}), f32[32,16,256]{2,1,0:T(8,128)S(1)}, u32[]{:S(2)}, u32[]{:S(2)}) %all-to-all-start.6) | async-done | bytes 524320 | tf_op jit(solution)/shard_map/all_to_all | solution.py:24
  219.7 6.2 %all-to-all-start.8 = ((f32[256,8,128]{2,1,0:T(8,128)}), f32[256,8,128]{2,1,0:T(8,128)S(1)}, u32[]{:S(2)}, u32[]{:S(2)}) async-start(f32[256,8,128]{2,1,0:T(8,128)} %bitcast.36), calls=%async_computation.8 | async-start | bytes 2097152 | tf_op jit(solution)/shard_map/all_to_all | solution.py:24
  227.6 29.2 %all-to-all-done.8 = f32[256,8,128]{2,1,0:T(8,128)S(1)} async-done(((f32[256,8,128]{2,1,0:T(8,128)}), f32[256,8,128]{2,1,0:T(8,128)S(1)}, u32[]{:S(2)}, u32[]{:S(2)}) %all-to-all-start.8) | async-done | bytes 1048608 | tf_op jit(solution)/shard_map/all_to_all | solution.py:24
  257.8 13.2 %table.1 = f32[64,4096]{1,0:T(8,128)} custom-call(f32[2048,128]{1,0:T(8,128)} %bitcast.37, s32[1,4096]{1,0:T(1,128)} %pad_add_fusion.ids_ref), custom_call_target="tpu_custom_call" | custom-call | tf_op jit(solution)/shard_map/table/pallas_call | solution.py:139
  (55 shorter events, 13.2 us)
Async XLA Ops:
  0.6 32.8 %copy-start = (bf16[256,256]{1,0:T(8,128)(2,1)S(1)}, bf16[256,256]{1,0:T(8,128)(2,1)}, u32[]{:S(2)}) copy-start(bf16[256,256]{1,0:T(8,128)(2,1)} %param.9) | copy-start | bytes 393220
  0.6 8.7 %copy-start.6 = (bf16[1,256,256]{2,1,0:T(8,128)(2,1)S(1)}, bf16[1,256,256]{2,1,0:T(8,128)(2,1)}, u32[]{:S(2)}) copy-start(bf16[1,256,256]{2,1,0:T(8,128)(2,1)} %param.11) | copy-start | bytes 393220
  2.7 21.7 %all-to-all-start.1 = ((bf16[8,256,256]{2,1,0:T(8,128)(2,1)}), bf16[8,256,256]{2,1,0:T(8,128)(2,1)S(1)}, u32[]{:S(2)}, u32[]{:S(2)}) async-start(bf16[8,256,256]{2,1,0:T(8,128)(2,1)} %broadcast_in_dim.38), calls=%async_computation.1 | async-start | bytes 2097152 | tf_op jit(solution)/shard_map/all_to_all | solution.py:24
  9.3 23.3 %copy-start.8 = (s32[1,256]{1,0:T(1,128)S(1)}, s32[1,256]{1,0:T(1,128)}, u32[]{:S(2)}) copy-start(s32[1,256]{1,0:T(1,128)} %param.13) | copy-start | bytes 3076
  9.3 23.4 %copy-start.10 = (f32[1,256]{1,0:T(1,128)S(1)}, f32[1,256]{1,0:T(1,128)}, u32[]{:S(2)}) copy-start(f32[1,256]{1,0:T(1,128)} %param.12) | copy-start | bytes 3076
  9.3 24.1 %copy-start.11 = (bf16[256,256]{1,0:T(8,128)(2,1)S(1)}, bf16[256,256]{1,0:T(8,128)(2,1)}, u32[]{:S(2)}) copy-start(bf16[256,256]{1,0:T(8,128)(2,1)} %param.10) | copy-start | bytes 393220
  25.4 36.5 %all-to-all-start = ((bf16[8,256,256]{1,2,0:T(8,128)(2,1)}), bf16[8,256,256]{1,2,0:T(8,128)(2,1)S(1)}, u32[]{:S(2)}, u32[]{:S(2)}) async-start(bf16[8,256,256]{1,2,0:T(8,128)(2,1)} %broadcast_in_dim.17), calls=%async_computation | async-start | bytes 2097152 | tf_op jit(solution)/shard_map/all_to_all | solution.py:24
  62.0 8.2 %copy-start.1 = (bf16[8,32,8,256]{3,2,0,1:T(8,128)(2,1)}, bf16[8,32,8,256]{3,2,0,1:T(8,128)(2,1)S(1)}, u32[]{:S(2)}) copy-start(bf16[8,32,8,256]{3,2,0,1:T(8,128)(2,1)S(1)} %copy.25) | copy-start | bytes 3145732
  70.1 9.7 %all-to-all-start.2 = ((f32[8,24,256]{2,1,0:T(8,128)}), f32[8,24,256]{2,1,0:T(8,128)S(1)}, u32[]{:S(2)}, u32[]{:S(2)}) async-start(f32[8,24,256]{2,1,0:T(8,128)} %stats.1), calls=%async_computation.2 | async-start | bytes 393216 | tf_op jit(solution)/shard_map/all_to_all | solution.py:24
  79.8 0.7 copy-start.4
  91.4 4.6 %copy-start.7 = (s32[1,256,1]{1,2,0:T(1,128)S(1)}, s32[1,256,1]{1,2,0:T(1,128)}, u32[]{:S(2)}) copy-start(s32[1,256,1]{1,2,0:T(1,128)} %param.14) | copy-start | bytes 3076
  91.4 4.8 %copy-start.5 = (bf16[1,256,256]{2,1,0:T(8,128)(2,1)S(1)}, bf16[1,256,256]{2,1,0:T(8,128)(2,1)}, u32[]{:S(2)}) copy-start(bf16[1,256,256]{2,1,0:T(8,128)(2,1)} %param.8) | copy-start | bytes 393220
  91.5 30.8 %all-to-all-start.3 = ((f32[8,256,256]{2,1,0:T(8,128)}), f32[8,256,256]{2,1,0:T(8,128)S(1)}, u32[]{:S(2)}, u32[]{:S(2)}) async-start(f32[8,256,256]{2,1,0:T(8,128)} %get-tuple-element.5), calls=%async_computation.3 | async-start | bytes 4194304 | tf_op jit(solution)/shard_map/all_to_all | solution.py:24
  122.8 7.3 %copy-start.9 = (s32[1,256]{1,0:T(1,128)S(1)}, s32[1,256]{1,0:T(1,128)}, u32[]{:S(2)}) copy-start(s32[1,256]{1,0:T(1,128)} %param.15) | copy-start | bytes 3076
  124.0 17.3 %all-to-all-start.4 = ((f32[32,16,256]{2,1,0:T(8,128)}), f32[32,16,256]{2,1,0:T(8,128)S(1)}, u32[]{:S(2)}, u32[]{:S(2)}) async-start(f32[32,16,256]{2,1,0:T(8,128)} %bitcast.6), calls=%async_computation.4 | async-start | bytes 1048576 | tf_op jit(solution)/shard_map/all_to_all | solution.py:24
  141.9 18.7 %all-to-all-start.9 = ((s32[256,1,16]{2,1,0:T(1,128)}), s32[256,1,16]{2,1,0:T(1,128)S(1)}, u32[]{:S(2)}, u32[]{:S(2)}) async-start(s32[256,1,16]{2,1,0:T(1,128)} %bitcast.16), calls=%async_computation.9 | async-start | bytes 262144 | tf_op jit(solution)/shard_map/all_to_all | solution.py:24
  170.8 32.6 %all-to-all-start.7 = ((bf16[8,256,256]{2,1,0:T(8,128)(2,1)}), bf16[8,256,256]{2,1,0:T(8,128)(2,1)S(1)}, u32[]{:S(2)}, u32[]{:S(2)}) async-start(bf16[8,256,256]{2,1,0:T(8,128)(2,1)} %bitcast.9), calls=%async_computation.7 | async-start | bytes 2097152 | tf_op jit(solution)/shard_map/all_to_all | solution.py:24
  203.4 5.7 %copy-start.2 = (bf16[8,256,256]{2,1,0:T(8,128)(2,1)}, bf16[8,256,256]{2,1,0:T(8,128)(2,1)S(1)}, u32[]{:S(2)}) copy-start(bf16[8,256,256]{2,1,0:T(8,128)(2,1)S(1)} %all-to-all-done.7.parts_ref) | copy-start | bytes 3145732
  204.3 15.3 %all-to-all-start.6 = ((f32[32,16,256]{2,1,0:T(8,128)}), f32[32,16,256]{2,1,0:T(8,128)S(1)}, u32[]{:S(2)}, u32[]{:S(2)}) async-start(f32[32,16,256]{2,1,0:T(8,128)} %broadcast_in_dim.41), calls=%async_computation.6 | async-start | bytes 1048576 | tf_op jit(solution)/shard_map/all_to_all | solution.py:24
  219.7 37.2 %all-to-all-start.8 = ((f32[256,8,128]{2,1,0:T(8,128)}), f32[256,8,128]{2,1,0:T(8,128)S(1)}, u32[]{:S(2)}, u32[]{:S(2)}) async-start(f32[256,8,128]{2,1,0:T(8,128)} %bitcast.36), calls=%async_computation.8 | async-start | bytes 2097152 | tf_op jit(solution)/shard_map/all_to_all | solution.py:24
  256.8 1.0 copy-start.3

commit v2 on v1

v2 whole, which is shorter than its diff:
```python
import jax
import jax.numpy as jnp
from jax import lax
from jax.experimental import pallas as pl
from jax.experimental.pallas import tpu as pltpu
from jax.sharding import Mesh
from jax.sharding import PartitionSpec as P

TABLE = 4096
CAP = 16
BLK = 256
XK = ("x", "k")
ZXK = ("z", "x", "k")
YZXK = ("y", "z", "x", "k")
F32 = jnp.float32
BF16 = jnp.bfloat16


def dot(left, right, dims):
    return lax.dot_general(left, right, ((dims[0:1], dims[1:2]), ((), ())), preferred_element_type=F32)


def exchange(value, axes):
    return lax.all_to_all(value, axes, 0, 0, tiled=True)


def to_all(value, axes):
    return exchange(jnp.broadcast_to(value[None], (lax.axis_size(axes), *value.shape)), axes)


def shifted(value, axis, step):
    count = lax.axis_size(axis)
    return lax.ppermute(value, axis, [(i, (i + step) % count) for i in range(count)])


def rotated(value, axis):
    return [value] + [shifted(value, axis, d) for d in range(1, lax.axis_size(axis))]


def place(axis, step=0):
    return (lax.axis_index(axis).astype(jnp.uint32) + jnp.uint32(step)) & jnp.uint32(lax.axis_size(axis) - 1)


def rows_at(value, start, count):
    zero = jnp.uint32(0)
    return lax.dynamic_slice(value, (start,) + (zero,) * (value.ndim - 1), (count, *value.shape[1:]))


def summed_share(value, axis):
    count = lax.axis_size(axis)
    rows = value.shape[0] // count
    total = rows_at(value, place(axis) * jnp.uint32(rows), rows)
    for d in range(1, count):
        total = total + shifted(rows_at(value, place(axis, d) * jnp.uint32(rows), rows), axis, d)
    return total


def joined(value, axis):
    count = lax.axis_size(axis)
    tiles = rotated(value, axis)
    rising = [tiles[-d % count] for d in range(count)]
    rows = value.shape[0]
    start = (jnp.uint32(count) - place(axis)) * jnp.uint32(rows)
    return rows_at(jnp.concatenate(rising + rising, axis=0), start, count * rows)


def stats_kernel(*refs):
    *item_refs, users_ref, own_ref, out_ref, items_ref = refs
    for d in range(8):
        items_ref[d * BLK : (d + 1) * BLK, :] = item_refs[d][...]

    def step(c, carry):
        scores = dot(items_ref[...], users_ref[pl.ds(c * BLK, BLK), :], (1, 1))
        top = jnp.max(scores, axis=0, keepdims=True)
        out_ref[0, pl.ds(c, 1), :] = top
        out_ref[0, pl.ds(8 + c, 1), :] = jnp.sum(jnp.exp(scores - top), axis=0, keepdims=True)
        return carry

    lax.fori_loop(0, 8, step, 0)
    out_ref[0, 16:24, :] = own_ref[...]
    for p in range(1, 8):
        out_ref[p] = out_ref[0]


def stats(items, users, own):
    return pl.pallas_call(
        stats_kernel,
        out_shape=jax.ShapeDtypeStruct((8, 24, BLK), F32),
        scratch_shapes=[pltpu.VMEM((8 * BLK, 256), BF16)],
        compiler_params=pltpu.CompilerParams(vmem_limit_bytes=56 * 2**20),
        name="stats",
    )(*items, users, own)


def grads_kernel(base_ref, *refs):
    *item_refs, users_ref, got_ref = refs[:10]
    *gi_refs, gu_ref, acc_ref, items_ref, turned_ref, index_ref = refs[10:]
    place = lax.broadcasted_iota(jnp.int32, (BLK, BLK), 0)
    for d in range(8):
        rows = slice(d * BLK, (d + 1) * BLK)
        items_ref[rows, :] = item_refs[d][...]
        turned_ref[:, rows] = item_refs[d][...].T
        index_ref[rows, :] = place + base_ref[d]
    acc_ref[...] = jnp.zeros_like(acc_ref)

    def step(c, carry):
        tops = got_ref[:, pl.ds(c, 1), :].reshape(8, BLK)
        parts = got_ref[:, pl.ds(8 + c, 1), :].reshape(8, BLK)
        top = jnp.max(tops, axis=0, keepdims=True)
        total = top + jnp.log(jnp.sum(parts * jnp.exp(tops - top), axis=0, keepdims=True))
        weight = got_ref[c, 16:17, :]
        target = got_ref[c, 17:18, :].astype(jnp.int32)
        users = users_ref[pl.ds(c * BLK, BLK), :]
        scores = dot(items_ref[...], users, (1, 1))
        chosen = (index_ref[...] == target).astype(F32)
        dscore = (weight * (jnp.exp(scores - total) - chosen)).astype(BF16)
        gu_ref[c] = dot(turned_ref[...], dscore, (1, 0))
        acc_ref[...] += dot(dscore, users, (1, 0))
        return carry

    lax.fori_loop(0, 8, step, 0)
    for d in range(8):
        part = acc_ref[d * BLK : (d + 1) * BLK, :]
        gi_refs[d][...] = part.astype(gi_refs[d].dtype)


def grads(base, items, users, got):
    vmem = pl.BlockSpec(memory_space=pltpu.VMEM)
    return pl.pallas_call(
        grads_kernel,
        in_specs=[pl.BlockSpec(memory_space=pltpu.SMEM)] + [vmem] * 10,
        out_shape=[jax.ShapeDtypeStruct((BLK, 256), F32 if d == 0 else BF16) for d in range(8)]
        + [jax.ShapeDtypeStruct((8, 256, BLK), F32)],
        scratch_shapes=[
            pltpu.VMEM((8 * BLK, 256), F32),
            pltpu.VMEM((8 * BLK, 256), BF16),
            pltpu.VMEM((256, 8 * BLK), BF16),
            pltpu.VMEM((8 * BLK, BLK), jnp.int32),
        ],
        compiler_params=pltpu.CompilerParams(vmem_limit_bytes=56 * 2**20),
        name="grads",
    )(base, *items, users, got)


def thirds(value):
    high = value.astype(BF16)
    rest = value - high.astype(F32)
    middle = rest.astype(BF16)
    return high, middle, (rest - middle.astype(F32)).astype(BF16)


def pack_kernel(*refs):
    *part_refs, owner_ref, rank_ref, out_ref = refs
    value = sum(ref[...].astype(F32) for ref in part_refs)
    pieces = thirds(value)
    lane = lax.broadcasted_iota(jnp.int32, (64 * 8, BLK), 0)
    halves = []
    for h in range(2):
        rank = rank_ref[...] - 8 * h
        slot = jnp.where((rank >= 0) & (rank < 8), owner_ref[...] * 8 + rank, -1)
        pick = (lane == slot).astype(F32).astype(BF16)
        halves.append(sum(dot(pick, piece, (1, 0)) for piece in pieces))
    for g in range(4):
        share = slice(64 * g, 64 * g + 64)
        both = jnp.concatenate([halves[0][:, share], halves[1][:, share]], axis=1)
        out_ref[g] = both.reshape(64, 8, 128)


def pack(parts, owner, rank):
    return pl.pallas_call(
        pack_kernel, out_shape=jax.ShapeDtypeStruct((4, 64, 8, 128), F32), name="pack"
    )(*parts, owner, rank)


def table_kernel(got_ref, ids_ref, out_ref):
    both = got_ref[...].T
    value = jnp.concatenate([both[:64], both[64:]], axis=1)
    pieces = jnp.concatenate(thirds(value), axis=0)
    ids = ids_ref[...]
    upper = ids >> 8
    lower = ids & 255
    pick = (lax.broadcasted_iota(jnp.int32, (256, TABLE), 0) == lower).astype(F32).astype(BF16)

    def step(a, carry):
        keep = jnp.broadcast_to((upper == a).astype(F32), (16, TABLE)).astype(BF16)
        kept = pieces * jnp.concatenate([keep] * 12, axis=0)
        part = dot(kept, pick, (1, 1))
        at = pl.multiple_of(a * 256, 256)
        out_ref[:, pl.ds(at, 256)] = part[:64] + part[64:128] + part[128:]
        return carry

    lax.fori_loop(0, 16, step, 0)


def table(got, ids):
    return pl.pallas_call(
        table_kernel,
        out_shape=jax.ShapeDtypeStruct((64, TABLE), F32),
        compiler_params=pltpu.CompilerParams(vmem_limit_bytes=56 * 2**20),
        name="table",
    )(got, ids)


def tower(features, w_first, w_second):
    pre_act = jnp.dot(features, w_first, preferred_element_type=F32)
    hidden = jax.nn.silu(pre_act).astype(BF16)
    return pre_act, hidden, jnp.dot(hidden, w_second, preferred_element_type=F32).astype(BF16)


def step_body(
    user_features, w_first, w_second, item_embed, example_weight, positive, item_owner, item_row
):
    features = user_features[0]
    owner = item_owner.reshape(1, BLK)
    items = rotated(item_embed[0], "z")
    block = to_all(features, XK).reshape(8 * BLK, 256)
    _, _, users = tower(block, w_first, w_second)

    member = (owner == lax.broadcasted_iota(jnp.int32, (64, 1), 0)).astype(F32)
    order = lax.broadcasted_iota(jnp.int32, (BLK, BLK), 0) < lax.broadcasted_iota(jnp.int32, (BLK, BLK), 1)
    before = dot(member.astype(BF16), order.astype(BF16), (1, 0))
    rank = jnp.sum(before * member, axis=0, keepdims=True).astype(jnp.int32)
    slot = owner * CAP + rank
    held = (slot == lax.broadcasted_iota(jnp.int32, (64 * CAP, 1), 0)).astype(jnp.int32)
    rows = jnp.sum(held * (item_row + 1), axis=1) - 1
    ids = exchange(rows.reshape(64, CAP), ZXK)
    ids = joined(ids, "y")
    ids = jnp.concatenate([ids[:, :8].reshape(1, -1), ids[:, 8:].reshape(1, -1)], axis=1)

    own = jnp.concatenate(
        [example_weight, positive.astype(F32), jnp.zeros((6, BLK), F32)], axis=0
    )
    got = exchange(stats(items, users, own), XK)
    source = (lax.axis_index("z") - jnp.arange(8)) % 8
    base = (source * 8 * BLK + lax.axis_index(XK) * BLK).astype(jnp.int32)
    *gi, gu = grads(base, items, users, got)
    gi = [gi[0]] + [shifted(gi[d], "z", -d) for d in range(1, 8)]
    gu = exchange(gu, XK)

    send = pack(gi, owner, rank).reshape(256, 8, 128)
    came = exchange(send, YZXK).reshape(256 * 8, 128)
    grad_table = table(came, ids).T

    pre_act, hidden, _ = tower(features, w_first, w_second)
    grad_user = jnp.sum(gu, axis=0).T.astype(BF16)
    d_second = dot(hidden, grad_user, (0, 0))
    back_grad = dot(grad_user, w_second, (1, 1))
    gate = jax.nn.sigmoid(pre_act)
    grad_pre = (back_grad * gate * (1.0 + pre_act * (1.0 - gate))).astype(BF16)
    d_first = dot(features, grad_pre, (0, 0))
    both = jnp.concatenate([d_first, d_second], axis=0)
    for axis in ("k", "y", "x"):
        both = summed_share(both, axis)
    for step in (1, 2, 4):
        both = both + lax.ppermute(both, "z", [(i, i ^ step) for i in range(8)])
    for axis in ("x", "y", "k"):
        both = joined(both, axis)
    return both[:256], both[256:], grad_table


def solution(mesh):
    torus = Mesh(mesh.devices.reshape(8, 4, 2, mesh.shape["grp"]), ("z", "x", "k", "y"))
    rows = ("z", "x", "k")
    placed = (
        P("y", rows, None),
        P(),
        P(),
        P("y", rows, None),
        P("y", rows),
        P("y", rows),
        P("y", rows, None),
        P("y", rows),
    )
    return jax.shard_map(
        step_body, mesh=torus, in_specs=placed, out_specs=(P(), P(), P(rows, "y")), check_vma=False
    )
```

time: 272 us -> 250 us (0.919)
  waiting for transfers between devices: 162 us -> 100 us
  starting transfers between devices: 48.3 us -> 90.7 us
  blocking collectives: 10.1 us -> 0 us
  Pallas kernels: 34.1 us -> 43.2 us
    all_to_all x9 -> x5, waiting for transfers between devices: 162 us -> 45.3 us  [exchange(): return lax.all_to_all(value, axes, 0, 0, tiled=True)]
    ppermute x0 -> x34, starting transfers between devices: none -> 55.8 us  [the longest x31 45.9 us: shifted(): lax.ppermute(value, axis, [(i, (i + step) % count) for i in range(count)])]
    ppermute x0 -> x34, waiting for transfers between devices: none -> 55.1 us  [the longest x31 55.1 us: shifted(): lax.ppermute(value, axis, [(i, (i + step) % count) for i in range(count)])]
    all_to_all x9 -> x5, starting transfers between devices: 48.3 us -> 34.9 us  [exchange(): return lax.all_to_all(value, axes, 0, 0, tiled=True)]
    all_to_all x1 -> x0, blocking collectives: 10.1 us -> none  [exchange(): return lax.all_to_all(value, axes, 0, 0, tiled=True)]
    pallas_call x1, Pallas kernels: 13.2 us -> 16.6 us  [table(): pl.pallas_call(table_kernel, out_shape=jax.ShapeDtypeStruct((64, TABLE),...]
    pallas_call x1, Pallas kernels: 6.8 us -> 9.75 us  [stats(): pl.pallas_call(stats_kernel, out_shape=jax.ShapeDtypeStruct((8, 24, BLK),...]
    pallas_call x1, Pallas kernels: 11 us -> 13.7 us  [grads(): pl.pallas_call(grads_kernel, in_specs=[pl.BlockSpec(memory_space=pltpu.SM...]
  transfers between devices with their start and end apart: 9 -> 39, of which waited for: 9 -> 24; matrix products, arithmetic and copies ran while one was open for 2% -> 3% of each run, Pallas kernels for 1% -> 8%
where the time goes in v2:
time: 250 us
  waiting for transfers between devices  100 us (40%)
  starting transfers between devices  90.7 us (36%)
  Pallas kernels  43.2 us (17%)
  local copies, waits for them, and re-layouts  7.93 us (3%)
  other arithmetic  3.4 us (1%)
  matrix products  2.86 us (1%)
    ppermute x31, waiting for transfers between devices, shifted(): lax.ppermute(value, axis, [(i, (i + step) % count) for i in range(count)])  55.1 us
    ppermute x31, starting transfers between devices, shifted(): lax.ppermute(value, axis, [(i, (i + step) % count) for i in range(count)])  45.9 us
    all_to_all x5, waiting for transfers between devices, exchange(): return lax.all_to_all(value, axes, 0, 0, tiled=True)  45.3 us
    all_to_all x5, starting transfers between devices, exchange(): return lax.all_to_all(value, axes, 0, 0, tiled=True)  34.9 us
    pallas_call x1, Pallas kernels, table(): pl.pallas_call(table_kernel, out_shape=jax.ShapeDtypeStruct((64, TABLE),...  16.6 us
    pallas_call x1, Pallas kernels, grads(): pl.pallas_call(grads_kernel, in_specs=[pl.BlockSpec(memory_space=pltpu.SM...  13.7 us
    ppermute x3, starting transfers between devices, step_body(): both = both + lax.ppermute(both, 'z', [(i, i ^ step) for i in range(8)])  9.9 us
    pallas_call x1, Pallas kernels, stats(): pl.pallas_call(stats_kernel, out_shape=jax.ShapeDtypeStruct((8, 24, BLK),...  9.75 us
  transfers between devices with their start and end apart: 39, of which 24 were waited for; matrix products, arithmetic and copies ran while one was open for 3% of the time, Pallas kernels for 8%

profile of v2, /device:TPU:1, one launch (start us, length us, event | category | flops | bytes accessed | tf_op | source)
XLA Modules:
  0.0 249.7 jit_solution(5427071153303156856)
XLA Ops:
  2.7 6.7 %all-to-all-start = ((bf16[8,256,256]{2,1,0:T(8,128)(2,1)}), bf16[8,256,256]{2,1,0:T(8,128)(2,1)S(1)}, u32[]{:S(2)}, u32[]{:S(2)}) async-start(bf16[8,256,256]{2,1,0:T(8,128)(2,1)} %broadcast_in_dim.12), calls=%async_computation | async-start | bytes 2097152 | tf_op jit(solution)/shard_map/all_to_all | solution.py:24
  13.2 3.8 %collective-permute-start.2 = (bf16[256,256]{1,0:T(8,128)(2,1)S(1)}, bf16[256,256]{1,0:T(8,128)(2,1)S(1)}, u32[]{:S(2)}, u32[]{:S(2)}) collective-permute-start(bf16[256,256]{1,0:T(8,128)(2,1)S(1)} %bitcast.33), channel_id=1, source_target_pairs={{0,96},{32,128},{64,160},{96,192},{128,224},{160,0},{192,32},{224,... | collective-permute-start | bytes 393224 | tf_op jit(solution)/shard_map/ppermute | solution.py:33
  17.4 4.5 %collective-permute-start.4 = (bf16[256,256]{1,0:T(8,128)(2,1)S(1)}, bf16[256,256]{1,0:T(8,128)(2,1)S(1)}, u32[]{:S(2)}, u32[]{:S(2)}) collective-permute-start(bf16[256,256]{1,0:T(8,128)(2,1)S(1)} %bitcast.35), channel_id=1, source_target_pairs={{0,160},{32,192},{64,224},{96,0},{128,32},{160,64},{192,96},{224,1... | collective-permute-start | bytes 393224 | tf_op jit(solution)/shard_map/ppermute | solution.py:33
  27.8 6.0 %collective-permute-done.2.refs_3_ = bf16[256,256]{1,0:T(8,128)(2,1)S(1)} collective-permute-done((bf16[256,256]{1,0:T(8,128)(2,1)S(1)}, bf16[256,256]{1,0:T(8,128)(2,1)S(1)}, u32[]{:S(2)}, u32[]{:S(2)}) %collective-permute-start.2) | collective-permute-done | bytes 131104 | tf_op jit(solution)/shard_map/ppermute | solution.py:33
  34.5 7.7 %collective-permute-done.5.refs_6_ = bf16[256,256]{1,0:T(8,128)(2,1)S(1)} collective-permute-done((bf16[256,256]{1,0:T(8,128)(2,1)S(1)}, bf16[256,256]{1,0:T(8,128)(2,1)S(1)}, u32[]{:S(2)}, u32[]{:S(2)}) %collective-permute-start.5) | collective-permute-done | bytes 131104 | tf_op jit(solution)/shard_map/ppermute | solution.py:33
  43.5 9.8 %stats.1 = f32[8,24,256]{2,1,0:T(8,128)} custom-call(bf16[256,256]{1,0:T(8,128)(2,1)} %bitcast.29, bf16[256,256]{1,0:T(8,128)(2,1)} %copy-done.4, bf16[256,256]{1,0:T(8,128)(2,1)} %copy-done.5, bf16[256,256]{1,0:T(8,128)(2,1)} %copy-done.6, bf16[256,256]{1,0:T(8,128)(2,1)} %copy-done.7, bf16[256,256]{1,0:T(8,128)(2,1)} %copy-done.8, ...), custom_call_target="tpu_custom_call" | custom-call | tf_op jit(solution)/shard_map/stats/pallas_call | solution.py:86
  53.2 4.8 %all-to-all-start.1 = ((f32[8,24,256]{2,1,0:T(8,128)}), f32[8,24,256]{2,1,0:T(8,128)S(1)}, u32[]{:S(2)}, u32[]{:S(2)}) async-start(f32[8,24,256]{2,1,0:T(8,128)} %stats.1), calls=%async_computation.1 | async-start | bytes 393216 | tf_op jit(solution)/shard_map/all_to_all | solution.py:24
  58.6 5.3 %all-to-all-done.1.refs_9_ = f32[8,24,256]{2,1,0:T(8,128)S(1)} async-done(((f32[8,24,256]{2,1,0:T(8,128)}), f32[8,24,256]{2,1,0:T(8,128)S(1)}, u32[]{:S(2)}, u32[]{:S(2)}) %all-to-all-start.1) | async-done | bytes 196640 | tf_op jit(solution)/shard_map/all_to_all | solution.py:24
  64.6 13.7 %grads.1 = (f32[256,256]{1,0:T(8,128)}, bf16[256,256]{1,0:T(8,128)(2,1)}, bf16[256,256]{1,0:T(8,128)(2,1)}, bf16[256,256]{1,0:T(8,128)(2,1)}, bf16[256,256]{1,0:...) custom-call(s32[8]{0:T(128)} %fusion.19.base_ref, ...), custom_call_target="tpu_custom_call" | custom-call | tf_op jit(solution)/shard_map/grads/pallas_call | solution.py:129
  78.3 4.6 %all-to-all-start.2 = ((f32[8,256,256]{2,1,0:T(8,128)}), f32[8,256,256]{2,1,0:T(8,128)S(1)}, u32[]{:S(2)}, u32[]{:S(2)}) async-start(f32[8,256,256]{2,1,0:T(8,128)} %get-tuple-element.12), calls=%async_computation.2 | async-start | bytes 4194304 | tf_op jit(solution)/shard_map/all_to_all | solution.py:24
  83.1 26.0 %all-to-all-done.2 = f32[8,256,256]{2,1,0:T(8,128)S(1)} async-done(((f32[8,256,256]{2,1,0:T(8,128)}), f32[8,256,256]{2,1,0:T(8,128)S(1)}, u32[]{:S(2)}, u32[]{:S(2)}) %all-to-all-start.2) | async-done | bytes 2097184 | tf_op jit(solution)/shard_map/all_to_all | solution.py:24
  132.2 11.6 %all-to-all-start.4 = ((s32[64,1,16]{2,1,0:T(1,128)}), s32[64,1,16]{2,1,0:T(1,128)S(1)}, u32[]{:S(2)}, u32[]{:S(2)}) async-start(s32[64,1,16]{2,1,0:T(1,128)} %bitcast.10), calls=%async_computation.4 | async-start | bytes 65536 | tf_op jit(solution)/shard_map/all_to_all | solution.py:24
  143.9 5.5 %collective-permute-start.16 = (f32[16,256]{1,0:T(8,128)S(1)}, f32[16,256]{1,0:T(8,128)S(1)}, u32[]{:S(2)}, u32[]{:S(2)}) collective-permute-start(f32[16,256]{1,0:T(8,128)S(1)} %add.124), channel_id=1, source_target_pairs={{0,128},{32,160},{64,192},{96,224},{128,0},{160,32},{192,64},{224,... | collective-permute-start | bytes 49160 | tf_op jit(solution)/shard_map/ppermute | solution.py:255
  149.3 4.0 %all-to-all-done.4 = s32[64,1,16]{2,1,0:T(1,128)S(1)} async-done(((s32[64,1,16]{2,1,0:T(1,128)}), s32[64,1,16]{2,1,0:T(1,128)S(1)}, u32[]{:S(2)}, u32[]{:S(2)}) %all-to-all-start.4) | async-done | bytes 4128 | tf_op jit(solution)/shard_map/all_to_all | solution.py:24
  156.6 3.2 %collective-permute-done.32 = s32[64,16]{1,0:T(8,128)S(1)} collective-permute-done((s32[64,16]{1,0:T(8,128)S(1)}, s32[64,16]{1,0:T(8,128)S(1)}, u32[]{:S(2)}, u32[]{:S(2)}) %collective-permute-start.32) | collective-permute-done | bytes 4128 | tf_op jit(solution)/shard_map/ppermute | solution.py:33
  161.2 3.1 %collective-permute-start.27 = (bf16[256,256]{1,0:T(8,128)(2,1)S(1)}, bf16[256,256]{1,0:T(8,128)(2,1)S(1)}, u32[]{:S(2)}, u32[]{:S(2)}) collective-permute-start(bf16[256,256]{1,0:T(8,128)(2,1)S(1)} %copy-done.27), channel_id=1, source_target_pairs={{0,128},{32,160},{64,192},{96,224},{128,0},{160,32},{192,64},{224,... | collective-permute-start | bytes 393224 | tf_op jit(solution)/shard_map/ppermute | solution.py:33
  170.6 10.4 %collective-permute-done.28.refs_5_ = bf16[256,256]{1,0:T(8,128)(2,1)S(1)} collective-permute-done((bf16[256,256]{1,0:T(8,128)(2,1)S(1)}, bf16[256,256]{1,0:T(8,128)(2,1)S(1)}, u32[]{:S(2)}, u32[]{:S(2)}) %collective-permute-start.28) | collective-permute-done | bytes 131104 | tf_op jit(solution)/shard_map/ppermute | solution.py:33
  181.0 7.7 %collective-permute-done.30.refs_7_ = bf16[256,256]{1,0:T(8,128)(2,1)S(1)} collective-permute-done((bf16[256,256]{1,0:T(8,128)(2,1)S(1)}, bf16[256,256]{1,0:T(8,128)(2,1)S(1)}, u32[]{:S(2)}, u32[]{:S(2)}) %collective-permute-start.30) | collective-permute-done | bytes 131104 | tf_op jit(solution)/shard_map/ppermute | solution.py:33
  189.3 3.2 %pack.1 = f32[4,64,8,128]{3,2,1,0:T(8,128)} custom-call(f32[256,256]{1,0:T(8,128)} %get-tuple-element.13.refs_0_, bf16[256,256]{1,0:T(8,128)(2,1)} %copy-done.12, bf16[256,256]{1,0:T(8,128)(2,1)} %copy-done.13, bf16[256,256]{1,0:T(8,128)(2,1)} %copy-done.14, bf16[256,256]{1,0:T(8,128)(2,1)} %copy-done.15, bf16[256,256]{1,0:T(8,128)(2,1)} %copy-done.16, ...), custom_call_target="tpu_custom_call" | custom-call | tf_op jit(solution)/shard_map/pack/pallas_call | solution.py:170
  192.5 7.2 %all-to-all-start.3 = ((f32[256,8,128]{2,1,0:T(8,128)}), f32[256,8,128]{2,1,0:T(8,128)S(1)}, u32[]{:S(2)}, u32[]{:S(2)}) async-start(f32[256,8,128]{2,1,0:T(8,128)} %bitcast.25), calls=%async_computation.3 | async-start | bytes 2097152 | tf_op jit(solution)/shard_map/all_to_all | solution.py:24
  211.1 4.3 %collective-permute-done.21 = f32[64,256]{1,0:T(8,128)S(1)} collective-permute-done((f32[64,256]{1,0:T(8,128)S(1)}, f32[64,256]{1,0:T(8,128)S(1)}, u32[]{:S(2)}, u32[]{:S(2)}) %collective-permute-start.21) | collective-permute-done | bytes 65568 | tf_op jit(solution)/shard_map/ppermute | solution.py:33
  216.8 3.3 %collective-permute-start.23 = (f32[256,256]{1,0:T(8,128)S(1)}, f32[256,256]{1,0:T(8,128)S(1)}, u32[]{:S(2)}, u32[]{:S(2)}) collective-permute-start(f32[256,256]{1,0:T(8,128)S(1)} %constant_dynamic-slice_fusion.1), channel_id=1, source_target_pairs={{0,4},{4,0},{1,5},{5,1},{2,6},{6,2},{3,7},{7,3},{8,12},{12,8},{9,1... | collective-permute-start | bytes 786440 | tf_op jit(solution)/shard_map/ppermute | solution.py:33
  220.8 10.0 %all-to-all-done.3 = f32[256,8,128]{2,1,0:T(8,128)S(1)} async-done(((f32[256,8,128]{2,1,0:T(8,128)}), f32[256,8,128]{2,1,0:T(8,128)S(1)}, u32[]{:S(2)}, u32[]{:S(2)}) %all-to-all-start.3) | async-done | bytes 1048608 | tf_op jit(solution)/shard_map/all_to_all | solution.py:24
  231.8 16.6 %table.1 = f32[64,4096]{1,0:T(8,128)} custom-call(f32[2048,128]{1,0:T(8,128)} %bitcast.26, s32[1,4096]{1,0:T(1,128)} %pad_add_fusion.ids_ref), custom_call_target="tpu_custom_call" | custom-call | tf_op jit(solution)/shard_map/table/pallas_call | solution.py:196
  (176 shorter events, 65.6 us)
Async XLA Ops:
  2.7 23.2 %all-to-all-start = ((bf16[8,256,256]{2,1,0:T(8,128)(2,1)}), bf16[8,256,256]{2,1,0:T(8,128)(2,1)S(1)}, u32[]{:S(2)}, u32[]{:S(2)}) async-start(bf16[8,256,256]{2,1,0:T(8,128)(2,1)} %broadcast_in_dim.12), calls=%async_computation | async-start | bytes 2097152 | tf_op jit(solution)/shard_map/all_to_all | solution.py:24
  9.4 13.2 %collective-permute-start = (bf16[256,256]{1,0:T(8,128)(2,1)S(1)}, bf16[256,256]{1,0:T(8,128)(2,1)S(1)}, u32[]{:S(2)}, u32[]{:S(2)}) collective-permute-start(bf16[256,256]{1,0:T(8,128)(2,1)S(1)} %bitcast.31), channel_id=1, source_target_pairs={{0,32},{32,64},{64,96},{96,128},{128,160},{160,192},{192,224},{224... | collective-permute-start | bytes 393224 | tf_op jit(solution)/shard_map/ppermute | solution.py:33
  10.2 14.8 %collective-permute-start.1 = (bf16[256,256]{1,0:T(8,128)(2,1)S(1)}, bf16[256,256]{1,0:T(8,128)(2,1)S(1)}, u32[]{:S(2)}, u32[]{:S(2)}) collective-permute-start(bf16[256,256]{1,0:T(8,128)(2,1)S(1)} %bitcast.32), channel_id=1, source_target_pairs={{0,64},{32,96},{64,128},{96,160},{128,192},{160,224},{192,0},{224,... | collective-permute-start | bytes 393224 | tf_op jit(solution)/shard_map/ppermute | solution.py:33
  13.2 20.7 %collective-permute-start.2 = (bf16[256,256]{1,0:T(8,128)(2,1)S(1)}, bf16[256,256]{1,0:T(8,128)(2,1)S(1)}, u32[]{:S(2)}, u32[]{:S(2)}) collective-permute-start(bf16[256,256]{1,0:T(8,128)(2,1)S(1)} %bitcast.33), channel_id=1, source_target_pairs={{0,96},{32,128},{64,160},{96,192},{128,224},{160,0},{192,32},{224,... | collective-permute-start | bytes 393224 | tf_op jit(solution)/shard_map/ppermute | solution.py:33
  16.9 17.5 %collective-permute-start.3 = (bf16[256,256]{1,0:T(8,128)(2,1)S(1)}, bf16[256,256]{1,0:T(8,128)(2,1)S(1)}, u32[]{:S(2)}, u32[]{:S(2)}) collective-permute-start(bf16[256,256]{1,0:T(8,128)(2,1)S(1)} %bitcast.34), channel_id=1, source_target_pairs={{0,128},{32,160},{64,192},{96,224},{128,0},{160,32},{192,64},{224,... | collective-permute-start | bytes 393224 | tf_op jit(solution)/shard_map/ppermute | solution.py:33
  17.4 17.1 %collective-permute-start.4 = (bf16[256,256]{1,0:T(8,128)(2,1)S(1)}, bf16[256,256]{1,0:T(8,128)(2,1)S(1)}, u32[]{:S(2)}, u32[]{:S(2)}) collective-permute-start(bf16[256,256]{1,0:T(8,128)(2,1)S(1)} %bitcast.35), channel_id=1, source_target_pairs={{0,160},{32,192},{64,224},{96,0},{128,32},{160,64},{192,96},{224,1... | collective-permute-start | bytes 393224 | tf_op jit(solution)/shard_map/ppermute | solution.py:33
  22.6 19.6 %collective-permute-start.5 = (bf16[256,256]{1,0:T(8,128)(2,1)S(1)}, bf16[256,256]{1,0:T(8,128)(2,1)S(1)}, u32[]{:S(2)}, u32[]{:S(2)}) collective-permute-start(bf16[256,256]{1,0:T(8,128)(2,1)S(1)} %bitcast.36), channel_id=1, source_target_pairs={{0,192},{32,224},{64,0},{96,32},{128,64},{160,96},{192,128},{224,1... | collective-permute-start | bytes 393224 | tf_op jit(solution)/shard_map/ppermute | solution.py:33
  25.0 17.6 %collective-permute-start.6 = (bf16[256,256]{1,0:T(8,128)(2,1)S(1)}, bf16[256,256]{1,0:T(8,128)(2,1)S(1)}, u32[]{:S(2)}, u32[]{:S(2)}) collective-permute-start(bf16[256,256]{1,0:T(8,128)(2,1)S(1)} %bitcast.37), channel_id=1, source_target_pairs={{0,224},{32,0},{64,32},{96,64},{128,96},{160,128},{192,160},{224,1... | collective-permute-start | bytes 393224 | tf_op jit(solution)/shard_map/ppermute | solution.py:33
  53.2 10.7 %all-to-all-start.1 = ((f32[8,24,256]{2,1,0:T(8,128)}), f32[8,24,256]{2,1,0:T(8,128)S(1)}, u32[]{:S(2)}, u32[]{:S(2)}) async-start(f32[8,24,256]{2,1,0:T(8,128)} %stats.1), calls=%async_computation.1 | async-start | bytes 393216 | tf_op jit(solution)/shard_map/all_to_all | solution.py:24
  78.3 30.8 %all-to-all-start.2 = ((f32[8,256,256]{2,1,0:T(8,128)}), f32[8,256,256]{2,1,0:T(8,128)S(1)}, u32[]{:S(2)}, u32[]{:S(2)}) async-start(f32[8,256,256]{2,1,0:T(8,128)} %get-tuple-element.12), calls=%async_computation.2 | async-start | bytes 4194304 | tf_op jit(solution)/shard_map/all_to_all | solution.py:24
  128.9 35.4 %collective-permute-start.24 = (bf16[256,256]{1,0:T(8,128)(2,1)S(1)}, bf16[256,256]{1,0:T(8,128)(2,1)S(1)}, u32[]{:S(2)}, u32[]{:S(2)}) collective-permute-start(bf16[256,256]{1,0:T(8,128)(2,1)S(1)} %copy-done.30), channel_id=1, source_target_pairs={{0,224},{32,0},{64,32},{96,64},{128,96},{160,128},{192,160},{224,1... | collective-permute-start | bytes 393224 | tf_op jit(solution)/shard_map/ppermute | solution.py:33
  129.0 35.4 %collective-permute-start.25 = (bf16[256,256]{1,0:T(8,128)(2,1)S(1)}, bf16[256,256]{1,0:T(8,128)(2,1)S(1)}, u32[]{:S(2)}, u32[]{:S(2)}) collective-permute-start(bf16[256,256]{1,0:T(8,128)(2,1)S(1)} %copy-done.29), channel_id=1, source_target_pairs={{0,192},{32,224},{64,0},{96,32},{128,64},{160,96},{192,128},{224,1... | collective-permute-start | bytes 393224 | tf_op jit(solution)/shard_map/ppermute | solution.py:33
  130.2 13.6 %collective-permute-start.15 = (f32[16,256]{1,0:T(8,128)S(1)}, f32[16,256]{1,0:T(8,128)S(1)}, u32[]{:S(2)}, u32[]{:S(2)}) collective-permute-start(f32[16,256]{1,0:T(8,128)S(1)} %add.123), channel_id=1, source_target_pairs={{0,64},{32,96},{64,0},{96,32},{128,192},{160,224},{192,128},{224,1... | collective-permute-start | bytes 49160 | tf_op jit(solution)/shard_map/ppermute | solution.py:255
  132.2 21.1 %all-to-all-start.4 = ((s32[64,1,16]{2,1,0:T(1,128)}), s32[64,1,16]{2,1,0:T(1,128)S(1)}, u32[]{:S(2)}, u32[]{:S(2)}) async-start(s32[64,1,16]{2,1,0:T(1,128)} %bitcast.10), calls=%async_computation.4 | async-start | bytes 65536 | tf_op jit(solution)/shard_map/all_to_all | solution.py:24
  143.9 23.1 %collective-permute-start.16 = (f32[16,256]{1,0:T(8,128)S(1)}, f32[16,256]{1,0:T(8,128)S(1)}, u32[]{:S(2)}, u32[]{:S(2)}) collective-permute-start(f32[16,256]{1,0:T(8,128)S(1)} %add.124), channel_id=1, source_target_pairs={{0,128},{32,160},{64,192},{96,224},{128,0},{160,32},{192,64},{224,... | collective-permute-start | bytes 49160 | tf_op jit(solution)/shard_map/ppermute | solution.py:255
  159.9 8.0 %collective-permute-start.26 = (bf16[256,256]{1,0:T(8,128)(2,1)S(1)}, bf16[256,256]{1,0:T(8,128)(2,1)S(1)}, u32[]{:S(2)}, u32[]{:S(2)}) collective-permute-start(bf16[256,256]{1,0:T(8,128)(2,1)S(1)} %copy-done.28), channel_id=1, source_target_pairs={{0,160},{32,192},{64,224},{96,0},{128,32},{160,64},{192,96},{224,1... | collective-permute-start | bytes 393224 | tf_op jit(solution)/shard_map/ppermute | solution.py:33
  161.2 9.4 %collective-permute-start.27 = (bf16[256,256]{1,0:T(8,128)(2,1)S(1)}, bf16[256,256]{1,0:T(8,128)(2,1)S(1)}, u32[]{:S(2)}, u32[]{:S(2)}) collective-permute-start(bf16[256,256]{1,0:T(8,128)(2,1)S(1)} %copy-done.27), channel_id=1, source_target_pairs={{0,128},{32,160},{64,192},{96,224},{128,0},{160,32},{192,64},{224,... | collective-permute-start | bytes 393224 | tf_op jit(solution)/shard_map/ppermute | solution.py:33
  164.3 16.6 %collective-permute-start.28 = (bf16[256,256]{1,0:T(8,128)(2,1)S(1)}, bf16[256,256]{1,0:T(8,128)(2,1)S(1)}, u32[]{:S(2)}, u32[]{:S(2)}) collective-permute-start(bf16[256,256]{1,0:T(8,128)(2,1)S(1)} %copy-done.26), channel_id=1, source_target_pairs={{0,96},{32,128},{64,160},{96,192},{128,224},{160,0},{192,32},{224,... | collective-permute-start | bytes 393224 | tf_op jit(solution)/shard_map/ppermute | solution.py:33
  164.5 16.5 %collective-permute-start.29 = (bf16[256,256]{1,0:T(8,128)(2,1)S(1)}, bf16[256,256]{1,0:T(8,128)(2,1)S(1)}, u32[]{:S(2)}, u32[]{:S(2)}) collective-permute-start(bf16[256,256]{1,0:T(8,128)(2,1)S(1)} %copy-done.25), channel_id=1, source_target_pairs={{0,64},{32,96},{64,128},{96,160},{128,192},{160,224},{192,0},{224,... | collective-permute-start | bytes 393224 | tf_op jit(solution)/shard_map/ppermute | solution.py:33
  167.0 21.6 %collective-permute-start.30 = (bf16[256,256]{1,0:T(8,128)(2,1)S(1)}, bf16[256,256]{1,0:T(8,128)(2,1)S(1)}, u32[]{:S(2)}, u32[]{:S(2)}) collective-permute-start(bf16[256,256]{1,0:T(8,128)(2,1)S(1)} %copy-done.24), channel_id=1, source_target_pairs={{0,32},{32,64},{64,96},{96,128},{128,160},{160,192},{192,224},{224... | collective-permute-start | bytes 393224 | tf_op jit(solution)/shard_map/ppermute | solution.py:33
  167.9 35.1 %collective-permute-start.17 = (f32[16,256]{1,0:T(8,128)S(1)}, f32[16,256]{1,0:T(8,128)S(1)}, u32[]{:S(2)}, u32[]{:S(2)}) collective-permute-start(f32[16,256]{1,0:T(8,128)S(1)} %get-tuple-element.24), channel_id=1, source_target_pairs={{0,24},{8,0},{16,8},{24,16},{1,25},{9,1},{17,9},{25,17},{2,26},{10... | collective-permute-start | bytes 49160 | tf_op jit(solution)/shard_map/ppermute | solution.py:33
  192.5 38.3 %all-to-all-start.3 = ((f32[256,8,128]{2,1,0:T(8,128)}), f32[256,8,128]{2,1,0:T(8,128)S(1)}, u32[]{:S(2)}, u32[]{:S(2)}) async-start(f32[256,8,128]{2,1,0:T(8,128)} %bitcast.25), calls=%async_computation.3 | async-start | bytes 2097152 | tf_op jit(solution)/shard_map/all_to_all | solution.py:24
  210.5 6.2 %collective-permute-start.22 = (f32[64,256]{1,0:T(8,128)S(1)}, f32[64,256]{1,0:T(8,128)S(1)}, u32[]{:S(2)}, u32[]{:S(2)}) collective-permute-start(f32[64,256]{1,0:T(8,128)S(1)} %get-tuple-element.22), channel_id=1, source_target_pairs={{0,1},{1,2},{2,3},{3,0},{4,5},{5,6},{6,7},{7,4},{8,9},{9,10},{10,1... | collective-permute-start | bytes 196616 | tf_op jit(solution)/shard_map/ppermute | solution.py:33
  216.8 31.6 %collective-permute-start.23 = (f32[256,256]{1,0:T(8,128)S(1)}, f32[256,256]{1,0:T(8,128)S(1)}, u32[]{:S(2)}, u32[]{:S(2)}) collective-permute-start(f32[256,256]{1,0:T(8,128)S(1)} %constant_dynamic-slice_fusion.1), channel_id=1, source_target_pairs={{0,4},{4,0},{1,5},{5,1},{2,6},{6,2},{3,7},{7,3},{8,12},{12,8},{9,1... | collective-permute-start | bytes 786440 | tf_op jit(solution)/shard_map/ppermute | solution.py:33
  (46 other events, 632.6 us)

commit v3 on v2

v3 whole, which is shorter than its diff:
```python
import jax
import jax.numpy as jnp
from jax import lax
from jax.experimental import pallas as pl
from jax.experimental.pallas import tpu as pltpu
from jax.sharding import Mesh
from jax.sharding import PartitionSpec as P

TABLE = 4096
CAP = 16
BLK = 256
ROWS = 8 * BLK
XK = ("x", "k")
KYX = ("k", "y", "x")
ZXK = ("z", "x", "k")
YZXK = ("y", "z", "x", "k")
F32 = jnp.float32
BF16 = jnp.bfloat16
VMEM = pl.BlockSpec(memory_space=pltpu.VMEM)
SMEM = pl.BlockSpec(memory_space=pltpu.SMEM)
PARAMS = pltpu.CompilerParams(vmem_limit_bytes=56 * 2**20)


def dot(left, right, dims):
    return lax.dot_general(left, right, ((dims[0:1], dims[1:2]), ((), ())), preferred_element_type=F32)


def exchange(value, axes):
    return lax.all_to_all(value, axes, 0, 0, tiled=True)


def to_all(value, axes):
    return exchange(jnp.broadcast_to(value[None], (lax.axis_size(axes), *value.shape)), axes)


def shifted(value, axis, step):
    count = lax.axis_size(axis)
    return lax.ppermute(value, axis, [(i, (i + step) % count) for i in range(count)])


def place(axis, step=0):
    return (lax.axis_index(axis).astype(jnp.uint32) + jnp.uint32(step)) & jnp.uint32(lax.axis_size(axis) - 1)


def rows_at(value, start, count):
    zero = jnp.uint32(0)
    return lax.dynamic_slice(value, (start,) + (zero,) * (value.ndim - 1), (count, *value.shape[1:]))


def summed_share(value, axis):
    count = lax.axis_size(axis)
    rows = value.shape[0] // count
    total = rows_at(value, place(axis) * jnp.uint32(rows), rows)
    for d in range(1, count):
        total = total + shifted(rows_at(value, place(axis, d) * jnp.uint32(rows), rows), axis, d)
    return total


def joined(value, axis):
    count = lax.axis_size(axis)
    tiles = [value] + [shifted(value, axis, d) for d in range(1, count)]
    rising = [tiles[-d % count] for d in range(count)]
    rows = value.shape[0]
    start = (jnp.uint32(count) - place(axis)) * jnp.uint32(rows)
    return rows_at(jnp.concatenate(rising + rising, axis=0), start, count * rows)


def stats_kernel(at_ref, items_ref, users_ref, own_ref, out_ref, even_ref, odd_ref):
    def score(c, buffer):
        users = users_ref[pl.ds(pl.multiple_of(at_ref[c], BLK), BLK), :]
        buffer[...] = dot(items_ref[...], users, (1, 1))

    def reduce(c, buffer):
        top = jnp.max(buffer[...], axis=0, keepdims=True)
        out_ref[0, pl.ds(c, 1), :] = top
        out_ref[0, pl.ds(8 + c, 1), :] = jnp.sum(jnp.exp(buffer[...] - top), axis=0, keepdims=True)

    score(0, even_ref)

    def step(i, carry):
        score(2 * i + 1, odd_ref)
        reduce(2 * i, even_ref)
        score(jnp.minimum(2 * i + 2, 7), even_ref)
        reduce(2 * i + 1, odd_ref)
        return carry

    lax.fori_loop(0, 4, step, 0)
    out_ref[0, 16:24, :] = own_ref[...]
    for p in range(1, 8):
        out_ref[p] = out_ref[0]


def stats(at, items, users, own):
    return pl.pallas_call(
        stats_kernel,
        in_specs=[SMEM, VMEM, VMEM, VMEM],
        out_shape=jax.ShapeDtypeStruct((8, 24, BLK), F32),
        scratch_shapes=[pltpu.VMEM((ROWS, BLK), F32)] * 2,
        compiler_params=PARAMS,
        name="stats",
    )(at, items, users, own)


def grads_kernel(
    at_ref, items_ref, users_ref, got_ref, gi_ref, keep_ref, give_ref,
    acc_ref, turned_ref, index_ref, even_ref, odd_ref, deven_ref, dodd_ref,
):
    turned_ref[...] = items_ref[...].T
    spot = lax.broadcasted_iota(jnp.int32, (ROWS, BLK), 0)
    index_ref[...] = (spot // BLK) * ROWS + spot % BLK + at_ref[16]
    acc_ref[...] = jnp.zeros_like(acc_ref)

    def chunk(c):
        return users_ref[pl.ds(pl.multiple_of(at_ref[c], BLK), BLK), :]

    def score(c, buffer):
        buffer[...] = dot(items_ref[...], chunk(c), (1, 1))

    def weigh(c, buffer, dbuffer):
        tops = got_ref[:, pl.ds(c, 1), :].reshape(8, BLK)
        parts = got_ref[:, pl.ds(8 + c, 1), :].reshape(8, BLK)
        top = jnp.max(tops, axis=0, keepdims=True)
        total = top + jnp.log(jnp.sum(parts * jnp.exp(tops - top), axis=0, keepdims=True))
        weight = got_ref[c, 16:17, :]
        target = got_ref[c, 17:18, :].astype(jnp.int32)
        chosen = (index_ref[...] == target).astype(F32)
        dbuffer[...] = (weight * (jnp.exp(buffer[...] - total) - chosen)).astype(BF16)

    def multiply(c, dbuffer):
        part = dot(turned_ref[...], dbuffer[...], (1, 0))
        slot = at_ref[8 + c]

        @pl.when(slot < 4)
        def _():
            keep_ref[slot] = part

        @pl.when(slot >= 4)
        def _():
            give_ref[slot - 4] = part

        acc_ref[...] += dot(dbuffer[...], chunk(c), (1, 0))

    score(0, even_ref)
    weigh(0, even_ref, deven_ref)
    score(1, odd_ref)

    def step(i, carry):
        weigh(2 * i + 1, odd_ref, dodd_ref)
        score(2 * i + 2, even_ref)
        multiply(2 * i, deven_ref)
        weigh(2 * i + 2, even_ref, deven_ref)
        score(2 * i + 3, odd_ref)
        multiply(2 * i + 1, dodd_ref)
        return carry

    lax.fori_loop(0, 3, step, 0)
    weigh(7, odd_ref, dodd_ref)
    multiply(6, deven_ref)
    multiply(7, dodd_ref)
    gi_ref[...] = acc_ref[...].astype(BF16)


def grads(at, items, users, got):
    share = jax.ShapeDtypeStruct((4, 256, BLK), F32)
    return pl.pallas_call(
        grads_kernel,
        in_specs=[SMEM, VMEM, VMEM, VMEM],
        out_shape=[jax.ShapeDtypeStruct((ROWS, 256), BF16), share, share],
        scratch_shapes=[
            pltpu.VMEM((ROWS, 256), F32),
            pltpu.VMEM((256, ROWS), BF16),
            pltpu.VMEM((ROWS, BLK), jnp.int32),
            pltpu.VMEM((ROWS, BLK), F32),
            pltpu.VMEM((ROWS, BLK), F32),
            pltpu.VMEM((ROWS, BLK), BF16),
            pltpu.VMEM((ROWS, BLK), BF16),
        ],
        compiler_params=PARAMS,
        name="grads",
    )(at, items, users, got)


def thirds(value):
    high = value.astype(BF16)
    rest = value - high.astype(F32)
    middle = rest.astype(BF16)
    return high, middle, (rest - middle.astype(F32)).astype(BF16)


def pack_kernel(parts_ref, owner_ref, rank_ref, out_ref):
    value = jnp.sum(parts_ref[...].astype(F32), axis=0)
    pieces = thirds(value)
    lane = lax.broadcasted_iota(jnp.int32, (64 * 8, BLK), 0)
    halves = []
    for h in range(2):
        rank = rank_ref[...] - 8 * h
        slot = jnp.where((rank >= 0) & (rank < 8), owner_ref[...] * 8 + rank, -1)
        pick = (lane == slot).astype(F32).astype(BF16)
        halves.append(sum(dot(pick, piece, (1, 0)) for piece in pieces))
    for g in range(4):
        share = slice(64 * g, 64 * g + 64)
        both = jnp.concatenate([halves[0][:, share], halves[1][:, share]], axis=1)
        out_ref[g] = both.reshape(64, 8, 128)


def pack(parts, owner, rank):
    return pl.pallas_call(
        pack_kernel,
        in_specs=[VMEM] * 3,
        out_shape=jax.ShapeDtypeStruct((4, 64, 8, 128), F32),
        compiler_params=PARAMS,
        name="pack",
    )(parts, owner, rank)


def table_kernel(got_ref, ids_ref, out_ref, pick_ref, kept_ref):
    both = got_ref[...].T
    value = jnp.concatenate([both[:64], both[64:]], axis=1)
    pieces = jnp.concatenate(thirds(value), axis=0)
    ids = ids_ref[...]
    upper = ids >> 8
    lower = ids & 255
    pick = (lax.broadcasted_iota(jnp.int32, (256, TABLE), 0) == lower).astype(F32).astype(BF16)
    pick_ref[...] = pick.T

    def step(j, carry):
        for q in range(4):
            keep = jnp.broadcast_to((upper == 4 * j + q).astype(F32), (16, TABLE)).astype(BF16)
            kept_ref[q * 192 : (q + 1) * 192, :] = pieces * jnp.concatenate([keep] * 12, axis=0)
        part = dot(kept_ref[...], pick_ref[...], (1, 0))
        for q in range(4):
            at = pl.multiple_of((4 * j + q) * 256, 256)
            own = part[q * 192 : (q + 1) * 192]
            out_ref[:, pl.ds(at, 256)] = own[:64] + own[64:128] + own[128:]
        return carry

    lax.fori_loop(0, 4, step, 0)


def table(got, ids):
    return pl.pallas_call(
        table_kernel,
        in_specs=[VMEM] * 2,
        out_shape=jax.ShapeDtypeStruct((64, TABLE), F32),
        scratch_shapes=[pltpu.VMEM((TABLE, 256), BF16), pltpu.VMEM((768, TABLE), BF16)],
        compiler_params=PARAMS,
        name="table",
    )(got, ids)


def tower(features, w_first, w_second):
    pre_act = jnp.dot(features, w_first, preferred_element_type=F32)
    hidden = jax.nn.silu(pre_act).astype(BF16)
    return pre_act, hidden, jnp.dot(hidden, w_second, preferred_element_type=F32).astype(BF16)


def step_body(
    user_features, w_first, w_second, item_embed, example_weight, positive, item_owner, item_row
):
    features = user_features[0]
    owner = item_owner.reshape(1, BLK)
    items = to_all(item_embed[0], "z").reshape(ROWS, 256)
    pair = jnp.concatenate([features, shifted(features, "k", 1)], axis=0)
    block = jnp.concatenate([pair] + [shifted(pair, "x", d) for d in range(1, 4)], axis=0)
    _, _, users = tower(block, w_first, w_second)
    chunk = jnp.arange(8, dtype=jnp.int32)
    other = (chunk % 2) ^ lax.axis_index("k")
    back = (lax.axis_index("x") - chunk // 2) & 3
    ahead = (chunk // 2 - lax.axis_index("x")) & 3
    base = (lax.axis_index(XK) * BLK).reshape(1)
    at = jnp.concatenate([(2 * back + other) * BLK, ahead + 4 * other, base]).astype(jnp.int32)

    member = (owner == lax.broadcasted_iota(jnp.int32, (64, 1), 0)).astype(F32)
    order = lax.broadcasted_iota(jnp.int32, (BLK, BLK), 0) < lax.broadcasted_iota(jnp.int32, (BLK, BLK), 1)
    before = dot(member.astype(BF16), order.astype(BF16), (1, 0))
    rank = jnp.sum(before * member, axis=0, keepdims=True).astype(jnp.int32)
    slot = owner * CAP + rank
    held = (slot == lax.broadcasted_iota(jnp.int32, (64 * CAP, 1), 0)).astype(jnp.int32)
    rows = jnp.sum(held * (item_row + 1), axis=1) - 1
    ids = exchange(rows.reshape(64, CAP), ZXK)
    ids = joined(ids, "y")
    ids = jnp.concatenate([ids[:, :8].reshape(1, -1), ids[:, 8:].reshape(1, -1)], axis=1)

    own = jnp.concatenate(
        [example_weight, positive.astype(F32), jnp.zeros((6, BLK), F32)], axis=0
    )
    got = exchange(stats(at[:8], items, users, own), XK)
    gi, keep, give = grads(at, items, users, got)
    gi = exchange(gi.reshape(8, BLK, 256), "z")
    gu = keep + shifted(give, "k", 1)
    grad_user = gu[0]
    for d in range(1, 4):
        grad_user = grad_user + shifted(gu[d], "x", d)
    grad_user = grad_user.T.astype(BF16)

    pre_act, hidden, _ = tower(features, w_first, w_second)
    d_second = dot(hidden, grad_user, (0, 0))
    back_grad = dot(grad_user, w_second, (1, 1))
    gate = jax.nn.sigmoid(pre_act)
    grad_pre = (back_grad * gate * (1.0 + pre_act * (1.0 - gate))).astype(BF16)
    d_first = dot(features, grad_pre, (0, 0))
    both = jnp.concatenate([d_first, d_second], axis=0)
    both = summed_share(both, "k")
    both = summed_share(both, "y")
    both = summed_share(both, "x")
    for step in (1, 2, 4):
        both = both + lax.ppermute(both, "z", [(i, i ^ step) for i in range(8)])

    send = pack(gi, owner, rank).reshape(256, 8, 128)
    came = exchange(send, YZXK).reshape(256 * 8, 128)
    both = to_all(both, KYX).reshape(512, 256)
    grad_table = table(came, ids).T
    return both[:256], both[256:], grad_table


def solution(mesh):
    torus = Mesh(mesh.devices.reshape(8, 4, 2, mesh.shape["grp"]), ("z", "x", "k", "y"))
    rows = ("z", "x", "k")
    placed = (
        P("y", rows, None),
        P(),
        P(),
        P("y", rows, None),
        P("y", rows),
        P("y", rows),
        P("y", rows, None),
        P("y", rows),
    )
    return jax.shard_map(
        step_body, mesh=torus, in_specs=placed, out_specs=(P(), P(), P(rows, "y")), check_vma=False
    )
```

time: 250 us -> 213 us (0.85)
  starting transfers between devices: 90.7 us -> 72.3 us
  waiting for transfers between devices: 100 us -> 84.5 us
  Pallas kernels: 43.2 us -> 38.7 us
    ppermute x31 -> x18, waiting for transfers between devices: 55.1 us -> 29.2 us  [shifted(): lax.ppermute(value, axis, [(i, (i + step) % count) for i in range(count)])]
    ppermute x31 -> x18, starting transfers between devices: 45.9 us -> 21.9 us  [shifted(): lax.ppermute(value, axis, [(i, (i + step) % count) for i in range(count)])]
    ppermute x3, waiting for transfers between devices: 0.01 us -> 8.89 us  [step_body(): both = both + lax.ppermute(both, 'z', [(i, i ^ step) for i in range(8)])]
    all_to_all x5 -> x6, starting transfers between devices: 34.9 us -> 41.7 us  [exchange(): return lax.all_to_all(value, axes, 0, 0, tiled=True)]
    pallas_call x4, Pallas kernels: 43.2 us -> 38.7 us  [the longest x1 16.8 us: grads(): pl.pallas_call(grads_kernel, in_specs=[SMEM, VMEM, VMEM, VMEM], out_shape...]
    all_to_all x5 -> x6, waiting for transfers between devices: 45.3 us -> 46.4 us  [exchange(): return lax.all_to_all(value, axes, 0, 0, tiled=True)]
  transfers between devices with their start and end apart: 39 -> 27, of which waited for: 24 -> 23; matrix products, arithmetic and copies ran while one was open for 3% -> 4% of each run, Pallas kernels for 8% -> 1%
where the time goes in v3:
time: 213 us; the launch traced here: 212 us
  waiting for transfers between devices  84.5 us (40%)
  starting transfers between devices  72.3 us (34%)
  Pallas kernels  38.7 us (18%)
  local copies, waits for them, and re-layouts  8.28 us (4%)
  other arithmetic  4.85 us (2%)
  matrix products  2.89 us (1%)
    all_to_all x6, waiting for transfers between devices, exchange(): return lax.all_to_all(value, axes, 0, 0, tiled=True)  46.4 us
    all_to_all x6, starting transfers between devices, exchange(): return lax.all_to_all(value, axes, 0, 0, tiled=True)  41.7 us
    ppermute x18, waiting for transfers between devices, shifted(): lax.ppermute(value, axis, [(i, (i + step) % count) for i in range(count)])  29.2 us
    ppermute x18, starting transfers between devices, shifted(): lax.ppermute(value, axis, [(i, (i + step) % count) for i in range(count)])  21.9 us
    pallas_call x1, Pallas kernels, grads(): pl.pallas_call(grads_kernel, in_specs=[SMEM, VMEM, VMEM, VMEM], out_shape...  16.8 us
    pallas_call x1, Pallas kernels, table(): pl.pallas_call(table_kernel, in_specs=[VMEM] * 2, out_shape=jax.ShapeDtyp...  10.3 us
    ppermute x3, waiting for transfers between devices, step_body(): both = both + lax.ppermute(both, 'z', [(i, i ^ step) for i in range(8)])  8.89 us
    ppermute x3, starting transfers between devices, step_body(): both = both + lax.ppermute(both, 'z', [(i, i ^ step) for i in range(8)])  8.77 us
  transfers between devices with their start and end apart: 27, of which 23 were waited for; matrix products, arithmetic and copies ran while one was open for 4% of the time, Pallas kernels for 1%

profile of v3, /device:TPU:1, one launch (start us, length us, event | category | flops | bytes accessed | tf_op | source)
XLA Modules:
  0.0 212.5 jit_solution(17261137459876428187)
XLA Ops:
  2.6 9.1 %all-to-all-start = ((bf16[8,256,256]{2,1,0:T(8,128)(2,1)}), bf16[8,256,256]{2,1,0:T(8,128)(2,1)S(1)}, u32[]{:S(2)}, u32[]{:S(2)}) async-start(bf16[8,256,256]{2,1,0:T(8,128)(2,1)} %broadcast_in_dim.18), calls=%async_computation | async-start | bytes 2097152 | tf_op jit(solution)/shard_map/all_to_all | solution.py:29
  15.8 2.5 %collective-permute-start.2 = (bf16[512,256]{1,0:T(8,128)(2,1)S(1)}, bf16[512,256]{1,0:T(8,128)(2,1)S(1)}, u32[]{:S(2)}, u32[]{:S(2)}) collective-permute-start(bf16[512,256]{1,0:T(8,128)(2,1)S(1)} %pad_maximum_fusion), channel_id=1, source_target_pairs={{0,16},{8,24},{16,0},{24,8},{1,17},{9,25},{17,1},{25,9},{2,18},{10... | collective-permute-start | bytes 786440 | tf_op jit(solution)/shard_map/ppermute | solution.py:38
  19.9 2.7 %collective-permute-done.1 = bf16[512,256]{1,0:T(8,128)(2,1)S(1)} collective-permute-done((bf16[512,256]{1,0:T(8,128)(2,1)S(1)}, bf16[512,256]{1,0:T(8,128)(2,1)S(1)}, u32[]{:S(2)}, u32[]{:S(2)}) %collective-permute-start.1) | collective-permute-done | bytes 262176 | tf_op jit(solution)/shard_map/ppermute | solution.py:38
  22.6 6.6 %collective-permute-done.2 = bf16[512,256]{1,0:T(8,128)(2,1)S(1)} collective-permute-done((bf16[512,256]{1,0:T(8,128)(2,1)S(1)}, bf16[512,256]{1,0:T(8,128)(2,1)S(1)}, u32[]{:S(2)}, u32[]{:S(2)}) %collective-permute-start.2) | collective-permute-done | bytes 262176 | tf_op jit(solution)/shard_map/ppermute | solution.py:38
  31.1 9.8 %all-to-all-done = bf16[8,256,256]{2,1,0:T(8,128)(2,1)S(1)} async-done(((bf16[8,256,256]{2,1,0:T(8,128)(2,1)}), bf16[8,256,256]{2,1,0:T(8,128)(2,1)S(1)}, u32[]{:S(2)}, u32[]{:S(2)}) %all-to-all-start) | async-done | bytes 1048608 | tf_op jit(solution)/shard_map/all_to_all | solution.py:29
  41.9 8.5 %stats.1 = f32[8,24,256]{2,1,0:T(8,128)} custom-call(s32[8]{0:T(128)} %add_multiply_fusion.at_ref, bf16[2048,256]{1,0:T(8,128)(2,1)} %bitcast.46, bf16[2048,256]{1,0:T(8,128)(2,1)} %convolution_convert_fusion.users_ref, f32[8,256]{1,0:T(8,128)} %maximum_maximum_fusion.own_ref), custom_call_target="tpu_custom_call" | custom-call | tf_op jit(solution)/shard_map/stats/pallas_call | solution.py:94
  50.4 4.8 %all-to-all-start.1 = ((f32[8,24,256]{2,1,0:T(8,128)}), f32[8,24,256]{2,1,0:T(8,128)S(1)}, u32[]{:S(2)}, u32[]{:S(2)}) async-start(f32[8,24,256]{2,1,0:T(8,128)} %stats.1), calls=%async_computation.1 | async-start | bytes 393216 | tf_op jit(solution)/shard_map/all_to_all | solution.py:29
  55.8 5.2 %all-to-all-done.1.got_ref = f32[8,24,256]{2,1,0:T(8,128)S(1)} async-done(((f32[8,24,256]{2,1,0:T(8,128)}), f32[8,24,256]{2,1,0:T(8,128)S(1)}, u32[]{:S(2)}, u32[]{:S(2)}) %all-to-all-start.1) | async-done | bytes 196640 | tf_op jit(solution)/shard_map/all_to_all | solution.py:29
  61.7 16.8 %grads.1 = (bf16[2048,256]{1,0:T(8,128)(2,1)}, f32[4,256,256]{2,1,0:T(8,128)}, f32[4,256,256]{2,1,0:T(8,128)}) custom-call(s32[17]{0:T(128)} %pad_add_fusion.1.at_ref, bf16[2048,256]{1,0:T(8,128)(2,1)} %bitcast.47, bf16[2048,256]{1,0:T(8,128)(2,1)} %convolution_convert_fusion.users_ref, f32[8,24,256]{2,1,0:T(8,128)} %copy-done.5), custom_call_target="tpu_custom_call" | custom-call | tf_op jit(solution)/shard_map/grads/pallas_call | solution.py:165
  87.0 5.6 %all-to-all-start.5 = ((s32[64,1,16]{2,1,0:T(1,128)}), s32[64,1,16]{2,1,0:T(1,128)S(1)}, u32[]{:S(2)}, u32[]{:S(2)}) async-start(s32[64,1,16]{2,1,0:T(1,128)} %bitcast.18), calls=%async_computation.5 | async-start | bytes 65536 | tf_op jit(solution)/shard_map/all_to_all | solution.py:29
  92.8 4.5 %collective-permute-done.6 = f32[256,256]{1,0:T(8,128)S(1)} collective-permute-done((f32[256,256]{1,0:T(8,128)S(1)}, f32[256,256]{1,0:T(8,128)S(1)}, u32[]{:S(2)}, u32[]{:S(2)}) %collective-permute-start.6) | collective-permute-done | bytes 262176 | tf_op jit(solution)/shard_map/ppermute | solution.py:38
  98.5 3.4 %all-to-all-done.5 = s32[64,1,16]{2,1,0:T(1,128)S(1)} async-done(((s32[64,1,16]{2,1,0:T(1,128)}), s32[64,1,16]{2,1,0:T(1,128)S(1)}, u32[]{:S(2)}, u32[]{:S(2)}) %all-to-all-start.5) | async-done | bytes 4128 | tf_op jit(solution)/shard_map/all_to_all | solution.py:29
  101.9 3.6 %all-to-all-start.3 = ((bf16[8,256,256]{2,1,0:T(8,128)(2,1)}), bf16[8,256,256]{2,1,0:T(8,128)(2,1)S(1)}, u32[]{:S(2)}, u32[]{:S(2)}) async-start(bf16[8,256,256]{2,1,0:T(8,128)(2,1)} %bitcast.11), calls=%async_computation.3 | async-start | bytes 2097152 | tf_op jit(solution)/shard_map/all_to_all | solution.py:29
  108.3 3.0 %collective-permute-start.10 = (f32[64,256]{1,0:T(8,128)S(1)}, f32[64,256]{1,0:T(8,128)S(1)}, u32[]{:S(2)}, u32[]{:S(2)}) collective-permute-start(f32[64,256]{1,0:T(8,128)S(1)} %get-tuple-element.16), channel_id=1, source_target_pairs={{0,2},{1,3},{2,0},{3,1},{4,6},{5,7},{6,4},{7,5},{8,10},{9,11},{10,... | collective-permute-start | bytes 196616 | tf_op jit(solution)/shard_map/ppermute | solution.py:38
  123.4 5.4 %collective-permute-done.15 = f32[16,256]{1,0:T(8,128)S(1)} collective-permute-done((f32[16,256]{1,0:T(8,128)S(1)}, f32[16,256]{1,0:T(8,128)S(1)}, u32[]{:S(2)}, u32[]{:S(2)}) %collective-permute-start.15) | collective-permute-done | bytes 16416 | tf_op jit(solution)/shard_map/ppermute | solution.py:307
  132.8 4.9 %collective-permute-start.17 = (f32[16,256]{1,0:T(8,128)S(1)}, f32[16,256]{1,0:T(8,128)S(1)}, u32[]{:S(2)}, u32[]{:S(2)}) collective-permute-start(f32[16,256]{1,0:T(8,128)S(1)} %add.141), channel_id=1, source_target_pairs={{0,128},{32,160},{64,192},{96,224},{128,0},{160,32},{192,64},{224,... | collective-permute-start | bytes 49160 | tf_op jit(solution)/shard_map/ppermute | solution.py:307
  140.3 10.0 %all-to-all-start.2 = ((f32[32,16,256]{2,1,0:T(8,128)}), f32[32,16,256]{2,1,0:T(8,128)S(1)}, u32[]{:S(2)}, u32[]{:S(2)}) async-start(f32[32,16,256]{2,1,0:T(8,128)} %broadcast_in_dim.20), calls=%async_computation.2 | async-start | bytes 1048576 | tf_op jit(solution)/shard_map/all_to_all | solution.py:29
  150.9 3.1 %pack.1 = f32[4,64,8,128]{3,2,1,0:T(8,128)} custom-call(bf16[8,256,256]{2,1,0:T(8,128)(2,1)} %copy-done.2, s32[1,256]{1,0:T(1,128)} %bitcast.60, s32[1,256]{1,0:T(1,128)} %bitcast.63), custom_call_target="tpu_custom_call" | custom-call | tf_op jit(solution)/shard_map/pack/pallas_call | solution.py:207
  154.0 7.4 %all-to-all-done.2 = f32[32,16,256]{2,1,0:T(8,128)S(1)} async-done(((f32[32,16,256]{2,1,0:T(8,128)}), f32[32,16,256]{2,1,0:T(8,128)S(1)}, u32[]{:S(2)}, u32[]{:S(2)}) %all-to-all-start.2) | async-done | bytes 524320 | tf_op jit(solution)/shard_map/all_to_all | solution.py:29
  161.5 8.6 %all-to-all-start.4 = ((f32[256,8,128]{2,1,0:T(8,128)}), f32[256,8,128]{2,1,0:T(8,128)S(1)}, u32[]{:S(2)}, u32[]{:S(2)}) async-start(f32[256,8,128]{2,1,0:T(8,128)} %bitcast.48), calls=%async_computation.4 | async-start | bytes 2097152 | tf_op jit(solution)/shard_map/all_to_all | solution.py:29
  170.1 2.7 %collective-permute-start.18 = (s32[64,16]{1,0:T(8,128)S(1)}, s32[64,16]{1,0:T(8,128)S(1)}, u32[]{:S(2)}, u32[]{:S(2)}) collective-permute-start(s32[64,16]{1,0:T(8,128)S(1)} %bitcast.56), channel_id=1, source_target_pairs={{0,3},{1,0},{2,1},{3,2},{4,7},{5,4},{6,5},{7,6},{8,11},{9,8},{10,9... | collective-permute-start | bytes 12296 | tf_op jit(solution)/shard_map/ppermute | solution.py:38
  174.1 3.6 %collective-permute-done.19 = s32[64,16]{1,0:T(8,128)S(1)} collective-permute-done((s32[64,16]{1,0:T(8,128)S(1)}, s32[64,16]{1,0:T(8,128)S(1)}, u32[]{:S(2)}, u32[]{:S(2)}) %collective-permute-start.19) | collective-permute-done | bytes 4128 | tf_op jit(solution)/shard_map/ppermute | solution.py:38
  180.8 20.5 %all-to-all-done.4 = f32[256,8,128]{2,1,0:T(8,128)S(1)} async-done(((f32[256,8,128]{2,1,0:T(8,128)}), f32[256,8,128]{2,1,0:T(8,128)S(1)}, u32[]{:S(2)}, u32[]{:S(2)}) %all-to-all-start.4) | async-done | bytes 1048608 | tf_op jit(solution)/shard_map/all_to_all | solution.py:29
  202.2 10.3 %table.1 = f32[64,4096]{1,0:T(8,128)} custom-call(f32[2048,128]{1,0:T(8,128)} %bitcast.49, s32[1,4096]{1,0:T(1,128)} %pad_add_fusion.ids_ref), custom_call_target="tpu_custom_call" | custom-call | tf_op jit(solution)/shard_map/table/pallas_call | solution.py:241
  (108 shorter events, 49.0 us)
Async XLA Ops:
  2.6 38.3 %all-to-all-start = ((bf16[8,256,256]{2,1,0:T(8,128)(2,1)}), bf16[8,256,256]{2,1,0:T(8,128)(2,1)S(1)}, u32[]{:S(2)}, u32[]{:S(2)}) async-start(bf16[8,256,256]{2,1,0:T(8,128)(2,1)} %broadcast_in_dim.18), calls=%async_computation | async-start | bytes 2097152 | tf_op jit(solution)/shard_map/all_to_all | solution.py:29
  13.8 8.8 %collective-permute-start.1 = (bf16[512,256]{1,0:T(8,128)(2,1)S(1)}, bf16[512,256]{1,0:T(8,128)(2,1)S(1)}, u32[]{:S(2)}, u32[]{:S(2)}) collective-permute-start(bf16[512,256]{1,0:T(8,128)(2,1)S(1)} %pad_maximum_fusion), channel_id=1, source_target_pairs={{0,8},{8,16},{16,24},{24,0},{1,9},{9,17},{17,25},{25,1},{2,10},{10... | collective-permute-start | bytes 786440 | tf_op jit(solution)/shard_map/ppermute | solution.py:38
  15.8 13.4 %collective-permute-start.2 = (bf16[512,256]{1,0:T(8,128)(2,1)S(1)}, bf16[512,256]{1,0:T(8,128)(2,1)S(1)}, u32[]{:S(2)}, u32[]{:S(2)}) collective-permute-start(bf16[512,256]{1,0:T(8,128)(2,1)S(1)} %pad_maximum_fusion), channel_id=1, source_target_pairs={{0,16},{8,24},{16,0},{24,8},{1,17},{9,25},{17,1},{25,9},{2,18},{10... | collective-permute-start | bytes 786440 | tf_op jit(solution)/shard_map/ppermute | solution.py:38
  18.8 10.5 %collective-permute-start.3 = (bf16[512,256]{1,0:T(8,128)(2,1)S(1)}, bf16[512,256]{1,0:T(8,128)(2,1)S(1)}, u32[]{:S(2)}, u32[]{:S(2)}) collective-permute-start(bf16[512,256]{1,0:T(8,128)(2,1)S(1)} %pad_maximum_fusion), channel_id=1, source_target_pairs={{0,24},{8,0},{16,8},{24,16},{1,25},{9,1},{17,9},{25,17},{2,26},{10... | collective-permute-start | bytes 786440 | tf_op jit(solution)/shard_map/ppermute | solution.py:38
  50.4 10.6 %all-to-all-start.1 = ((f32[8,24,256]{2,1,0:T(8,128)}), f32[8,24,256]{2,1,0:T(8,128)S(1)}, u32[]{:S(2)}, u32[]{:S(2)}) async-start(f32[8,24,256]{2,1,0:T(8,128)} %stats.1), calls=%async_computation.1 | async-start | bytes 393216 | tf_op jit(solution)/shard_map/all_to_all | solution.py:29
  78.5 3.5 %collective-permute-start.4 = (f32[4,256,256]{2,1,0:T(8,128)}, f32[4,256,256]{2,1,0:T(8,128)S(1)}, u32[]{:S(2)}, u32[]{:S(2)}) collective-permute-start(f32[4,256,256]{2,1,0:T(8,128)} %get-tuple-element.7), channel_id=1, source_target_pairs={{0,4},{4,0},{1,5},{5,1},{2,6},{6,2},{3,7},{7,3},{8,12},{12,8},{9,1... | collective-permute-start | bytes 3145736 | tf_op jit(solution)/shard_map/ppermute | solution.py:38
  83.4 9.4 %collective-permute-start.5 = (f32[256,256]{1,0:T(8,128)S(1)}, f32[256,256]{1,0:T(8,128)S(1)}, u32[]{:S(2)}, u32[]{:S(2)}) collective-permute-start(f32[256,256]{1,0:T(8,128)S(1)} %get-tuple-element.9), channel_id=1, source_target_pairs={{0,8},{8,16},{16,24},{24,0},{1,9},{9,17},{17,25},{25,1},{2,10},{10... | collective-permute-start | bytes 786440 | tf_op jit(solution)/shard_map/ppermute | solution.py:38
  83.8 13.5 %collective-permute-start.6 = (f32[256,256]{1,0:T(8,128)S(1)}, f32[256,256]{1,0:T(8,128)S(1)}, u32[]{:S(2)}, u32[]{:S(2)}) collective-permute-start(f32[256,256]{1,0:T(8,128)S(1)} %get-tuple-element.11), channel_id=1, source_target_pairs={{0,16},{8,24},{16,0},{24,8},{1,17},{9,25},{17,1},{25,9},{2,18},{10... | collective-permute-start | bytes 786440 | tf_op jit(solution)/shard_map/ppermute | solution.py:38
  85.6 12.8 %collective-permute-start.7 = (f32[256,256]{1,0:T(8,128)S(1)}, f32[256,256]{1,0:T(8,128)S(1)}, u32[]{:S(2)}, u32[]{:S(2)}) collective-permute-start(f32[256,256]{1,0:T(8,128)S(1)} %get-tuple-element.10), channel_id=1, source_target_pairs={{0,24},{8,0},{16,8},{24,16},{1,25},{9,1},{17,9},{25,17},{2,26},{10... | collective-permute-start | bytes 786440 | tf_op jit(solution)/shard_map/ppermute | solution.py:38
  87.0 14.9 %all-to-all-start.5 = ((s32[64,1,16]{2,1,0:T(1,128)}), s32[64,1,16]{2,1,0:T(1,128)S(1)}, u32[]{:S(2)}, u32[]{:S(2)}) async-start(s32[64,1,16]{2,1,0:T(1,128)} %bitcast.18), calls=%async_computation.5 | async-start | bytes 65536 | tf_op jit(solution)/shard_map/all_to_all | solution.py:29
  101.9 37.5 %all-to-all-start.3 = ((bf16[8,256,256]{2,1,0:T(8,128)(2,1)}), bf16[8,256,256]{2,1,0:T(8,128)(2,1)S(1)}, u32[]{:S(2)}, u32[]{:S(2)}) async-start(bf16[8,256,256]{2,1,0:T(8,128)(2,1)} %bitcast.11), calls=%async_computation.3 | async-start | bytes 2097152 | tf_op jit(solution)/shard_map/all_to_all | solution.py:29
  108.3 4.7 %collective-permute-start.10 = (f32[64,256]{1,0:T(8,128)S(1)}, f32[64,256]{1,0:T(8,128)S(1)}, u32[]{:S(2)}, u32[]{:S(2)}) collective-permute-start(f32[64,256]{1,0:T(8,128)S(1)} %get-tuple-element.16), channel_id=1, source_target_pairs={{0,2},{1,3},{2,0},{3,1},{4,6},{5,7},{6,4},{7,5},{8,10},{9,11},{10,... | collective-permute-start | bytes 196616 | tf_op jit(solution)/shard_map/ppermute | solution.py:38
  111.3 3.9 %collective-permute-start.11 = (f32[64,256]{1,0:T(8,128)S(1)}, f32[64,256]{1,0:T(8,128)S(1)}, u32[]{:S(2)}, u32[]{:S(2)}) collective-permute-start(f32[64,256]{1,0:T(8,128)S(1)} %get-tuple-element.15), channel_id=1, source_target_pairs={{0,3},{1,0},{2,1},{3,2},{4,7},{5,4},{6,5},{7,6},{8,11},{9,8},{10,9... | collective-permute-start | bytes 196616 | tf_op jit(solution)/shard_map/ppermute | solution.py:38
  112.1 4.6 %collective-permute-start.9 = (f32[64,256]{1,0:T(8,128)S(1)}, f32[64,256]{1,0:T(8,128)S(1)}, u32[]{:S(2)}, u32[]{:S(2)}) collective-permute-start(f32[64,256]{1,0:T(8,128)S(1)} %get-tuple-element.14), channel_id=1, source_target_pairs={{0,1},{1,2},{2,3},{3,0},{4,5},{5,6},{6,7},{7,4},{8,9},{9,10},{10,1... | collective-permute-start | bytes 196616 | tf_op jit(solution)/shard_map/ppermute | solution.py:38
  116.8 4.2 %collective-permute-start.12 = (f32[16,256]{1,0:T(8,128)S(1)}, f32[16,256]{1,0:T(8,128)S(1)}, u32[]{:S(2)}, u32[]{:S(2)}) collective-permute-start(f32[16,256]{1,0:T(8,128)S(1)} %get-tuple-element.17), channel_id=1, source_target_pairs={{0,8},{8,16},{16,24},{24,0},{1,9},{9,17},{17,25},{25,1},{2,10},{10... | collective-permute-start | bytes 49160 | tf_op jit(solution)/shard_map/ppermute | solution.py:38
  117.1 4.4 %collective-permute-start.13 = (f32[16,256]{1,0:T(8,128)S(1)}, f32[16,256]{1,0:T(8,128)S(1)}, u32[]{:S(2)}, u32[]{:S(2)}) collective-permute-start(f32[16,256]{1,0:T(8,128)S(1)} %get-tuple-element.19), channel_id=1, source_target_pairs={{0,16},{8,24},{16,0},{24,8},{1,17},{9,25},{17,1},{25,9},{2,18},{10... | collective-permute-start | bytes 49160 | tf_op jit(solution)/shard_map/ppermute | solution.py:38
  121.7 7.1 %collective-permute-start.15 = (f32[16,256]{1,0:T(8,128)S(1)}, f32[16,256]{1,0:T(8,128)S(1)}, u32[]{:S(2)}, u32[]{:S(2)}) collective-permute-start(f32[16,256]{1,0:T(8,128)S(1)} %add_add_fusion.1), channel_id=1, source_target_pairs={{0,32},{32,0},{64,96},{96,64},{128,160},{160,128},{192,224},{224,1... | collective-permute-start | bytes 49160 | tf_op jit(solution)/shard_map/ppermute | solution.py:307
  128.8 4.0 %collective-permute-start.16 = (f32[16,256]{1,0:T(8,128)S(1)}, f32[16,256]{1,0:T(8,128)S(1)}, u32[]{:S(2)}, u32[]{:S(2)}) collective-permute-start(f32[16,256]{1,0:T(8,128)S(1)} %add.140), channel_id=1, source_target_pairs={{0,64},{32,96},{64,0},{96,32},{128,192},{160,224},{192,128},{224,1... | collective-permute-start | bytes 49160 | tf_op jit(solution)/shard_map/ppermute | solution.py:307
  132.8 6.6 %collective-permute-start.17 = (f32[16,256]{1,0:T(8,128)S(1)}, f32[16,256]{1,0:T(8,128)S(1)}, u32[]{:S(2)}, u32[]{:S(2)}) collective-permute-start(f32[16,256]{1,0:T(8,128)S(1)} %add.141), channel_id=1, source_target_pairs={{0,128},{32,160},{64,192},{96,224},{128,0},{160,32},{192,64},{224,... | collective-permute-start | bytes 49160 | tf_op jit(solution)/shard_map/ppermute | solution.py:307
  140.3 21.1 %all-to-all-start.2 = ((f32[32,16,256]{2,1,0:T(8,128)}), f32[32,16,256]{2,1,0:T(8,128)S(1)}, u32[]{:S(2)}, u32[]{:S(2)}) async-start(f32[32,16,256]{2,1,0:T(8,128)} %broadcast_in_dim.20), calls=%async_computation.2 | async-start | bytes 1048576 | tf_op jit(solution)/shard_map/all_to_all | solution.py:29
  161.5 39.8 %all-to-all-start.4 = ((f32[256,8,128]{2,1,0:T(8,128)}), f32[256,8,128]{2,1,0:T(8,128)S(1)}, u32[]{:S(2)}, u32[]{:S(2)}) async-start(f32[256,8,128]{2,1,0:T(8,128)} %bitcast.48), calls=%async_computation.4 | async-start | bytes 2097152 | tf_op jit(solution)/shard_map/all_to_all | solution.py:29
  170.1 3.9 %collective-permute-start.18 = (s32[64,16]{1,0:T(8,128)S(1)}, s32[64,16]{1,0:T(8,128)S(1)}, u32[]{:S(2)}, u32[]{:S(2)}) collective-permute-start(s32[64,16]{1,0:T(8,128)S(1)} %bitcast.56), channel_id=1, source_target_pairs={{0,3},{1,0},{2,1},{3,2},{4,7},{5,4},{6,5},{7,6},{8,11},{9,8},{10,9... | collective-permute-start | bytes 12296 | tf_op jit(solution)/shard_map/ppermute | solution.py:38
  172.8 4.9 %collective-permute-start.19 = (s32[64,16]{1,0:T(8,128)S(1)}, s32[64,16]{1,0:T(8,128)S(1)}, u32[]{:S(2)}, u32[]{:S(2)}) collective-permute-start(s32[64,16]{1,0:T(8,128)S(1)} %bitcast.57), channel_id=1, source_target_pairs={{0,2},{1,3},{2,0},{3,1},{4,6},{5,7},{6,4},{7,5},{8,10},{9,11},{10,... | collective-permute-start | bytes 12296 | tf_op jit(solution)/shard_map/ppermute | solution.py:38
  173.3 5.2 %collective-permute-start.20 = (s32[64,16]{1,0:T(8,128)S(1)}, s32[64,16]{1,0:T(8,128)S(1)}, u32[]{:S(2)}, u32[]{:S(2)}) collective-permute-start(s32[64,16]{1,0:T(8,128)S(1)} %bitcast.58), channel_id=1, source_target_pairs={{0,1},{1,2},{2,3},{3,0},{4,5},{5,6},{6,7},{7,4},{8,9},{9,10},{10,1... | collective-permute-start | bytes 12296 | tf_op jit(solution)/shard_map/ppermute | solution.py:38
  (15 other events, 157.8 us)

commit v4 on v3

--- a/solution.py
+++ b/solution.py
@@ -12,13 +12,11 @@
 ROWS = 8 * BLK
 XK = ("x", "k")
 KYX = ("k", "y", "x")
-ZXK = ("z", "x", "k")
 YZXK = ("y", "z", "x", "k")
 F32 = jnp.float32
 BF16 = jnp.bfloat16
 VMEM = pl.BlockSpec(memory_space=pltpu.VMEM)
 SMEM = pl.BlockSpec(memory_space=pltpu.SMEM)
-PARAMS = pltpu.CompilerParams(vmem_limit_bytes=56 * 2**20)
 
 
 def dot(left, right, dims):
@@ -65,27 +63,13 @@
     return rows_at(jnp.concatenate(rising + rising, axis=0), start, count * rows)
 
 
-def stats_kernel(at_ref, items_ref, users_ref, own_ref, out_ref, even_ref, odd_ref):
-    def score(c, buffer):
-        users = users_ref[pl.ds(pl.multiple_of(at_ref[c], BLK), BLK), :]
-        buffer[...] = dot(items_ref[...], users, (1, 1))
-
-    def reduce(c, buffer):
-        top = jnp.max(buffer[...], axis=0, keepdims=True)
-        out_ref[0, pl.ds(c, 1), :] = top
-        out_ref[0, pl.ds(8 + c, 1), :] = jnp.sum(jnp.exp(buffer[...] - top), axis=0, keepdims=True)
-
-    score(0, even_ref)
-
-    def step(i, carry):
-        score(2 * i + 1, odd_ref)
-        reduce(2 * i, even_ref)
-        score(jnp.minimum(2 * i + 2, 7), even_ref)
-        reduce(2 * i + 1, odd_ref)
-        return carry
-
-    lax.fori_loop(0, 4, step, 0)
-    out_ref[0, 16:24, :] = own_ref[...]
+def stats_kernel(at_ref, items_ref, users_ref, own_ref, out_ref):
+    for b in range(8):
+        scores = dot(items_ref[...], users_ref[b * BLK : (b + 1) * BLK, :], (1, 1))
+        top = jnp.max(scores, axis=0, keepdims=True)
+        out_ref[0, pl.ds(at_ref[b], 1), :] = top
+        out_ref[0, pl.ds(8 + at_ref[b], 1), :] = jnp.sum(jnp.exp(scores - top), axis=0, keepdims=True)
+    out_ref[0, 16:40, :] = own_ref[...]
     for p in range(1, 8):
         out_ref[p] = out_ref[0]
 
@@ -94,70 +78,53 @@
     return pl.pallas_call(
         stats_kernel,
         in_specs=[SMEM, VMEM, VMEM, VMEM],
-        out_shape=jax.ShapeDtypeStruct((8, 24, BLK), F32),
-        scratch_shapes=[pltpu.VMEM((ROWS, BLK), F32)] * 2,
-        compiler_params=PARAMS,
+        out_shape=jax.ShapeDtypeStruct((8, 40, BLK), F32),
+        compiler_params=pltpu.CompilerParams(vmem_limit_bytes=20 * 2**20),
         name="stats",
     )(at, items, users, own)
 
 
 def grads_kernel(
     at_ref, items_ref, users_ref, got_ref, gi_ref, keep_ref, give_ref,
-    acc_ref, turned_ref, index_ref, even_ref, odd_ref, deven_ref, dodd_ref,
+    all_ref, turned_ref, index_ref, ids_ref,
 ):
     turned_ref[...] = items_ref[...].T
     spot = lax.broadcasted_iota(jnp.int32, (ROWS, BLK), 0)
-    index_ref[...] = (spot // BLK) * ROWS + spot % BLK + at_ref[16]
-    acc_ref[...] = jnp.zeros_like(acc_ref)
-
-    def chunk(c):
-        return users_ref[pl.ds(pl.multiple_of(at_ref[c], BLK), BLK), :]
-
-    def score(c, buffer):
-        buffer[...] = dot(items_ref[...], chunk(c), (1, 1))
-
-    def weigh(c, buffer, dbuffer):
+    index_ref[...] = (spot // BLK) * ROWS + spot % BLK + at_ref[8]
+    for b in range(8):
+        c = at_ref[b]
         tops = got_ref[:, pl.ds(c, 1), :].reshape(8, BLK)
         parts = got_ref[:, pl.ds(8 + c, 1), :].reshape(8, BLK)
+        own = got_ref[pl.ds(c, 1), 16:18, :].reshape(2, BLK)
+        weight = own[0:1]
+        target = own[1:2].astype(jnp.int32)
         top = jnp.max(tops, axis=0, keepdims=True)
         total = top + jnp.log(jnp.sum(parts * jnp.exp(tops - top), axis=0, keepdims=True))
-        weight = got_ref[c, 16:17, :]
-        target = got_ref[c, 17:18, :].astype(jnp.int32)
-        chosen = (index_ref[...] == target).astype(F32)
-        dbuffer[...] = (weight * (jnp.exp(buffer[...] - total) - chosen)).astype(BF16)
-
-    def multiply(c, dbuffer):
-        part = dot(turned_ref[...], dbuffer[...], (1, 0))
-        slot = at_ref[8 + c]
-
-        @pl.when(slot < 4)
-        def _():
-            keep_ref[slot] = part
-
-        @pl.when(slot >= 4)
-        def _():
-            give_ref[slot - 4] = part
-
-        acc_ref[...] += dot(dbuffer[...], chunk(c), (1, 0))
-
-    score(0, even_ref)
-    weigh(0, even_ref, deven_ref)
-    score(1, odd_ref)
-
-    def step(i, carry):
-        weigh(2 * i + 1, odd_ref, dodd_ref)
-        score(2 * i + 2, even_ref)
-        multiply(2 * i, deven_ref)
-        weigh(2 * i + 2, even_ref, deven_ref)
-        score(2 * i + 3, odd_ref)
-        multiply(2 * i + 1, dodd_ref)
-        return carry
-
-    lax.fori_loop(0, 3, step, 0)
-    weigh(7, odd_ref, dodd_ref)
-    multiply(6, deven_ref)
-    multiply(7, dodd_ref)
-    gi_ref[...] = acc_ref[...].astype(BF16)
+        total = total - jnp.log(weight)
+        scores = dot(items_ref[...], users_ref[b * BLK : (b + 1) * BLK, :], (1, 1))
+        share = jnp.exp(scores - total)
+        dscore = jnp.where(index_ref[...] == target, share - weight, share).astype(BF16)
+        all_ref[:, b * BLK : (b + 1) * BLK] = dscore
+        part = dot(turned_ref[...], dscore, (1, 0))
+        if b % 2 == 0:
+            keep_ref[b // 2] = part
+        else:
+            give_ref[b // 2] = part
+    gi = dot(all_ref[...], users_ref[...], (1, 0)).astype(BF16)
+    for z in range(8):
+        gi_ref[z, :BLK, :] = gi[z * BLK : (z + 1) * BLK]
+    lane = lax.broadcasted_iota(jnp.int32, (8, 128), 1) // CAP
+    ids_ref[...] = jnp.zeros_like(ids_ref)
+    for y in range(4):
+        row = jnp.zeros((8, 128), F32)
+        for p in range(8):
+            piece = got_ref[p, 24 + 8 * (y // 2) : 32 + 8 * (y // 2), 128 * (y % 2) : 128 * (y % 2) + 128]
+            turn = ((p - at_ref[9]) & 7) * CAP
+            row = jnp.where(lane == p, pltpu.roll(piece, turn, 1), row)
+        high = jnp.floor(row * (1.0 / 64.0))
+        ids_ref[:, y, :128] = high
+        ids_ref[:, y, 128:] = row - 64.0 * high
+    gi_ref[:, BLK:, :] = ids_ref[...].astype(BF16)
 
 
 def grads(at, items, users, got):
@@ -165,17 +132,14 @@
     return pl.pallas_call(
         grads_kernel,
         in_specs=[SMEM, VMEM, VMEM, VMEM],
-        out_shape=[jax.ShapeDtypeStruct((ROWS, 256), BF16), share, share],
+        out_shape=[jax.ShapeDtypeStruct((8, BLK + 8, 256), BF16), share, share],
         scratch_shapes=[
-            pltpu.VMEM((ROWS, 256), F32),
+            pltpu.VMEM((ROWS, ROWS), BF16),
             pltpu.VMEM((256, ROWS), BF16),
             pltpu.VMEM((ROWS, BLK), jnp.int32),
-            pltpu.VMEM((ROWS, BLK), F32),
-            pltpu.VMEM((ROWS, BLK), F32),
-            pltpu.VMEM((ROWS, BLK), BF16),
-            pltpu.VMEM((ROWS, BLK), BF16),
+            pltpu.VMEM((8, 8, 256), F32),
         ],
-        compiler_params=PARAMS,
+        compiler_params=pltpu.CompilerParams(vmem_limit_bytes=40 * 2**20),
         name="grads",
     )(at, items, users, got)
 
@@ -188,7 +152,7 @@
 
 
 def pack_kernel(parts_ref, owner_ref, rank_ref, out_ref):
-    value = jnp.sum(parts_ref[...].astype(F32), axis=0)
+    value = sum(parts_ref[z, :BLK, :].astype(F32) for z in range(8))
     pieces = thirds(value)
     lane = lax.broadcasted_iota(jnp.int32, (64 * 8, BLK), 0)
     halves = []
@@ -208,7 +172,7 @@
         pack_kernel,
         in_specs=[VMEM] * 3,
         out_shape=jax.ShapeDtypeStruct((4, 64, 8, 128), F32),
-        compiler_params=PARAMS,
+        compiler_params=pltpu.CompilerParams(vmem_limit_bytes=16 * 2**20),
         name="pack",
     )(parts, owner, rank)
 
@@ -243,7 +207,7 @@
         in_specs=[VMEM] * 2,
         out_shape=jax.ShapeDtypeStruct((64, TABLE), F32),
         scratch_shapes=[pltpu.VMEM((TABLE, 256), BF16), pltpu.VMEM((768, TABLE), BF16)],
-        compiler_params=PARAMS,
+        compiler_params=pltpu.CompilerParams(vmem_limit_bytes=36 * 2**20),
         name="table",
     )(got, ids)
 
@@ -263,12 +227,10 @@
     pair = jnp.concatenate([features, shifted(features, "k", 1)], axis=0)
     block = jnp.concatenate([pair] + [shifted(pair, "x", d) for d in range(1, 4)], axis=0)
     _, _, users = tower(block, w_first, w_second)
-    chunk = jnp.arange(8, dtype=jnp.int32)
-    other = (chunk % 2) ^ lax.axis_index("k")
-    back = (lax.axis_index("x") - chunk // 2) & 3
-    ahead = (chunk // 2 - lax.axis_index("x")) & 3
-    base = (lax.axis_index(XK) * BLK).reshape(1)
-    at = jnp.concatenate([(2 * back + other) * BLK, ahead + 4 * other, base]).astype(jnp.int32)
+    block_no = jnp.arange(8, dtype=jnp.int32)
+    source = 2 * ((lax.axis_index("x") - block_no // 2) & 3) + ((block_no % 2) ^ lax.axis_index("k"))
+    own_place = lax.axis_index(XK).reshape(1)
+    at = jnp.concatenate([source, own_place * BLK, own_place]).astype(jnp.int32)
 
     member = (owner == lax.broadcasted_iota(jnp.int32, (64, 1), 0)).astype(F32)
     order = lax.broadcasted_iota(jnp.int32, (BLK, BLK), 0) < lax.broadcasted_iota(jnp.int32, (BLK, BLK), 1)
@@ -276,22 +238,24 @@
     rank = jnp.sum(before * member, axis=0, keepdims=True).astype(jnp.int32)
     slot = owner * CAP + rank
     held = (slot == lax.broadcasted_iota(jnp.int32, (64 * CAP, 1), 0)).astype(jnp.int32)
-    rows = jnp.sum(held * (item_row + 1), axis=1) - 1
-    ids = exchange(rows.reshape(64, CAP), ZXK)
-    ids = joined(ids, "y")
-    ids = jnp.concatenate([ids[:, :8].reshape(1, -1), ids[:, 8:].reshape(1, -1)], axis=1)
-
+    rows = jnp.sum(held * (item_row + 1), axis=1).astype(F32).reshape(64, CAP)
+    rows = joined(rows, "y")
+    rows = rows.reshape(2, 2, 8, 128).swapaxes(1, 2).reshape(16, BLK)
     own = jnp.concatenate(
-        [example_weight, positive.astype(F32), jnp.zeros((6, BLK), F32)], axis=0
+        [example_weight, positive.astype(F32), jnp.zeros((6, BLK), F32), rows], axis=0
     )
-    got = exchange(stats(at[:8], items, users, own), XK)
+    got = exchange(stats(at, items, users, own), XK)
     gi, keep, give = grads(at, items, users, got)
-    gi = exchange(gi.reshape(8, BLK, 256), "z")
+    gi = exchange(gi, "z")
     gu = keep + shifted(give, "k", 1)
     grad_user = gu[0]
     for d in range(1, 4):
-        grad_user = grad_user + shifted(gu[d], "x", d)
+        grad_user = grad_user + shifted(gu[d], "x", -d)
     grad_user = grad_user.T.astype(BF16)
+    ids = gi[:, BLK : BLK + 4, :].astype(F32)
+    ids = (64.0 * ids[:, :, :128] + ids[:, :, 128:]).astype(jnp.int32) - 1
+    ids = ids.swapaxes(0, 1).reshape(4 * 64, CAP)
+    ids = jnp.concatenate([ids[:, :8].reshape(1, -1), ids[:, 8:].reshape(1, -1)], axis=1)
 
     pre_act, hidden, _ = tower(features, w_first, w_second)
     d_second = dot(hidden, grad_user, (0, 0))
@@ -326,6 +290,4 @@
         P("y", rows, None),
         P("y", rows),
     )
-    return jax.shard_map(
-        step_body, mesh=torus, in_specs=placed, out_specs=(P(), P(), P(rows, "y")), check_vma=False
-    )
+    return jax.shard_map(step_body, mesh=torus, in_specs=placed, out_specs=(P(), P(), P(rows, "y")), check_vma=False)

time: 213 us -> 188 us (0.88)
  Pallas kernels: 38.7 us -> 25.1 us
  blocking collectives: 0 us -> 12 us
  starting transfers between devices: 72.3 us -> 60.5 us
  waiting for transfers between devices: 84.5 us -> 75.1 us
  other arithmetic: 4.85 us -> 1.89 us
    all_to_all x0 -> x1, blocking collectives: none -> 12 us  [exchange(): return lax.all_to_all(value, axes, 0, 0, tiled=True)]
    all_to_all x6 -> x4, starting transfers between devices: 41.7 us -> 31.7 us  [exchange(): return lax.all_to_all(value, axes, 0, 0, tiled=True)]
    pallas_call x1, Pallas kernels: 16.8 us -> 8.93 us  [grads(): pl.pallas_call(grads_kernel, in_specs=[SMEM, VMEM, VMEM, VMEM], out_shape...]
    ppermute x18, waiting for transfers between devices: 29.2 us -> 22.8 us  [shifted(): lax.ppermute(value, axis, [(i, (i + step) % count) for i in range(count)])]
    ppermute x3, starting transfers between devices: 8.77 us -> 3.74 us  [step_body(): both = both + lax.ppermute(both, 'z', [(i, i ^ step) for i in range(8)])]
    all_to_all x6 -> x4, waiting for transfers between devices: 46.4 us -> 43.1 us  [exchange(): return lax.all_to_all(value, axes, 0, 0, tiled=True)]
    pallas_call x1, Pallas kernels: 8.48 us -> 5.22 us  [stats(): pl.pallas_call(stats_kernel, in_specs=[SMEM, VMEM, VMEM, VMEM], out_shape...]
    ppermute x18, starting transfers between devices: 21.9 us -> 25 us  [shifted(): lax.ppermute(value, axis, [(i, (i + step) % count) for i in range(count)])]
  transfers between devices with their start and end apart: 27 -> 25, of which waited for: 23 -> 18; matrix products, arithmetic and copies ran while one was open for 4% -> 6% of each run, Pallas kernels for 1% -> 1%
where the time goes in v4:
time: 188 us
  waiting for transfers between devices  75.1 us (40%)
  starting transfers between devices  60.5 us (32%)
  Pallas kernels  25.1 us (13%)
  blocking collectives  12 us (6%)
  local copies, waits for them, and re-layouts  9.26 us (5%)
  matrix products  3.11 us (2%)
  other arithmetic  1.89 us (1%)
    all_to_all x4, waiting for transfers between devices, exchange(): return lax.all_to_all(value, axes, 0, 0, tiled=True)  43.1 us
    all_to_all x4, starting transfers between devices, exchange(): return lax.all_to_all(value, axes, 0, 0, tiled=True)  31.7 us
    ppermute x18, starting transfers between devices, shifted(): lax.ppermute(value, axis, [(i, (i + step) % count) for i in range(count)])  25 us
    ppermute x18, waiting for transfers between devices, shifted(): lax.ppermute(value, axis, [(i, (i + step) % count) for i in range(count)])  22.8 us
    all_to_all x1, blocking collectives, exchange(): return lax.all_to_all(value, axes, 0, 0, tiled=True)  12 us
    ppermute x3, waiting for transfers between devices, step_body(): both = both + lax.ppermute(both, 'z', [(i, i ^ step) for i in range(8)])  9.27 us
    pallas_call x1, Pallas kernels, table(): pl.pallas_call(table_kernel, in_specs=[VMEM] * 2, out_shape=jax.ShapeDtyp...  9.03 us
    pallas_call x1, Pallas kernels, grads(): pl.pallas_call(grads_kernel, in_specs=[SMEM, VMEM, VMEM, VMEM], out_shape...  8.93 us
  transfers between devices with their start and end apart: 25, of which 18 were waited for; matrix products, arithmetic and copies ran while one was open for 6% of the time, Pallas kernels for 1%

profile of v4, /device:TPU:1, one launch (start us, length us, event | category | flops | bytes accessed | tf_op | source)
XLA Modules:
  0.0 187.9 jit_solution(1771769292482681219)
XLA Ops:
  2.6 9.1 %all-to-all-start = ((bf16[8,256,256]{2,1,0:T(8,128)(2,1)}), bf16[8,256,256]{2,1,0:T(8,128)(2,1)S(1)}, u32[]{:S(2)}, u32[]{:S(2)}) async-start(bf16[8,256,256]{2,1,0:T(8,128)(2,1)} %broadcast_in_dim.18), calls=%async_computation | async-start | bytes 2097152 | tf_op jit(solution)/shard_map/all_to_all | solution.py:27
  12.3 2.8 %collective-permute-start.4 = (f32[64,16]{1,0:T(8,128)S(1)}, f32[64,16]{1,0:T(8,128)S(1)}, u32[]{:S(2)}, u32[]{:S(2)}) collective-permute-start(f32[64,16]{1,0:T(8,128)S(1)} %convert_element_type.69), channel_id=1, source_target_pairs={{0,3},{1,0},{2,1},{3,2},{4,7},{5,4},{6,5},{7,6},{8,11},{9,8},{10,9... | collective-permute-start | bytes 12296 | tf_op jit(solution)/shard_map/ppermute | solution.py:36
  21.5 2.5 %collective-permute-start.2 = (bf16[512,256]{1,0:T(8,128)(2,1)S(1)}, bf16[512,256]{1,0:T(8,128)(2,1)S(1)}, u32[]{:S(2)}, u32[]{:S(2)}) collective-permute-start(bf16[512,256]{1,0:T(8,128)(2,1)S(1)} %pad_maximum_fusion), channel_id=1, source_target_pairs={{0,16},{8,24},{16,0},{24,8},{1,17},{9,25},{17,1},{25,9},{2,18},{10... | collective-permute-start | bytes 786440 | tf_op jit(solution)/shard_map/ppermute | solution.py:36
  27.7 5.7 %collective-permute-done.2 = bf16[512,256]{1,0:T(8,128)(2,1)S(1)} collective-permute-done((bf16[512,256]{1,0:T(8,128)(2,1)S(1)}, bf16[512,256]{1,0:T(8,128)(2,1)S(1)}, u32[]{:S(2)}, u32[]{:S(2)}) %collective-permute-start.2) | collective-permute-done | bytes 262176 | tf_op jit(solution)/shard_map/ppermute | solution.py:36
  36.9 4.1 %all-to-all-done = bf16[8,256,256]{2,1,0:T(8,128)(2,1)S(1)} async-done(((bf16[8,256,256]{2,1,0:T(8,128)(2,1)}), bf16[8,256,256]{2,1,0:T(8,128)(2,1)S(1)}, u32[]{:S(2)}, u32[]{:S(2)}) %all-to-all-start) | async-done | bytes 1048608 | tf_op jit(solution)/shard_map/all_to_all | solution.py:27
  41.0 5.2 %stats.1 = f32[8,40,256]{2,1,0:T(8,128)S(1)} custom-call(s32[10]{0:T(128)S(1)} %pad_add_fusion.1.at_ref, bf16[2048,256]{1,0:T(8,128)(2,1)S(1)} %bitcast.48, bf16[2048,256]{1,0:T(8,128)(2,1)S(1)} %convolution_convert_fusion.users_ref, f32[24,256]{1,0:T(8,128)S(1)} %pad_maximum_fusion.1.own_ref), custom_call_target="tpu_custom_call" | custom-call | tf_op jit(solution)/shard_map/stats/pallas_call | solution.py:78
  46.2 12.0 %all_to_all.25.got_ref = f32[8,40,256]{2,1,0:T(8,128)S(1)} all-to-all(f32[8,40,256]{2,1,0:T(8,128)S(1)} %stats.1), channel_id=1, replica_groups=mesh['z'=8,'x'=4,'k'=2,'y'=4] {'x','k'}, dimensions={0} | all-to-all | bytes 655360 | tf_op jit(solution)/shard_map/all_to_all | solution.py:27
  58.2 8.9 %grads.1 = (bf16[8,264,256]{2,1,0:T(8,128)(2,1)}, f32[4,256,256]{2,1,0:T(8,128)S(1)}, f32[4,256,256]{2,1,0:T(8,128)S(1)}) custom-call(s32[10]{0:T(128)S(1)} %pad_add_fusion.1.at_ref, bf16[2048,256]{1,0:T(8,128)(2,1)S(1)} %bitcast.49, bf16[2048,256]{1,0:T(8,128)(2,1)S(1)} %convolution_convert_fusion.users_ref, f32[8,40,256]{2,1,0:T(8,128)S(1)} %all_to_all.25.got_ref), custom_call_target="tpu_custom_call" | custom-call | tf_op jit(solution)/shard_map/grads/pallas_call | solution.py:132
  67.9 2.3 %collective-permute-done.7 = f32[4,256,256]{2,1,0:T(8,128)S(1)} collective-permute-done((f32[4,256,256]{2,1,0:T(8,128)S(1)}, f32[4,256,256]{2,1,0:T(8,128)S(1)}, u32[]{:S(2)}, u32[]{:S(2)}) %collective-permute-start.7) | collective-permute-done | bytes 1048608 | tf_op jit(solution)/shard_map/ppermute | solution.py:36
  71.5 2.4 %collective-permute-start.8 = (f32[256,256]{1,0:T(8,128)}, f32[256,256]{1,0:T(8,128)}, u32[]{:S(2)}, u32[]{:S(2)}) collective-permute-start(f32[256,256]{1,0:T(8,128)} %get-tuple-element.9), channel_id=1, source_target_pairs={{0,24},{8,0},{16,8},{24,16},{1,25},{9,1},{17,9},{25,17},{2,26},{10... | collective-permute-start | bytes 786440 | tf_op jit(solution)/shard_map/ppermute | solution.py:36
  74.1 4.7 %all-to-all-start.3 = ((bf16[8,264,256]{2,1,0:T(8,128)(2,1)}), bf16[8,264,256]{2,1,0:T(8,128)(2,1)S(1)}, u32[]{:S(2)}, u32[]{:S(2)}) async-start(bf16[8,264,256]{2,1,0:T(8,128)(2,1)} %get-tuple-element.8), calls=%async_computation.3 | async-start | bytes 2162688 | tf_op jit(solution)/shard_map/all_to_all | solution.py:27
  80.7 4.6 %collective-permute-done.9 = f32[256,256]{1,0:T(8,128)} collective-permute-done((f32[256,256]{1,0:T(8,128)S(1)}, f32[256,256]{1,0:T(8,128)}, u32[]{:S(2)}, u32[]{:S(2)}) %collective-permute-start.9) | collective-permute-done | bytes 262176 | tf_op jit(solution)/shard_map/ppermute | solution.py:36
  91.9 2.6 %collective-permute-start.13 = (f32[64,256]{1,0:T(8,128)S(1)}, f32[64,256]{1,0:T(8,128)S(1)}, u32[]{:S(2)}, u32[]{:S(2)}) collective-permute-start(f32[64,256]{1,0:T(8,128)S(1)} %get-tuple-element.16), channel_id=1, source_target_pairs={{0,2},{1,3},{2,0},{3,1},{4,6},{5,7},{6,4},{7,5},{8,10},{9,11},{10,... | collective-permute-start | bytes 196616 | tf_op jit(solution)/shard_map/ppermute | solution.py:36
  95.5 2.1 %collective-permute-done.13 = f32[64,256]{1,0:T(8,128)S(1)} collective-permute-done((f32[64,256]{1,0:T(8,128)S(1)}, f32[64,256]{1,0:T(8,128)S(1)}, u32[]{:S(2)}, u32[]{:S(2)}) %collective-permute-start.13) | collective-permute-done | bytes 65568 | tf_op jit(solution)/shard_map/ppermute | solution.py:36
  98.7 3.3 %collective-permute-start.16 = (f32[16,256]{1,0:T(8,128)S(1)}, f32[16,256]{1,0:T(8,128)S(1)}, u32[]{:S(2)}, u32[]{:S(2)}) collective-permute-start(f32[16,256]{1,0:T(8,128)S(1)} %get-tuple-element.21), channel_id=1, source_target_pairs={{0,16},{8,24},{16,0},{24,8},{1,17},{9,25},{17,1},{25,9},{2,18},{10... | collective-permute-start | bytes 49160 | tf_op jit(solution)/shard_map/ppermute | solution.py:36
  105.2 2.6 %collective-permute-done.18 = f32[16,256]{1,0:T(8,128)S(1)} collective-permute-done((f32[16,256]{1,0:T(8,128)S(1)}, f32[16,256]{1,0:T(8,128)S(1)}, u32[]{:S(2)}, u32[]{:S(2)}) %collective-permute-start.18) | collective-permute-done | bytes 16416 | tf_op jit(solution)/shard_map/ppermute | solution.py:271
  109.0 2.4 %collective-permute-done.19 = f32[16,256]{1,0:T(8,128)S(1)} collective-permute-done((f32[16,256]{1,0:T(8,128)S(1)}, f32[16,256]{1,0:T(8,128)S(1)}, u32[]{:S(2)}, u32[]{:S(2)}) %collective-permute-start.19) | collective-permute-done | bytes 16416 | tf_op jit(solution)/shard_map/ppermute | solution.py:271
  111.4 2.2 %collective-permute-start.20 = (f32[16,256]{1,0:T(8,128)S(1)}, f32[16,256]{1,0:T(8,128)S(1)}, u32[]{:S(2)}, u32[]{:S(2)}) collective-permute-start(f32[16,256]{1,0:T(8,128)S(1)} %add.134), channel_id=1, source_target_pairs={{0,128},{32,160},{64,192},{96,224},{128,0},{160,32},{192,64},{224,... | collective-permute-start | bytes 49160 | tf_op jit(solution)/shard_map/ppermute | solution.py:271
  113.6 4.3 %collective-permute-done.20 = f32[16,256]{1,0:T(8,128)S(1)} collective-permute-done((f32[16,256]{1,0:T(8,128)S(1)}, f32[16,256]{1,0:T(8,128)S(1)}, u32[]{:S(2)}, u32[]{:S(2)}) %collective-permute-start.20) | collective-permute-done | bytes 16416 | tf_op jit(solution)/shard_map/ppermute | solution.py:271
  118.7 11.5 %all-to-all-start.2 = ((f32[32,16,256]{2,1,0:T(8,128)}), f32[32,16,256]{2,1,0:T(8,128)S(1)}, u32[]{:S(2)}, u32[]{:S(2)}) async-start(f32[32,16,256]{2,1,0:T(8,128)} %broadcast_in_dim.20), calls=%async_computation.2 | async-start | bytes 1048576 | tf_op jit(solution)/shard_map/all_to_all | solution.py:27
  132.1 9.3 %all-to-all-done.2 = f32[32,16,256]{2,1,0:T(8,128)S(1)} async-done(((f32[32,16,256]{2,1,0:T(8,128)}), f32[32,16,256]{2,1,0:T(8,128)S(1)}, u32[]{:S(2)}, u32[]{:S(2)}) %all-to-all-start.2) | async-done | bytes 524320 | tf_op jit(solution)/shard_map/all_to_all | solution.py:27
  141.4 6.4 %all-to-all-start.4 = ((f32[256,8,128]{2,1,0:T(8,128)}), f32[256,8,128]{2,1,0:T(8,128)S(1)}, u32[]{:S(2)}, u32[]{:S(2)}) async-start(f32[256,8,128]{2,1,0:T(8,128)} %bitcast.17), calls=%async_computation.4 | async-start | bytes 2097152 | tf_op jit(solution)/shard_map/all_to_all | solution.py:27
  149.1 29.8 %all-to-all-done.4 = f32[256,8,128]{2,1,0:T(8,128)S(1)} async-done(((f32[256,8,128]{2,1,0:T(8,128)}), f32[256,8,128]{2,1,0:T(8,128)S(1)}, u32[]{:S(2)}, u32[]{:S(2)}) %all-to-all-start.4) | async-done | bytes 1048608 | tf_op jit(solution)/shard_map/all_to_all | solution.py:27
  178.9 9.0 %table.1 = f32[64,4096]{1,0:T(8,128)} custom-call(f32[2048,128]{1,0:T(8,128)S(1)} %bitcast.50, s32[1,4096]{1,0:T(1,128)S(1)} %pad_add_fusion.ids_ref), custom_call_target="tpu_custom_call" | custom-call | tf_op jit(solution)/shard_map/table/pallas_call | solution.py:205
  (99 shorter events, 37.3 us)
Async XLA Ops:
  2.6 38.3 %all-to-all-start = ((bf16[8,256,256]{2,1,0:T(8,128)(2,1)}), bf16[8,256,256]{2,1,0:T(8,128)(2,1)S(1)}, u32[]{:S(2)}, u32[]{:S(2)}) async-start(bf16[8,256,256]{2,1,0:T(8,128)(2,1)} %broadcast_in_dim.18), calls=%async_computation | async-start | bytes 2097152 | tf_op jit(solution)/shard_map/all_to_all | solution.py:27
  12.3 6.5 %collective-permute-start.4 = (f32[64,16]{1,0:T(8,128)S(1)}, f32[64,16]{1,0:T(8,128)S(1)}, u32[]{:S(2)}, u32[]{:S(2)}) collective-permute-start(f32[64,16]{1,0:T(8,128)S(1)} %convert_element_type.69), channel_id=1, source_target_pairs={{0,3},{1,0},{2,1},{3,2},{4,7},{5,4},{6,5},{7,6},{8,11},{9,8},{10,9... | collective-permute-start | bytes 12296 | tf_op jit(solution)/shard_map/ppermute | solution.py:36
  15.1 4.3 %collective-permute-start.5 = (f32[64,16]{1,0:T(8,128)S(1)}, f32[64,16]{1,0:T(8,128)S(1)}, u32[]{:S(2)}, u32[]{:S(2)}) collective-permute-start(f32[64,16]{1,0:T(8,128)S(1)} %convert_element_type.69), channel_id=1, source_target_pairs={{0,2},{1,3},{2,0},{3,1},{4,6},{5,7},{6,4},{7,5},{8,10},{9,11},{10,... | collective-permute-start | bytes 12296 | tf_op jit(solution)/shard_map/ppermute | solution.py:36
  15.4 4.3 %collective-permute-start.6 = (f32[64,16]{1,0:T(8,128)S(1)}, f32[64,16]{1,0:T(8,128)S(1)}, u32[]{:S(2)}, u32[]{:S(2)}) collective-permute-start(f32[64,16]{1,0:T(8,128)S(1)} %convert_element_type.69), channel_id=1, source_target_pairs={{0,1},{1,2},{2,3},{3,0},{4,5},{5,6},{6,7},{7,4},{8,9},{9,10},{10,1... | collective-permute-start | bytes 12296 | tf_op jit(solution)/shard_map/ppermute | solution.py:36
  16.1 4.0 %collective-permute-start = (bf16[256,256]{1,0:T(8,128)(2,1)S(1)}, bf16[256,256]{1,0:T(8,128)(2,1)S(1)}, u32[]{:S(2)}, u32[]{:S(2)}) collective-permute-start(bf16[256,256]{1,0:T(8,128)(2,1)S(1)} %bitcast.55), channel_id=1, source_target_pairs={{0,4},{4,0},{1,5},{5,1},{2,6},{6,2},{3,7},{7,3},{8,12},{12,8},{9,1... | collective-permute-start | bytes 393224 | tf_op jit(solution)/shard_map/ppermute | solution.py:36
  20.2 6.8 %collective-permute-start.1 = (bf16[512,256]{1,0:T(8,128)(2,1)S(1)}, bf16[512,256]{1,0:T(8,128)(2,1)S(1)}, u32[]{:S(2)}, u32[]{:S(2)}) collective-permute-start(bf16[512,256]{1,0:T(8,128)(2,1)S(1)} %pad_maximum_fusion), channel_id=1, source_target_pairs={{0,8},{8,16},{16,24},{24,0},{1,9},{9,17},{17,25},{25,1},{2,10},{10... | collective-permute-start | bytes 786440 | tf_op jit(solution)/shard_map/ppermute | solution.py:36
  21.5 11.9 %collective-permute-start.2 = (bf16[512,256]{1,0:T(8,128)(2,1)S(1)}, bf16[512,256]{1,0:T(8,128)(2,1)S(1)}, u32[]{:S(2)}, u32[]{:S(2)}) collective-permute-start(bf16[512,256]{1,0:T(8,128)(2,1)S(1)} %pad_maximum_fusion), channel_id=1, source_target_pairs={{0,16},{8,24},{16,0},{24,8},{1,17},{9,25},{17,1},{25,9},{2,18},{10... | collective-permute-start | bytes 786440 | tf_op jit(solution)/shard_map/ppermute | solution.py:36
  24.0 10.1 %collective-permute-start.3 = (bf16[512,256]{1,0:T(8,128)(2,1)S(1)}, bf16[512,256]{1,0:T(8,128)(2,1)S(1)}, u32[]{:S(2)}, u32[]{:S(2)}) collective-permute-start(bf16[512,256]{1,0:T(8,128)(2,1)S(1)} %pad_maximum_fusion), channel_id=1, source_target_pairs={{0,24},{8,0},{16,8},{24,16},{1,25},{9,1},{17,9},{25,17},{2,26},{10... | collective-permute-start | bytes 786440 | tf_op jit(solution)/shard_map/ppermute | solution.py:36
  67.2 3.0 %collective-permute-start.7 = (f32[4,256,256]{2,1,0:T(8,128)S(1)}, f32[4,256,256]{2,1,0:T(8,128)S(1)}, u32[]{:S(2)}, u32[]{:S(2)}) collective-permute-start(f32[4,256,256]{2,1,0:T(8,128)S(1)} %get-tuple-element.7), channel_id=1, source_target_pairs={{0,4},{4,0},{1,5},{5,1},{2,6},{6,2},{3,7},{7,3},{8,12},{12,8},{9,1... | collective-permute-start | bytes 3145736 | tf_op jit(solution)/shard_map/ppermute | solution.py:36
  71.2 9.5 %collective-permute-start.10 = (f32[256,256]{1,0:T(8,128)}, f32[256,256]{1,0:T(8,128)S(1)}, u32[]{:S(2)}, u32[]{:S(2)}) collective-permute-start(f32[256,256]{1,0:T(8,128)} %get-tuple-element.10), channel_id=1, source_target_pairs={{0,8},{8,16},{16,24},{24,0},{1,9},{9,17},{17,25},{25,1},{2,10},{10... | collective-permute-start | bytes 786440 | tf_op jit(solution)/shard_map/ppermute | solution.py:36
  71.5 9.2 %collective-permute-start.8 = (f32[256,256]{1,0:T(8,128)}, f32[256,256]{1,0:T(8,128)}, u32[]{:S(2)}, u32[]{:S(2)}) collective-permute-start(f32[256,256]{1,0:T(8,128)} %get-tuple-element.9), channel_id=1, source_target_pairs={{0,24},{8,0},{16,8},{24,16},{1,25},{9,1},{17,9},{25,17},{2,26},{10... | collective-permute-start | bytes 786440 | tf_op jit(solution)/shard_map/ppermute | solution.py:36
  73.9 11.4 %collective-permute-start.9 = (f32[256,256]{1,0:T(8,128)S(1)}, f32[256,256]{1,0:T(8,128)}, u32[]{:S(2)}, u32[]{:S(2)}) collective-permute-start(f32[256,256]{1,0:T(8,128)S(1)} %get-tuple-element.11), channel_id=1, source_target_pairs={{0,16},{8,24},{16,0},{24,8},{1,17},{9,25},{17,1},{25,9},{2,18},{10... | collective-permute-start | bytes 786440 | tf_op jit(solution)/shard_map/ppermute | solution.py:36
  74.1 43.8 %all-to-all-start.3 = ((bf16[8,264,256]{2,1,0:T(8,128)(2,1)}), bf16[8,264,256]{2,1,0:T(8,128)(2,1)S(1)}, u32[]{:S(2)}, u32[]{:S(2)}) async-start(bf16[8,264,256]{2,1,0:T(8,128)(2,1)} %get-tuple-element.8), calls=%async_computation.3 | async-start | bytes 2162688 | tf_op jit(solution)/shard_map/all_to_all | solution.py:27
  87.2 2.9 %collective-permute-start.11 = (f32[256,256]{1,0:T(8,128)S(1)}, f32[256,256]{1,0:T(8,128)S(1)}, u32[]{:S(2)}, u32[]{:S(2)}) collective-permute-start(f32[256,256]{1,0:T(8,128)S(1)} %fusion.3), channel_id=1, source_target_pairs={{0,4},{4,0},{1,5},{5,1},{2,6},{6,2},{3,7},{7,3},{8,12},{12,8},{9,1... | collective-permute-start | bytes 786440 | tf_op jit(solution)/shard_map/ppermute | solution.py:36
  90.3 5.3 %collective-permute-start.12 = (f32[64,256]{1,0:T(8,128)S(1)}, f32[64,256]{1,0:T(8,128)S(1)}, u32[]{:S(2)}, u32[]{:S(2)}) collective-permute-start(f32[64,256]{1,0:T(8,128)S(1)} %get-tuple-element.14), channel_id=1, source_target_pairs={{0,1},{1,2},{2,3},{3,0},{4,5},{5,6},{6,7},{7,4},{8,9},{9,10},{10,1... | collective-permute-start | bytes 196616 | tf_op jit(solution)/shard_map/ppermute | solution.py:36
  91.9 5.8 %collective-permute-start.13 = (f32[64,256]{1,0:T(8,128)S(1)}, f32[64,256]{1,0:T(8,128)S(1)}, u32[]{:S(2)}, u32[]{:S(2)}) collective-permute-start(f32[64,256]{1,0:T(8,128)S(1)} %get-tuple-element.16), channel_id=1, source_target_pairs={{0,2},{1,3},{2,0},{3,1},{4,6},{5,7},{6,4},{7,5},{8,10},{9,11},{10,... | collective-permute-start | bytes 196616 | tf_op jit(solution)/shard_map/ppermute | solution.py:36
  94.5 3.4 %collective-permute-start.14 = (f32[64,256]{1,0:T(8,128)S(1)}, f32[64,256]{1,0:T(8,128)S(1)}, u32[]{:S(2)}, u32[]{:S(2)}) collective-permute-start(f32[64,256]{1,0:T(8,128)S(1)} %get-tuple-element.15), channel_id=1, source_target_pairs={{0,3},{1,0},{2,1},{3,2},{4,7},{5,4},{6,5},{7,6},{8,11},{9,8},{10,9... | collective-permute-start | bytes 196616 | tf_op jit(solution)/shard_map/ppermute | solution.py:36
  97.9 4.0 %collective-permute-start.15 = (f32[16,256]{1,0:T(8,128)S(1)}, f32[16,256]{1,0:T(8,128)S(1)}, u32[]{:S(2)}, u32[]{:S(2)}) collective-permute-start(f32[16,256]{1,0:T(8,128)S(1)} %get-tuple-element.19), channel_id=1, source_target_pairs={{0,8},{8,16},{16,24},{24,0},{1,9},{9,17},{17,25},{25,1},{2,10},{10... | collective-permute-start | bytes 49160 | tf_op jit(solution)/shard_map/ppermute | solution.py:36
  98.7 4.9 %collective-permute-start.16 = (f32[16,256]{1,0:T(8,128)S(1)}, f32[16,256]{1,0:T(8,128)S(1)}, u32[]{:S(2)}, u32[]{:S(2)}) collective-permute-start(f32[16,256]{1,0:T(8,128)S(1)} %get-tuple-element.21), channel_id=1, source_target_pairs={{0,16},{8,24},{16,0},{24,8},{1,17},{9,25},{17,1},{25,9},{2,18},{10... | collective-permute-start | bytes 49160 | tf_op jit(solution)/shard_map/ppermute | solution.py:36
  104.9 3.0 %collective-permute-start.18 = (f32[16,256]{1,0:T(8,128)S(1)}, f32[16,256]{1,0:T(8,128)S(1)}, u32[]{:S(2)}, u32[]{:S(2)}) collective-permute-start(f32[16,256]{1,0:T(8,128)S(1)} %add_add_fusion.1), channel_id=1, source_target_pairs={{0,32},{32,0},{64,96},{96,64},{128,160},{160,128},{192,224},{224,1... | collective-permute-start | bytes 49160 | tf_op jit(solution)/shard_map/ppermute | solution.py:271
  107.8 3.5 %collective-permute-start.19 = (f32[16,256]{1,0:T(8,128)S(1)}, f32[16,256]{1,0:T(8,128)S(1)}, u32[]{:S(2)}, u32[]{:S(2)}) collective-permute-start(f32[16,256]{1,0:T(8,128)S(1)} %add.133), channel_id=1, source_target_pairs={{0,64},{32,96},{64,0},{96,32},{128,192},{160,224},{192,128},{224,1... | collective-permute-start | bytes 49160 | tf_op jit(solution)/shard_map/ppermute | solution.py:271
  111.4 6.5 %collective-permute-start.20 = (f32[16,256]{1,0:T(8,128)S(1)}, f32[16,256]{1,0:T(8,128)S(1)}, u32[]{:S(2)}, u32[]{:S(2)}) collective-permute-start(f32[16,256]{1,0:T(8,128)S(1)} %add.134), channel_id=1, source_target_pairs={{0,128},{32,160},{64,192},{96,224},{128,0},{160,32},{192,64},{224,... | collective-permute-start | bytes 49160 | tf_op jit(solution)/shard_map/ppermute | solution.py:271
  118.7 22.6 %all-to-all-start.2 = ((f32[32,16,256]{2,1,0:T(8,128)}), f32[32,16,256]{2,1,0:T(8,128)S(1)}, u32[]{:S(2)}, u32[]{:S(2)}) async-start(f32[32,16,256]{2,1,0:T(8,128)} %broadcast_in_dim.20), calls=%async_computation.2 | async-start | bytes 1048576 | tf_op jit(solution)/shard_map/all_to_all | solution.py:27
  141.4 37.5 %all-to-all-start.4 = ((f32[256,8,128]{2,1,0:T(8,128)}), f32[256,8,128]{2,1,0:T(8,128)S(1)}, u32[]{:S(2)}, u32[]{:S(2)}) async-start(f32[256,8,128]{2,1,0:T(8,128)} %bitcast.17), calls=%async_computation.4 | async-start | bytes 2097152 | tf_op jit(solution)/shard_map/all_to_all | solution.py:27
  (8 other events, 112.1 us)

commit v5 on v4

--- a/solution.py
+++ b/solution.py
@@ -110,7 +110,10 @@
             keep_ref[b // 2] = part
         else:
             give_ref[b // 2] = part
-    gi = dot(all_ref[...], users_ref[...], (1, 0)).astype(BF16)
+    largest = jnp.max(jnp.abs(users_ref[...].astype(F32)), axis=0, keepdims=True)
+    largest = jnp.maximum(jnp.max(largest, axis=1, keepdims=True) * 416.0, 1e-30)
+    power = jnp.ceil(jnp.log(largest) * 1.4426950408889634)
+    gi = dot(all_ref[...], users_ref[...], (1, 0)) * jnp.exp2(15.0 - power)
     for z in range(8):
         gi_ref[z, :BLK, :] = gi[z * BLK : (z + 1) * BLK]
     lane = lax.broadcasted_iota(jnp.int32, (8, 128), 1) // CAP
@@ -124,7 +127,8 @@
         high = jnp.floor(row * (1.0 / 64.0))
         ids_ref[:, y, :128] = high
         ids_ref[:, y, 128:] = row - 64.0 * high
-    gi_ref[:, BLK:, :] = ids_ref[...].astype(BF16)
+    ids_ref[:, 4, :] = jnp.broadcast_to(power, (8, 256))
+    gi_ref[:, BLK:, :] = ids_ref[...]
 
 
 def grads(at, items, users, got):
@@ -132,7 +136,7 @@
     return pl.pallas_call(
         grads_kernel,
         in_specs=[SMEM, VMEM, VMEM, VMEM],
-        out_shape=[jax.ShapeDtypeStruct((8, BLK + 8, 256), BF16), share, share],
+        out_shape=[jax.ShapeDtypeStruct((8, BLK + 8, 256), F32), share, share],
         scratch_shapes=[
             pltpu.VMEM((ROWS, ROWS), BF16),
             pltpu.VMEM((256, ROWS), BF16),
@@ -144,43 +148,33 @@
     )(at, items, users, got)
 
 
-def thirds(value):
-    high = value.astype(BF16)
-    rest = value - high.astype(F32)
-    middle = rest.astype(BF16)
-    return high, middle, (rest - middle.astype(F32)).astype(BF16)
-
-
-def pack_kernel(parts_ref, owner_ref, rank_ref, out_ref):
-    value = sum(parts_ref[z, :BLK, :].astype(F32) for z in range(8))
-    pieces = thirds(value)
+def pack_kernel(item_ref, owner_ref, rank_ref, out_ref):
     lane = lax.broadcasted_iota(jnp.int32, (64 * 8, BLK), 0)
     halves = []
     for h in range(2):
         rank = rank_ref[...] - 8 * h
         slot = jnp.where((rank >= 0) & (rank < 8), owner_ref[...] * 8 + rank, -1)
         pick = (lane == slot).astype(F32).astype(BF16)
-        halves.append(sum(dot(pick, piece, (1, 0)) for piece in pieces))
+        halves.append(dot(pick, item_ref[...], (1, 0)))
     for g in range(4):
         share = slice(64 * g, 64 * g + 64)
         both = jnp.concatenate([halves[0][:, share], halves[1][:, share]], axis=1)
-        out_ref[g] = both.reshape(64, 8, 128)
-
-
-def pack(parts, owner, rank):
+        out_ref[g * 512 : (g + 1) * 512, :] = both.astype(BF16)
+
+
+def pack(item, owner, rank):
     return pl.pallas_call(
         pack_kernel,
         in_specs=[VMEM] * 3,
-        out_shape=jax.ShapeDtypeStruct((4, 64, 8, 128), F32),
+        out_shape=jax.ShapeDtypeStruct((4 * 512, 128), BF16),
         compiler_params=pltpu.CompilerParams(vmem_limit_bytes=16 * 2**20),
         name="pack",
-    )(parts, owner, rank)
+    )(item, owner, rank)
 
 
 def table_kernel(got_ref, ids_ref, out_ref, pick_ref, kept_ref):
     both = got_ref[...].T
     value = jnp.concatenate([both[:64], both[64:]], axis=1)
-    pieces = jnp.concatenate(thirds(value), axis=0)
     ids = ids_ref[...]
     upper = ids >> 8
     lower = ids & 255
@@ -190,12 +184,11 @@
     def step(j, carry):
         for q in range(4):
             keep = jnp.broadcast_to((upper == 4 * j + q).astype(F32), (16, TABLE)).astype(BF16)
-            kept_ref[q * 192 : (q + 1) * 192, :] = pieces * jnp.concatenate([keep] * 12, axis=0)
+            kept_ref[q * 64 : (q + 1) * 64, :] = value * jnp.concatenate([keep] * 4, axis=0)
         part = dot(kept_ref[...], pick_ref[...], (1, 0))
         for q in range(4):
             at = pl.multiple_of((4 * j + q) * 256, 256)
-            own = part[q * 192 : (q + 1) * 192]
-            out_ref[:, pl.ds(at, 256)] = own[:64] + own[64:128] + own[128:]
+            out_ref[:, pl.ds(at, 256)] = part[q * 64 : (q + 1) * 64]
         return carry
 
     lax.fori_loop(0, 4, step, 0)
@@ -206,8 +199,8 @@
         table_kernel,
         in_specs=[VMEM] * 2,
         out_shape=jax.ShapeDtypeStruct((64, TABLE), F32),
-        scratch_shapes=[pltpu.VMEM((TABLE, 256), BF16), pltpu.VMEM((768, TABLE), BF16)],
-        compiler_params=pltpu.CompilerParams(vmem_limit_bytes=36 * 2**20),
+        scratch_shapes=[pltpu.VMEM((TABLE, 256), BF16), pltpu.VMEM((256, TABLE), BF16)],
+        compiler_params=pltpu.CompilerParams(vmem_limit_bytes=28 * 2**20),
         name="table",
     )(got, ids)
 
@@ -246,7 +239,9 @@
     )
     got = exchange(stats(at, items, users, own), XK)
     gi, keep, give = grads(at, items, users, got)
-    gi = exchange(gi, "z")
+    gi = exchange(gi.astype(jnp.float16), "z")
+    scale = jnp.exp2(gi[:, BLK + 4, 0].astype(F32) - 15.0)
+    item = sum(gi[z, :BLK].astype(F32) * scale[z] for z in range(8)).astype(BF16)
     gu = keep + shifted(give, "k", 1)
     grad_user = gu[0]
     for d in range(1, 4):
@@ -270,7 +265,7 @@
     for step in (1, 2, 4):
         both = both + lax.ppermute(both, "z", [(i, i ^ step) for i in range(8)])
 
-    send = pack(gi, owner, rank).reshape(256, 8, 128)
+    send = pack(item, owner, rank).reshape(256, 8, 128)
     came = exchange(send, YZXK).reshape(256 * 8, 128)
     both = to_all(both, KYX).reshape(512, 256)
     grad_table = table(came, ids).T

time: 188 us -> 172 us (0.915)
  waiting for transfers between devices: 75.1 us -> 57.5 us
  other arithmetic: 1.89 us -> 9.83 us
  Pallas kernels: 25.1 us -> 18.9 us
    all_to_all x4, waiting for transfers between devices: 43.1 us -> 27.5 us  [exchange(): return lax.all_to_all(value, axes, 0, 0, tiled=True)]
    convert_element_type x0 -> x2, other arithmetic: none -> 7.92 us  [the longest x1 5.14 us: step_body(): sum((gi[z, :BLK].astype(F32) * scale[z] for z in range(8))).astype(BF16)]
    pallas_call x1, Pallas kernels: 9.03 us -> 4.56 us  [table(): pl.pallas_call(table_kernel, in_specs=[VMEM] * 2, out_shape=jax.ShapeDtyp...]
    ppermute x18, waiting for transfers between devices: 22.8 us -> 20 us  [shifted(): lax.ppermute(value, axis, [(i, (i + step) % count) for i in range(count)])]
  transfers between devices with their start and end apart: 25 -> 25, of which waited for: 18 -> 18; matrix products, arithmetic and copies ran while one was open for 6% -> 11% of each run, Pallas kernels for 1% -> 1%
where the time goes in v5:
time: 172 us
  starting transfers between devices  59.5 us (35%)
  waiting for transfers between devices  57.5 us (33%)
  Pallas kernels  18.9 us (11%)
  blocking collectives  12.1 us (7%)
  local copies, waits for them, and re-layouts  9.87 us (6%)
  other arithmetic  9.83 us (6%)
  matrix products  3.11 us (2%)
    all_to_all x4, starting transfers between devices, exchange(): return lax.all_to_all(value, axes, 0, 0, tiled=True)  31.1 us
    all_to_all x4, waiting for transfers between devices, exchange(): return lax.all_to_all(value, axes, 0, 0, tiled=True)  27.5 us
    ppermute x18, starting transfers between devices, shifted(): lax.ppermute(value, axis, [(i, (i + step) % count) for i in range(count)])  25.1 us
    ppermute x18, waiting for transfers between devices, shifted(): lax.ppermute(value, axis, [(i, (i + step) % count) for i in range(count)])  20 us
    all_to_all x1, blocking collectives, exchange(): return lax.all_to_all(value, axes, 0, 0, tiled=True)  12.1 us
    ppermute x3, waiting for transfers between devices, step_body(): both = both + lax.ppermute(both, 'z', [(i, i ^ step) for i in range(8)])  10.1 us
    pallas_call x1, Pallas kernels, grads(): pl.pallas_call(grads_kernel, in_specs=[SMEM, VMEM, VMEM, VMEM], out_shape...  7.98 us
    pallas_call x1, Pallas kernels, stats(): pl.pallas_call(stats_kernel, in_specs=[SMEM, VMEM, VMEM, VMEM], out_shape...  5.21 us
  transfers between devices with their start and end apart: 25, of which 18 were waited for; matrix products, arithmetic and copies ran while one was open for 11% of the time, Pallas kernels for 1%

profile of v5, /device:TPU:1, one launch (start us, length us, event | category | flops | bytes accessed | tf_op | source)
XLA Modules:
  0.0 171.8 jit_solution(3664375372663987566)
XLA Ops:
  2.7 9.1 %all-to-all-start = ((bf16[8,256,256]{2,1,0:T(8,128)(2,1)}), bf16[8,256,256]{2,1,0:T(8,128)(2,1)S(1)}, u32[]{:S(2)}, u32[]{:S(2)}) async-start(bf16[8,256,256]{2,1,0:T(8,128)(2,1)} %broadcast_in_dim.18), calls=%async_computation | async-start | bytes 2097152 | tf_op jit(solution)/shard_map/all_to_all | solution.py:27
  12.4 2.8 %collective-permute-start.4 = (f32[64,16]{1,0:T(8,128)S(1)}, f32[64,16]{1,0:T(8,128)S(1)}, u32[]{:S(2)}, u32[]{:S(2)}) collective-permute-start(f32[64,16]{1,0:T(8,128)S(1)} %convert_element_type.111), channel_id=1, source_target_pairs={{0,3},{1,0},{2,1},{3,2},{4,7},{5,4},{6,5},{7,6},{8,11},{9,8},{10,9... | collective-permute-start | bytes 12296 | tf_op jit(solution)/shard_map/ppermute | solution.py:36
  21.5 2.5 %collective-permute-start.2 = (bf16[512,256]{1,0:T(8,128)(2,1)S(1)}, bf16[512,256]{1,0:T(8,128)(2,1)S(1)}, u32[]{:S(2)}, u32[]{:S(2)}) collective-permute-start(bf16[512,256]{1,0:T(8,128)(2,1)S(1)} %pad_maximum_fusion), channel_id=1, source_target_pairs={{0,16},{8,24},{16,0},{24,8},{1,17},{9,25},{17,1},{25,9},{2,18},{10... | collective-permute-start | bytes 786440 | tf_op jit(solution)/shard_map/ppermute | solution.py:36
  27.8 5.7 %collective-permute-done.2 = bf16[512,256]{1,0:T(8,128)(2,1)S(1)} collective-permute-done((bf16[512,256]{1,0:T(8,128)(2,1)S(1)}, bf16[512,256]{1,0:T(8,128)(2,1)S(1)}, u32[]{:S(2)}, u32[]{:S(2)}) %collective-permute-start.2) | collective-permute-done | bytes 262176 | tf_op jit(solution)/shard_map/ppermute | solution.py:36
  37.0 4.1 %all-to-all-done = bf16[8,256,256]{2,1,0:T(8,128)(2,1)S(1)} async-done(((bf16[8,256,256]{2,1,0:T(8,128)(2,1)}), bf16[8,256,256]{2,1,0:T(8,128)(2,1)S(1)}, u32[]{:S(2)}, u32[]{:S(2)}) %all-to-all-start) | async-done | bytes 1048608 | tf_op jit(solution)/shard_map/all_to_all | solution.py:27
  41.0 5.2 %stats.1 = f32[8,40,256]{2,1,0:T(8,128)S(1)} custom-call(s32[10]{0:T(128)S(1)} %pad_add_fusion.1.at_ref, bf16[2048,256]{1,0:T(8,128)(2,1)S(1)} %bitcast.58, bf16[2048,256]{1,0:T(8,128)(2,1)S(1)} %convolution_convert_fusion.users_ref, f32[24,256]{1,0:T(8,128)S(1)} %pad_maximum_fusion.1.own_ref), custom_call_target="tpu_custom_call" | custom-call | tf_op jit(solution)/shard_map/stats/pallas_call | solution.py:78
  46.3 12.1 %all_to_all.25.got_ref = f32[8,40,256]{2,1,0:T(8,128)S(1)} all-to-all(f32[8,40,256]{2,1,0:T(8,128)S(1)} %stats.1), channel_id=1, replica_groups=mesh['z'=8,'x'=4,'k'=2,'y'=4] {'x','k'}, dimensions={0} | all-to-all | bytes 655360 | tf_op jit(solution)/shard_map/all_to_all | solution.py:27
  58.3 8.0 %grads.1 = (f32[8,264,256]{2,1,0:T(8,128)S(1)}, f32[4,256,256]{2,1,0:T(8,128)S(1)}, f32[4,256,256]{2,1,0:T(8,128)S(1)}) custom-call(s32[10]{0:T(128)S(1)} %pad_add_fusion.1.at_ref, bf16[2048,256]{1,0:T(8,128)(2,1)S(1)} %bitcast.59, bf16[2048,256]{1,0:T(8,128)(2,1)S(1)} %convolution_convert_fusion.users_ref, f32[8,40,256]{2,1,0:T(8,128)S(1)} %all_to_all.25.got_ref), custom_call_target="tpu_custom_call" | custom-call | tf_op jit(solution)/shard_map/grads/pallas_call | solution.py:136
  70.7 2.4 %collective-permute-start.8 = (f32[256,256]{1,0:T(8,128)}, f32[256,256]{1,0:T(8,128)}, u32[]{:S(2)}, u32[]{:S(2)}) collective-permute-start(f32[256,256]{1,0:T(8,128)} %get-tuple-element.9), channel_id=1, source_target_pairs={{0,24},{8,0},{16,8},{24,16},{1,25},{9,1},{17,9},{25,17},{2,26},{10... | collective-permute-start | bytes 786440 | tf_op jit(solution)/shard_map/ppermute | solution.py:36
  73.3 2.8 %convert_element_type.118 = f16[8,264,256]{2,1,0:T(8,128)(2,1)} convert(f32[8,264,256]{2,1,0:T(8,128)} %copy-done.1) | non-fusion elementwise | flops 540672 | bytes 3244032 | tf_op jit(solution)/shard_map/convert_element_type | solution.py:242
  76.1 4.7 %all-to-all-start.3 = ((f16[8,264,256]{2,1,0:T(8,128)(2,1)}), f16[8,264,256]{2,1,0:T(8,128)(2,1)S(1)}, u32[]{:S(2)}, u32[]{:S(2)}) async-start(f16[8,264,256]{2,1,0:T(8,128)(2,1)} %convert_element_type.118), calls=%async_computation.3 | async-start | bytes 2162688 | tf_op jit(solution)/shard_map/all_to_all | solution.py:27
  80.8 3.7 %collective-permute-done.9 = f32[256,256]{1,0:T(8,128)} collective-permute-done((f32[256,256]{1,0:T(8,128)S(1)}, f32[256,256]{1,0:T(8,128)}, u32[]{:S(2)}, u32[]{:S(2)}) %collective-permute-start.9) | collective-permute-done | bytes 262176 | tf_op jit(solution)/shard_map/ppermute | solution.py:36
  91.1 2.6 %collective-permute-start.13 = (f32[64,256]{1,0:T(8,128)S(1)}, f32[64,256]{1,0:T(8,128)S(1)}, u32[]{:S(2)}, u32[]{:S(2)}) collective-permute-start(f32[64,256]{1,0:T(8,128)S(1)} %get-tuple-element.16), channel_id=1, source_target_pairs={{0,2},{1,3},{2,0},{3,1},{4,6},{5,7},{6,4},{7,5},{8,10},{9,11},{10,... | collective-permute-start | bytes 196616 | tf_op jit(solution)/shard_map/ppermute | solution.py:36
  97.9 3.3 %collective-permute-start.16 = (f32[16,256]{1,0:T(8,128)S(1)}, f32[16,256]{1,0:T(8,128)S(1)}, u32[]{:S(2)}, u32[]{:S(2)}) collective-permute-start(f32[16,256]{1,0:T(8,128)S(1)} %get-tuple-element.21), channel_id=1, source_target_pairs={{0,16},{8,24},{16,0},{24,8},{1,17},{9,25},{17,1},{25,9},{2,18},{10... | collective-permute-start | bytes 49160 | tf_op jit(solution)/shard_map/ppermute | solution.py:36
  104.4 2.6 %collective-permute-done.18 = f32[16,256]{1,0:T(8,128)S(1)} collective-permute-done((f32[16,256]{1,0:T(8,128)S(1)}, f32[16,256]{1,0:T(8,128)S(1)}, u32[]{:S(2)}, u32[]{:S(2)}) %collective-permute-start.18) | collective-permute-done | bytes 16416 | tf_op jit(solution)/shard_map/ppermute | solution.py:266
  107.3 3.7 %collective-permute-done.19 = f32[16,256]{1,0:T(8,128)S(1)} collective-permute-done((f32[16,256]{1,0:T(8,128)S(1)}, f32[16,256]{1,0:T(8,128)S(1)}, u32[]{:S(2)}, u32[]{:S(2)}) %collective-permute-start.19) | collective-permute-done | bytes 16416 | tf_op jit(solution)/shard_map/ppermute | solution.py:266
  111.0 2.7 %collective-permute-start.20 = (f32[16,256]{1,0:T(8,128)S(1)}, f32[16,256]{1,0:T(8,128)S(1)}, u32[]{:S(2)}, u32[]{:S(2)}) collective-permute-start(f32[16,256]{1,0:T(8,128)S(1)} %add.161), channel_id=1, source_target_pairs={{0,128},{32,160},{64,192},{96,224},{128,0},{160,32},{192,64},{224,... | collective-permute-start | bytes 49160 | tf_op jit(solution)/shard_map/ppermute | solution.py:266
  113.7 3.8 %collective-permute-done.20 = f32[16,256]{1,0:T(8,128)S(1)} collective-permute-done((f32[16,256]{1,0:T(8,128)S(1)}, f32[16,256]{1,0:T(8,128)S(1)}, u32[]{:S(2)}, u32[]{:S(2)}) %collective-permute-start.20) | collective-permute-done | bytes 16416 | tf_op jit(solution)/shard_map/ppermute | solution.py:266
  118.4 10.9 %all-to-all-start.2 = ((f32[32,16,256]{2,1,0:T(8,128)}), f32[32,16,256]{2,1,0:T(8,128)S(1)}, u32[]{:S(2)}, u32[]{:S(2)}) async-start(f32[32,16,256]{2,1,0:T(8,128)} %broadcast_in_dim.20), calls=%async_computation.2 | async-start | bytes 1048576 | tf_op jit(solution)/shard_map/all_to_all | solution.py:27
  129.8 5.1 %fusion.15.item_ref = bf16[256,256]{1,0:T(8,128)(2,1)S(1)} fusion(f32[]{:T(128)} %bitcast.22, f16[8,264,256]{2,1,0:T(8,128)(2,1)S(1)} %all-to-all-done.3, f32[]{:T(128)} %bitcast.21, f32[]{:T(128)} %bitcast.20, f32[]{:T(128)} %bitcast.19, f32[]{:T(128)} %bitcast.18, f32[]{:T(128)} %bitcast.17, f32[]{:T(128)} %bitcast.16, f32[]{:T(128)} %bitcast.15), kind=kLoop, calls=%fused_computation.35 | loop fusion | flops 1572864 | bytes 1179680 | tf_op jit(solution)/shard_map/convert_element_type | solution.py:244
  136.2 4.2 %all-to-all-done.2 = f32[32,16,256]{2,1,0:T(8,128)S(1)} async-done(((f32[32,16,256]{2,1,0:T(8,128)}), f32[32,16,256]{2,1,0:T(8,128)S(1)}, u32[]{:S(2)}, u32[]{:S(2)}) %all-to-all-start.2) | async-done | bytes 524320 | tf_op jit(solution)/shard_map/all_to_all | solution.py:27
  140.4 6.4 %all-to-all-start.4 = ((bf16[256,8,128]{2,1,0:T(8,128)(2,1)}), bf16[256,8,128]{2,1,0:T(8,128)(2,1)S(1)}, u32[]{:S(2)}, u32[]{:S(2)}) async-start(bf16[256,8,128]{2,1,0:T(8,128)(2,1)} %bitcast.26), calls=%async_computation.4 | async-start | bytes 1048576 | tf_op jit(solution)/shard_map/all_to_all | solution.py:27
  148.1 19.2 %all-to-all-done.4 = bf16[256,8,128]{2,1,0:T(8,128)(2,1)S(1)} async-done(((bf16[256,8,128]{2,1,0:T(8,128)(2,1)}), bf16[256,8,128]{2,1,0:T(8,128)(2,1)S(1)}, u32[]{:S(2)}, u32[]{:S(2)}) %all-to-all-start.4) | async-done | bytes 524320 | tf_op jit(solution)/shard_map/all_to_all | solution.py:27
  167.2 4.6 %table.1 = f32[64,4096]{1,0:T(8,128)} custom-call(bf16[2048,128]{1,0:T(8,128)(2,1)S(1)} %bitcast.60, s32[1,4096]{1,0:T(1,128)S(1)} %pad_add_fusion.ids_ref), custom_call_target="tpu_custom_call" | custom-call | tf_op jit(solution)/shard_map/table/pallas_call | solution.py:198
  (105 shorter events, 38.9 us)
Async XLA Ops:
  2.7 38.3 %all-to-all-start = ((bf16[8,256,256]{2,1,0:T(8,128)(2,1)}), bf16[8,256,256]{2,1,0:T(8,128)(2,1)S(1)}, u32[]{:S(2)}, u32[]{:S(2)}) async-start(bf16[8,256,256]{2,1,0:T(8,128)(2,1)} %broadcast_in_dim.18), calls=%async_computation | async-start | bytes 2097152 | tf_op jit(solution)/shard_map/all_to_all | solution.py:27
  12.4 6.5 %collective-permute-start.4 = (f32[64,16]{1,0:T(8,128)S(1)}, f32[64,16]{1,0:T(8,128)S(1)}, u32[]{:S(2)}, u32[]{:S(2)}) collective-permute-start(f32[64,16]{1,0:T(8,128)S(1)} %convert_element_type.111), channel_id=1, source_target_pairs={{0,3},{1,0},{2,1},{3,2},{4,7},{5,4},{6,5},{7,6},{8,11},{9,8},{10,9... | collective-permute-start | bytes 12296 | tf_op jit(solution)/shard_map/ppermute | solution.py:36
  15.1 4.3 %collective-permute-start.5 = (f32[64,16]{1,0:T(8,128)S(1)}, f32[64,16]{1,0:T(8,128)S(1)}, u32[]{:S(2)}, u32[]{:S(2)}) collective-permute-start(f32[64,16]{1,0:T(8,128)S(1)} %convert_element_type.111), channel_id=1, source_target_pairs={{0,2},{1,3},{2,0},{3,1},{4,6},{5,7},{6,4},{7,5},{8,10},{9,11},{10,... | collective-permute-start | bytes 12296 | tf_op jit(solution)/shard_map/ppermute | solution.py:36
  15.5 4.3 %collective-permute-start.6 = (f32[64,16]{1,0:T(8,128)S(1)}, f32[64,16]{1,0:T(8,128)S(1)}, u32[]{:S(2)}, u32[]{:S(2)}) collective-permute-start(f32[64,16]{1,0:T(8,128)S(1)} %convert_element_type.111), channel_id=1, source_target_pairs={{0,1},{1,2},{2,3},{3,0},{4,5},{5,6},{6,7},{7,4},{8,9},{9,10},{10,1... | collective-permute-start | bytes 12296 | tf_op jit(solution)/shard_map/ppermute | solution.py:36
  16.2 4.0 %collective-permute-start = (bf16[256,256]{1,0:T(8,128)(2,1)S(1)}, bf16[256,256]{1,0:T(8,128)(2,1)S(1)}, u32[]{:S(2)}, u32[]{:S(2)}) collective-permute-start(bf16[256,256]{1,0:T(8,128)(2,1)S(1)} %bitcast.65), channel_id=1, source_target_pairs={{0,4},{4,0},{1,5},{5,1},{2,6},{6,2},{3,7},{7,3},{8,12},{12,8},{9,1... | collective-permute-start | bytes 393224 | tf_op jit(solution)/shard_map/ppermute | solution.py:36
  20.2 6.8 %collective-permute-start.1 = (bf16[512,256]{1,0:T(8,128)(2,1)S(1)}, bf16[512,256]{1,0:T(8,128)(2,1)S(1)}, u32[]{:S(2)}, u32[]{:S(2)}) collective-permute-start(bf16[512,256]{1,0:T(8,128)(2,1)S(1)} %pad_maximum_fusion), channel_id=1, source_target_pairs={{0,8},{8,16},{16,24},{24,0},{1,9},{9,17},{17,25},{25,1},{2,10},{10... | collective-permute-start | bytes 786440 | tf_op jit(solution)/shard_map/ppermute | solution.py:36
  21.5 11.9 %collective-permute-start.2 = (bf16[512,256]{1,0:T(8,128)(2,1)S(1)}, bf16[512,256]{1,0:T(8,128)(2,1)S(1)}, u32[]{:S(2)}, u32[]{:S(2)}) collective-permute-start(bf16[512,256]{1,0:T(8,128)(2,1)S(1)} %pad_maximum_fusion), channel_id=1, source_target_pairs={{0,16},{8,24},{16,0},{24,8},{1,17},{9,25},{17,1},{25,9},{2,18},{10... | collective-permute-start | bytes 786440 | tf_op jit(solution)/shard_map/ppermute | solution.py:36
  24.1 10.1 %collective-permute-start.3 = (bf16[512,256]{1,0:T(8,128)(2,1)S(1)}, bf16[512,256]{1,0:T(8,128)(2,1)S(1)}, u32[]{:S(2)}, u32[]{:S(2)}) collective-permute-start(bf16[512,256]{1,0:T(8,128)(2,1)S(1)} %pad_maximum_fusion), channel_id=1, source_target_pairs={{0,24},{8,0},{16,8},{24,16},{1,25},{9,1},{17,9},{25,17},{2,26},{10... | collective-permute-start | bytes 786440 | tf_op jit(solution)/shard_map/ppermute | solution.py:36
  66.3 3.1 %collective-permute-start.7 = (f32[4,256,256]{2,1,0:T(8,128)S(1)}, f32[4,256,256]{2,1,0:T(8,128)S(1)}, u32[]{:S(2)}, u32[]{:S(2)}) collective-permute-start(f32[4,256,256]{2,1,0:T(8,128)S(1)} %get-tuple-element.7), channel_id=1, source_target_pairs={{0,4},{4,0},{1,5},{5,1},{2,6},{6,2},{3,7},{7,3},{8,12},{12,8},{9,1... | collective-permute-start | bytes 3145736 | tf_op jit(solution)/shard_map/ppermute | solution.py:36
  70.4 10.3 %collective-permute-start.10 = (f32[256,256]{1,0:T(8,128)}, f32[256,256]{1,0:T(8,128)S(1)}, u32[]{:S(2)}, u32[]{:S(2)}) collective-permute-start(f32[256,256]{1,0:T(8,128)} %get-tuple-element.10), channel_id=1, source_target_pairs={{0,8},{8,16},{16,24},{24,0},{1,9},{9,17},{17,25},{25,1},{2,10},{10... | collective-permute-start | bytes 786440 | tf_op jit(solution)/shard_map/ppermute | solution.py:36
  70.7 10.1 %collective-permute-start.8 = (f32[256,256]{1,0:T(8,128)}, f32[256,256]{1,0:T(8,128)}, u32[]{:S(2)}, u32[]{:S(2)}) collective-permute-start(f32[256,256]{1,0:T(8,128)} %get-tuple-element.9), channel_id=1, source_target_pairs={{0,24},{8,0},{16,8},{24,16},{1,25},{9,1},{17,9},{25,17},{2,26},{10... | collective-permute-start | bytes 786440 | tf_op jit(solution)/shard_map/ppermute | solution.py:36
  73.1 11.4 %collective-permute-start.9 = (f32[256,256]{1,0:T(8,128)S(1)}, f32[256,256]{1,0:T(8,128)}, u32[]{:S(2)}, u32[]{:S(2)}) collective-permute-start(f32[256,256]{1,0:T(8,128)S(1)} %get-tuple-element.11), channel_id=1, source_target_pairs={{0,16},{8,24},{16,0},{24,8},{1,17},{9,25},{17,1},{25,9},{2,18},{10... | collective-permute-start | bytes 786440 | tf_op jit(solution)/shard_map/ppermute | solution.py:36
  76.1 41.4 %all-to-all-start.3 = ((f16[8,264,256]{2,1,0:T(8,128)(2,1)}), f16[8,264,256]{2,1,0:T(8,128)(2,1)S(1)}, u32[]{:S(2)}, u32[]{:S(2)}) async-start(f16[8,264,256]{2,1,0:T(8,128)(2,1)} %convert_element_type.118), calls=%async_computation.3 | async-start | bytes 2162688 | tf_op jit(solution)/shard_map/all_to_all | solution.py:27
  86.4 2.9 %collective-permute-start.11 = (f32[256,256]{1,0:T(8,128)S(1)}, f32[256,256]{1,0:T(8,128)S(1)}, u32[]{:S(2)}, u32[]{:S(2)}) collective-permute-start(f32[256,256]{1,0:T(8,128)S(1)} %fusion.3), channel_id=1, source_target_pairs={{0,4},{4,0},{1,5},{5,1},{2,6},{6,2},{3,7},{7,3},{8,12},{12,8},{9,1... | collective-permute-start | bytes 786440 | tf_op jit(solution)/shard_map/ppermute | solution.py:36
  89.5 5.3 %collective-permute-start.12 = (f32[64,256]{1,0:T(8,128)S(1)}, f32[64,256]{1,0:T(8,128)S(1)}, u32[]{:S(2)}, u32[]{:S(2)}) collective-permute-start(f32[64,256]{1,0:T(8,128)S(1)} %get-tuple-element.14), channel_id=1, source_target_pairs={{0,1},{1,2},{2,3},{3,0},{4,5},{5,6},{6,7},{7,4},{8,9},{9,10},{10,1... | collective-permute-start | bytes 196616 | tf_op jit(solution)/shard_map/ppermute | solution.py:36
  91.1 5.7 %collective-permute-start.13 = (f32[64,256]{1,0:T(8,128)S(1)}, f32[64,256]{1,0:T(8,128)S(1)}, u32[]{:S(2)}, u32[]{:S(2)}) collective-permute-start(f32[64,256]{1,0:T(8,128)S(1)} %get-tuple-element.16), channel_id=1, source_target_pairs={{0,2},{1,3},{2,0},{3,1},{4,6},{5,7},{6,4},{7,5},{8,10},{9,11},{10,... | collective-permute-start | bytes 196616 | tf_op jit(solution)/shard_map/ppermute | solution.py:36
  93.7 3.4 %collective-permute-start.14 = (f32[64,256]{1,0:T(8,128)S(1)}, f32[64,256]{1,0:T(8,128)S(1)}, u32[]{:S(2)}, u32[]{:S(2)}) collective-permute-start(f32[64,256]{1,0:T(8,128)S(1)} %get-tuple-element.15), channel_id=1, source_target_pairs={{0,3},{1,0},{2,1},{3,2},{4,7},{5,4},{6,5},{7,6},{8,11},{9,8},{10,9... | collective-permute-start | bytes 196616 | tf_op jit(solution)/shard_map/ppermute | solution.py:36
  97.1 4.3 %collective-permute-start.15 = (f32[16,256]{1,0:T(8,128)S(1)}, f32[16,256]{1,0:T(8,128)S(1)}, u32[]{:S(2)}, u32[]{:S(2)}) collective-permute-start(f32[16,256]{1,0:T(8,128)S(1)} %get-tuple-element.19), channel_id=1, source_target_pairs={{0,8},{8,16},{16,24},{24,0},{1,9},{9,17},{17,25},{25,1},{2,10},{10... | collective-permute-start | bytes 49160 | tf_op jit(solution)/shard_map/ppermute | solution.py:36
  97.9 4.7 %collective-permute-start.16 = (f32[16,256]{1,0:T(8,128)S(1)}, f32[16,256]{1,0:T(8,128)S(1)}, u32[]{:S(2)}, u32[]{:S(2)}) collective-permute-start(f32[16,256]{1,0:T(8,128)S(1)} %get-tuple-element.21), channel_id=1, source_target_pairs={{0,16},{8,24},{16,0},{24,8},{1,17},{9,25},{17,1},{25,9},{2,18},{10... | collective-permute-start | bytes 49160 | tf_op jit(solution)/shard_map/ppermute | solution.py:36
  104.1 3.0 %collective-permute-start.18 = (f32[16,256]{1,0:T(8,128)S(1)}, f32[16,256]{1,0:T(8,128)S(1)}, u32[]{:S(2)}, u32[]{:S(2)}) collective-permute-start(f32[16,256]{1,0:T(8,128)S(1)} %add_add_fusion.1), channel_id=1, source_target_pairs={{0,32},{32,0},{64,96},{96,64},{128,160},{160,128},{192,224},{224,1... | collective-permute-start | bytes 49160 | tf_op jit(solution)/shard_map/ppermute | solution.py:266
  107.1 3.9 %collective-permute-start.19 = (f32[16,256]{1,0:T(8,128)S(1)}, f32[16,256]{1,0:T(8,128)S(1)}, u32[]{:S(2)}, u32[]{:S(2)}) collective-permute-start(f32[16,256]{1,0:T(8,128)S(1)} %add.160), channel_id=1, source_target_pairs={{0,64},{32,96},{64,0},{96,32},{128,192},{160,224},{192,128},{224,1... | collective-permute-start | bytes 49160 | tf_op jit(solution)/shard_map/ppermute | solution.py:266
  111.0 6.5 %collective-permute-start.20 = (f32[16,256]{1,0:T(8,128)S(1)}, f32[16,256]{1,0:T(8,128)S(1)}, u32[]{:S(2)}, u32[]{:S(2)}) collective-permute-start(f32[16,256]{1,0:T(8,128)S(1)} %add.161), channel_id=1, source_target_pairs={{0,128},{32,160},{64,192},{96,224},{128,0},{160,32},{192,64},{224,... | collective-permute-start | bytes 49160 | tf_op jit(solution)/shard_map/ppermute | solution.py:266
  118.4 22.0 %all-to-all-start.2 = ((f32[32,16,256]{2,1,0:T(8,128)}), f32[32,16,256]{2,1,0:T(8,128)S(1)}, u32[]{:S(2)}, u32[]{:S(2)}) async-start(f32[32,16,256]{2,1,0:T(8,128)} %broadcast_in_dim.20), calls=%async_computation.2 | async-start | bytes 1048576 | tf_op jit(solution)/shard_map/all_to_all | solution.py:27
  140.4 26.9 %all-to-all-start.4 = ((bf16[256,8,128]{2,1,0:T(8,128)(2,1)}), bf16[256,8,128]{2,1,0:T(8,128)(2,1)S(1)}, u32[]{:S(2)}, u32[]{:S(2)}) async-start(bf16[256,8,128]{2,1,0:T(8,128)(2,1)} %bitcast.26), calls=%async_computation.4 | async-start | bytes 1048576 | tf_op jit(solution)/shard_map/all_to_all | solution.py:27
  (9 other events, 141.8 us)
